TPU v7x, 32 devices: a whole 2x2x4 slice. The times are simulated.
32 devices in a mesh: tm: 8 (over y, x, core), space: 4 (over z).
Axes of the slice: x: 2, y: 2, z: 4, core: 2. Of those that a mesh axis runs over, the one named last changes fastest.
Arguments:
- state: float32 [16, 32, 64, 256], P('tm', 'space'), may hold values from -1.5 to 1.5
- initial: float32 [32, 64, 256], P('space'), may hold values from -1.5 to 1.5
Outputs:
- updated: float32 [16, 32, 64, 256], P('tm', 'space')
- residual: float32 [16, 32, 64, 256], P('tm', 'space')
All inputs are finite; a program needn't handle non-finite values.
Results may differ from a plain program's by a relative error of at most 0.0003.
Values sent between devices are 32-bit elements; how exact they have to be, the bound alone decides.
No kernel may reach another device: no remote copies, remote signals or barrier semaphores. Data moves between devices by JAX's collectives and lax.ppermute only.
A program may use at most 64 MiB of HBM per device.

v0:
```python
import math

import jax
import jax.numpy as jnp
from jax import lax
from jax.sharding import PartitionSpec as P

SWEEPS = 6


alpha_value = 0.1
time_step = 0.1
couple_first = 0.4
couple_cross = 0.05
reaction_shift = 0.1
relaxation = 0.9


def shifted(block, axis, distance):
    devices = range(lax.axis_size(axis))
    route = [(i - distance, i) for i in devices if i - distance in devices]
    return lax.ppermute(block, axis, route)


def extended(block, sides, width):
    for axis, dim in sides:
        count = lax.axis_size(axis)
        forward = [(i, i + 1) for i in range(count - 1)]
        forward.append((count - 1, 0))
        backward = [(target, source) for source, target in forward]
        low = lax.ppermute(
            lax.slice_in_dim(block, block.shape[dim] - width, None, axis=dim), axis, forward
        )
        high = lax.ppermute(lax.slice_in_dim(block, 0, width, axis=dim), axis, backward)
        block = jnp.concatenate([low, block, high], axis=dim)
    return block


def cross_sum(field):
    return (
        jnp.roll(field, 1, -2)
        + jnp.roll(field, -1, -2)
        + jnp.roll(field, 1, -1)
        + jnp.roll(field, -1, -1)
    )


def phases(lefts, rights, horizon):
    products = lefts[:, None] * rights[None, :] % horizon
    return 2.0 * math.pi / horizon * products.astype(jnp.float32)


def scales(horizon):
    counter = jnp.arange(horizon)
    return jnp.power(alpha_value, counter.astype(jnp.float32) / horizon)


def mode_diagonal(modes, horizon):
    root_alpha = alpha_value ** (1.0 / horizon)
    angles = 2.0 * math.pi / horizon * modes.astype(jnp.float32)
    diag_real = (
        1.0
        - root_alpha * jnp.cos(angles)
        + reaction_shift
        + 2.0 * couple_first
        + 4.0 * couple_cross
    )
    diag_imag = root_alpha * jnp.sin(angles)
    return (diag_real, diag_imag)


def complex_entries(modes, horizon):
    diag_real, diag_imag = mode_diagonal(modes, horizon)
    magnitude = diag_real * diag_real + diag_imag * diag_imag
    inv_real = diag_real / magnitude
    inv_imag = -diag_imag / magnitude
    return (inv_real, -inv_imag, inv_imag, inv_real)


def apply_pairs(source, entries):
    upper_left, upper_right, lower_left, lower_right = [e[:, None, None, None] for e in entries]
    upper_row = upper_left * source[:, 0] + upper_right * source[:, 1]
    lower_row = lower_left * source[:, 0] + lower_right * source[:, 1]
    return jnp.stack([upper_row, lower_row], axis=1)


def body(state, initial):
    steps_local, slab_width, second, third = state.shape
    horizon = steps_local * lax.axis_size("tm")
    position = lax.axis_index("tm")
    highest = lax.Precision.HIGHEST
    carried = shifted(state[steps_local - 1], "tm", 1)
    carried = jnp.where(position == 0, initial, carried)
    before = jnp.concatenate([carried[None], state[:-1]], axis=0)
    padded = extended(state, (("space", 1),), 1)
    laplace = couple_first * (padded[:, 2:] + padded[:, :-2] - 2.0 * state) + couple_cross * (
        cross_sum(state) - 4.0 * state
    )
    residual = before - state + laplace + time_step * (state - state * state * state)
    flattened = residual.reshape(steps_local, slab_width * second, third)
    counter = jnp.arange(horizon)
    weight = scales(horizon)
    modes = jnp.where(counter == 1, horizon // 2, counter // 2)
    odd_rows = (counter % 2 == 1) & (counter != 1)
    angles = phases(modes, counter, horizon)
    basis = jnp.where(odd_rows[:, None], -jnp.sin(angles), jnp.cos(angles))
    factor = jnp.where(counter < 2, 1.0, 2.0)
    fore_rows = basis * weight[None, :]
    back_rows = (basis * factor[:, None]).T / (horizon * weight[:, None])

    def forward(pieces):
        return jnp.einsum("pn,nci->pci", fore_rows, pieces, precision=highest)

    spectra = forward(lax.all_to_all(flattened, "tm", split_axis=1, concat_axis=0, tiled=True))
    owned = lax.all_to_all(spectra, "tm", split_axis=0, concat_axis=1, tiled=True)
    pair_count = steps_local // 2
    fields = owned.reshape(pair_count, 2, slab_width, second, third)
    pair_modes = position * pair_count + jnp.arange(pair_count)
    upper_left, upper_right, lower_left, lower_right = complex_entries(pair_modes, horizon)
    lowest, unused_low = mode_diagonal(jnp.zeros_like(pair_modes), horizon)
    highest_mode, unused_high = mode_diagonal(jnp.zeros_like(pair_modes) + horizon // 2, horizon)
    leading = pair_modes == 0
    entries = (
        jnp.where(leading, 1.0 / lowest, upper_left),
        jnp.where(leading, 0.0, upper_right),
        jnp.where(leading, 0.0, lower_left),
        jnp.where(leading, 1.0 / highest_mode, lower_right),
    )
    solved = relaxation * apply_pairs(fields, entries)
    for sweep_index in range(SWEEPS - 1):
        framed = extended(solved, (("space", 2),), 1)
        nearby = couple_first * (framed[:, :, 2:] + framed[:, :, :-2]) + couple_cross * cross_sum(
            solved
        )
        solved = (1.0 - relaxation) * solved + relaxation * apply_pairs(fields + nearby, entries)
    solved_rows = solved.reshape(steps_local, slab_width * second, third)

    def backward(pieces):
        return jnp.einsum("np,pci->nci", back_rows, pieces, precision=highest)

    restored = backward(lax.all_to_all(solved_rows, "tm", split_axis=1, concat_axis=0, tiled=True))
    delta = lax.all_to_all(restored, "tm", split_axis=0, concat_axis=1, tiled=True).reshape(
        state.shape
    )
    return (state + delta, residual)


def solution(mesh):
    in_specs = (P("tm", "space", None, None), P("space", None, None))
    out_specs = (P("tm", "space", None, None), P("tm", "space", None, None))
    return jax.shard_map(body, mesh=mesh, in_specs=in_specs, out_specs=out_specs, check_vma=False)
```

profile of v0, /device:TPU:4, one launch (start us, length us, event | category | flops | bytes accessed | tf_op | source)
XLA Modules:
  0.0 158.9 jit_solution(17836695816250505258)
XLA Ops:
  0.6 2.2 %slice_bitcast_fusion = (f32[8,64,256]{2,1,0:T(8,128)}, f32[1,8,64,256]{3,2,1,0:T(8,128)S(1)}) fusion(f32[2,8,64,256]{3,2,1,0:T(8,128)} %param.2), kind=kLoop, calls=%fused_computation.105 | loop fusion | bytes 2097152 | tf_op jit(solution)/shard_map/squeeze | solution.py:92
  2.8 1.9 %collective-permute-start = (f32[8,64,256]{2,1,0:T(8,128)}, f32[8,64,256]{2,1,0:T(8,128)}, u32[]{:S(2)}, u32[]{:S(2)}) collective-permute-start(f32[8,64,256]{2,1,0:T(8,128)} %get-tuple-element.72), channel_id=1, source_target_pairs={{0,4},{4,8},{8,12},{12,16},{16,20},{20,24},{24,28},{1,5},{5,9},{9,... | collective-permute-start | bytes 1572872 | tf_op jit(solution)/shard_map/ppermute | solution.py:22
  4.7 0.7 fusion.145
  5.4 3.6 %collective-permute-start.1 = (f32[2,1,64,256]{3,2,1,0:T(8,128)}, f32[2,1,64,256]{3,2,1,0:T(8,128)S(1)}, u32[]{:S(2)}, u32[]{:S(2)}) collective-permute-start(f32[2,1,64,256]{3,2,1,0:T(8,128)} %get-tuple-element.74), channel_id=1, source_target_pairs={{1,0},{2,1},{3,2},{0,3},{5,4},{6,5},{7,6},{4,7},{9,8},{10,9},{11,1... | collective-permute-start | bytes 393224 | tf_op jit(solution)/shard_map/ppermute | solution.py:34
  9.0 1.3 fusion.141
  10.4 1.0 fusion.142
  11.6 2.9 %collective-permute-done = f32[8,64,256]{2,1,0:T(8,128)} collective-permute-done((f32[8,64,256]{2,1,0:T(8,128)}, f32[8,64,256]{2,1,0:T(8,128)}, u32[]{:S(2)}, u32[]{:S(2)}) %collective-permute-start) | collective-permute-done | bytes 524320 | tf_op jit(solution)/shard_map/ppermute | solution.py:22
  14.5 1.1 select_bitcast_fusion
  15.7 1.2 collective-permute-done.2
  16.9 1.0 fusion.1
  17.9 1.8 %copy.18 = f32[2,8,64,256]{3,0,2,1:T(2,128)} copy(f32[2,8,64,256]{3,2,1,0:T(8,128)S(1)} %fusion.1) | data formatting | bytes 2097152 | tf_op jit(solution)/shard_map/add | solution.py:99
  19.7 4.7 %all-to-all-start = ((f32[2,512,256]{2,0,1:T(2,128)}), f32[2,512,256]{2,0,1:T(2,128)S(1)}, u32[]{:S(2)}, u32[]{:S(2)}) async-start(f32[2,512,256]{2,0,1:T(2,128)} %bitcast.8), calls=%async_computation | async-start | bytes 2097152 | tf_op jit(solution)/shard_map/all_to_all | solution.py:114
  24.4 13.9 %all-to-all-done = f32[2,512,256]{2,0,1:T(2,128)S(1)} async-done(((f32[2,512,256]{2,0,1:T(2,128)}), f32[2,512,256]{2,0,1:T(2,128)S(1)}, u32[]{:S(2)}, u32[]{:S(2)}) %all-to-all-start) | async-done | bytes 1048608 | tf_op jit(solution)/shard_map/all_to_all | solution.py:114
  38.4 0.8 copy.20
  39.2 0.7 all_to_all.51
  39.9 1.1 fusion.66
  41.0 1.6 copy.21
  42.6 5.0 %all-to-all-start.1 = ((f32[16,64,256]{2,1,0:T(8,128)}), f32[16,64,256]{2,1,0:T(8,128)S(1)}, u32[]{:S(2)}, u32[]{:S(2)}) async-start(f32[16,64,256]{2,1,0:T(8,128)} %copy.21), calls=%async_computation.1 | async-start | bytes 2097152 | tf_op jit(solution)/shard_map/all_to_all | solution.py:115
  47.8 13.7 %all-to-all-done.1 = f32[16,64,256]{2,1,0:T(8,128)S(1)} async-done(((f32[16,64,256]{2,1,0:T(8,128)}), f32[16,64,256]{2,1,0:T(8,128)S(1)}, u32[]{:S(2)}, u32[]{:S(2)}) %all-to-all-start.1) | async-done | bytes 1048608 | tf_op jit(solution)/shard_map/all_to_all | solution.py:115
  62.6 1.5 collective-permute-start.3
  64.7 4.2 %collective-permute-done.3 = f32[1,2,1,64,256]{4,3,1,2,0:T(8,128)S(1)} collective-permute-done((f32[1,2,1,64,256]{4,3,1,2,0:T(8,128)S(1)}, f32[1,2,1,64,256]{4,3,1,2,0:T(8,128)S(1)}, u32[]{:S(2)}, u32[]{:S(2)}) %collective-permute-start.3) | collective-permute-done | bytes 131104 | tf_op jit(solution)/shard_map/ppermute | solution.py:34
  68.8 2.0 %collective-permute-done.4 = f32[1,2,1,64,256]{4,3,1,2,0:T(8,128)S(1)} collective-permute-done((f32[1,2,1,64,256]{4,3,1,2,0:T(8,128)S(1)}, f32[1,2,1,64,256]{4,3,1,2,0:T(8,128)S(1)}, u32[]{:S(2)}, u32[]{:S(2)}) %collective-permute-start.4) | collective-permute-done | bytes 131104 | tf_op jit(solution)/shard_map/ppermute | solution.py:31
  70.8 0.8 fusion.21
  73.4 1.4 collective-permute-start.6
  74.9 3.2 %collective-permute-done.5 = f32[1,2,1,64,256]{4,3,1,2,0:T(8,128)S(1)} collective-permute-done((f32[1,2,1,64,256]{4,3,1,2,0:T(8,128)S(1)}, f32[1,2,1,64,256]{4,3,1,2,0:T(8,128)S(1)}, u32[]{:S(2)}, u32[]{:S(2)}) %collective-permute-start.5) | collective-permute-done | bytes 131104 | tf_op jit(solution)/shard_map/ppermute | solution.py:34
  78.1 2.1 %collective-permute-done.6 = f32[1,2,1,64,256]{4,3,1,2,0:T(8,128)S(1)} collective-permute-done((f32[1,2,1,64,256]{4,3,1,2,0:T(8,128)S(1)}, f32[1,2,1,64,256]{4,3,1,2,0:T(8,128)S(1)}, u32[]{:S(2)}, u32[]{:S(2)}) %collective-permute-start.6) | collective-permute-done | bytes 131104 | tf_op jit(solution)/shard_map/ppermute | solution.py:31
  80.2 0.8 fusion.17
  82.3 1.0 collective-permute-start.7
  83.4 1.0 collective-permute-start.8
  84.4 2.9 %collective-permute-done.7 = f32[1,2,1,64,256]{4,3,1,2,0:T(8,128)S(1)} collective-permute-done((f32[1,2,1,64,256]{4,3,1,2,0:T(8,128)S(1)}, f32[1,2,1,64,256]{4,3,1,2,0:T(8,128)S(1)}, u32[]{:S(2)}, u32[]{:S(2)}) %collective-permute-start.7) | collective-permute-done | bytes 131104 | tf_op jit(solution)/shard_map/ppermute | solution.py:34
  87.3 2.9 %collective-permute-done.8 = f32[1,2,1,64,256]{4,3,1,2,0:T(8,128)S(1)} collective-permute-done((f32[1,2,1,64,256]{4,3,1,2,0:T(8,128)S(1)}, f32[1,2,1,64,256]{4,3,1,2,0:T(8,128)S(1)}, u32[]{:S(2)}, u32[]{:S(2)}) %collective-permute-start.8) | collective-permute-done | bytes 131104 | tf_op jit(solution)/shard_map/ppermute | solution.py:31
  90.2 0.8 fusion.13
  92.5 3.8 %collective-permute-start.9 = (f32[1,2,1,64,256]{4,3,1,2,0:T(8,128)S(1)}, f32[1,2,1,64,256]{4,3,1,2,0:T(8,128)S(1)}, u32[]{:S(2)}, u32[]{:S(2)}) collective-permute-start(f32[1,2,1,64,256]{4,3,1,2,0:T(8,128)S(1)} %get-tuple-element.24), channel_id=1, source_target_pairs={{1,0},{2,1},{3,2},{0,3},{5,4},{6,5},{7,6},{4,7},{9,8},{10,9},{11,1... | collective-permute-start | bytes 393224 | tf_op jit(solution)/shard_map/ppermute | solution.py:34
  96.4 3.1 %collective-permute-done.10 = f32[1,2,1,64,256]{4,3,1,2,0:T(8,128)S(1)} collective-permute-done((f32[1,2,1,64,256]{4,3,1,2,0:T(8,128)S(1)}, f32[1,2,1,64,256]{4,3,1,2,0:T(8,128)S(1)}, u32[]{:S(2)}, u32[]{:S(2)}) %collective-permute-start.10) | collective-permute-done | bytes 131104 | tf_op jit(solution)/shard_map/ppermute | solution.py:31
  99.4 0.8 fusion.9
  101.8 4.2 %collective-permute-start.11 = (f32[1,2,1,64,256]{4,3,1,2,0:T(8,128)S(1)}, f32[1,2,1,64,256]{4,3,1,2,0:T(8,128)S(1)}, u32[]{:S(2)}, u32[]{:S(2)}) collective-permute-start(f32[1,2,1,64,256]{4,3,1,2,0:T(8,128)S(1)} %get-tuple-element.12), channel_id=1, source_target_pairs={{1,0},{2,1},{3,2},{0,3},{5,4},{6,5},{7,6},{4,7},{9,8},{10,9},{11,1... | collective-permute-start | bytes 393224 | tf_op jit(solution)/shard_map/ppermute | solution.py:34
  106.1 2.5 %collective-permute-done.11 = f32[1,2,1,64,256]{4,3,1,2,0:T(8,128)S(1)} collective-permute-done((f32[1,2,1,64,256]{4,3,1,2,0:T(8,128)S(1)}, f32[1,2,1,64,256]{4,3,1,2,0:T(8,128)S(1)}, u32[]{:S(2)}, u32[]{:S(2)}) %collective-permute-start.11) | collective-permute-done | bytes 131104 | tf_op jit(solution)/shard_map/ppermute | solution.py:34
  108.6 4.2 %collective-permute-done.12 = f32[1,2,1,64,256]{4,3,1,2,0:T(8,128)S(1)} collective-permute-done((f32[1,2,1,64,256]{4,3,1,2,0:T(8,128)S(1)}, f32[1,2,1,64,256]{4,3,1,2,0:T(8,128)S(1)}, u32[]{:S(2)}, u32[]{:S(2)}) %collective-permute-start.12) | collective-permute-done | bytes 131104 | tf_op jit(solution)/shard_map/ppermute | solution.py:31
  112.8 0.8 fusion.5
  113.8 0.7 fusion.39
  114.5 1.8 %copy.22 = f32[2,512,256]{2,0,1:T(2,128)} copy(f32[2,512,256]{2,1,0:T(8,128)S(1)} %fusion.39) | data formatting | bytes 2097152 | tf_op jit(solution)/shard_map/add | solution.py:135
  116.3 6.5 %all-to-all-start.2 = ((f32[2,512,256]{2,0,1:T(2,128)}), f32[2,512,256]{2,0,1:T(2,128)S(1)}, u32[]{:S(2)}, u32[]{:S(2)}) async-start(f32[2,512,256]{2,0,1:T(2,128)} %copy.22), calls=%async_computation.2 | async-start | bytes 2097152 | tf_op jit(solution)/shard_map/all_to_all | solution.py:141
  122.8 13.9 %all-to-all-done.2 = f32[2,512,256]{2,0,1:T(2,128)S(1)} async-done(((f32[2,512,256]{2,0,1:T(2,128)}), f32[2,512,256]{2,0,1:T(2,128)S(1)}, u32[]{:S(2)}, u32[]{:S(2)}) %all-to-all-start.2) | async-done | bytes 1048608 | tf_op jit(solution)/shard_map/all_to_all | solution.py:141
  136.8 0.8 copy.24
  137.6 0.7 all_to_all.58
  138.3 1.1 fusion.68
  140.0 17.8 %all_to_all.66 = f32[16,64,256]{2,1,0:T(8,128)S(1)} all-to-all(f32[16,64,256]{2,1,0:T(8,128)S(1)} %copy.25), channel_id=1, replica_groups=mesh['tm'=8,'space'=4] {'tm'}, dimensions={0} | all-to-all | bytes 2097152 | tf_op jit(solution)/shard_map/all_to_all | solution.py:142
  157.8 1.1 bitcast_add_fusion
  (62 shorter events, 9.0 us)
Async XLA Ops:
  0.6 4.1 %copy-start = (f32[2,8,64,256]{3,2,1,0:T(8,128)S(1)}, f32[2,8,64,256]{3,2,1,0:T(8,128)}, u32[]{:S(2)}) copy-start(f32[2,8,64,256]{3,2,1,0:T(8,128)} %param.2) | copy-start | bytes 3145732
  2.8 11.7 %collective-permute-start = (f32[8,64,256]{2,1,0:T(8,128)}, f32[8,64,256]{2,1,0:T(8,128)}, u32[]{:S(2)}, u32[]{:S(2)}) collective-permute-start(f32[8,64,256]{2,1,0:T(8,128)} %get-tuple-element.72), channel_id=1, source_target_pairs={{0,4},{4,8},{8,12},{12,16},{16,20},{20,24},{24,28},{1,5},{5,9},{9,... | collective-permute-start | bytes 1572872 | tf_op jit(solution)/shard_map/ppermute | solution.py:22
  5.4 10.2 %collective-permute-start.1 = (f32[2,1,64,256]{3,2,1,0:T(8,128)}, f32[2,1,64,256]{3,2,1,0:T(8,128)S(1)}, u32[]{:S(2)}, u32[]{:S(2)}) collective-permute-start(f32[2,1,64,256]{3,2,1,0:T(8,128)} %get-tuple-element.74), channel_id=1, source_target_pairs={{1,0},{2,1},{3,2},{0,3},{5,4},{6,5},{7,6},{4,7},{9,8},{10,9},{11,1... | collective-permute-start | bytes 393224 | tf_op jit(solution)/shard_map/ppermute | solution.py:34
  9.0 7.8 %collective-permute-start.2 = (f32[2,1,64,256]{3,2,1,0:T(8,128)S(1)}, f32[2,1,64,256]{3,2,1,0:T(8,128)S(1)}, u32[]{:S(2)}, u32[]{:S(2)}) collective-permute-start(f32[2,1,64,256]{3,2,1,0:T(8,128)S(1)} %get-tuple-element.75), channel_id=1, source_target_pairs={{0,1},{1,2},{2,3},{3,0},{4,5},{5,6},{6,7},{7,4},{8,9},{9,10},{10,1... | collective-permute-start | bytes 393224 | tf_op jit(solution)/shard_map/ppermute | solution.py:31
  11.4 3.1 %copy-start.4 = (f32[8,64,256]{2,1,0:T(8,128)S(1)}, f32[8,64,256]{2,1,0:T(8,128)}, u32[]{:S(2)}) copy-start(f32[8,64,256]{2,1,0:T(8,128)} %param.3) | copy-start | bytes 1572868
  11.6 5.2 %copy-start.2 = (f32[2,8,64,255]{3,2,1,0:T(8,128)S(1)}, f32[2,8,64,255]{3,2,1,0:T(8,128)}, u32[]{:S(2)}) copy-start(f32[2,8,64,255]{3,2,1,0:T(8,128)} %get-tuple-element.65) | copy-start | bytes 3133444
  11.6 5.2 %copy-start.3 = (f32[2,8,64,1]{3,2,1,0:T(8,128)S(1)}, f32[2,8,64,1]{3,2,1,0:T(8,128)}, u32[]{:S(2)}) copy-start(f32[2,8,64,1]{3,2,1,0:T(8,128)} %get-tuple-element.67) | copy-start | bytes 12292
  17.9 1.8 %copy-start.1 = (f32[2,8,64,256]{3,2,1,0:T(8,128)}, f32[2,8,64,256]{3,2,1,0:T(8,128)S(1)}, u32[]{:S(2)}) copy-start(f32[2,8,64,256]{3,2,1,0:T(8,128)S(1)} %fusion.1) | copy-start | bytes 3145732
  19.7 18.6 %all-to-all-start = ((f32[2,512,256]{2,0,1:T(2,128)}), f32[2,512,256]{2,0,1:T(2,128)S(1)}, u32[]{:S(2)}, u32[]{:S(2)}) async-start(f32[2,512,256]{2,0,1:T(2,128)} %bitcast.8), calls=%async_computation | async-start | bytes 2097152 | tf_op jit(solution)/shard_map/all_to_all | solution.py:114
  42.6 18.9 %all-to-all-start.1 = ((f32[16,64,256]{2,1,0:T(8,128)}), f32[16,64,256]{2,1,0:T(8,128)S(1)}, u32[]{:S(2)}, u32[]{:S(2)}) async-start(f32[16,64,256]{2,1,0:T(8,128)} %copy.21), calls=%async_computation.1 | async-start | bytes 2097152 | tf_op jit(solution)/shard_map/all_to_all | solution.py:115
  62.6 6.3 %collective-permute-start.3 = (f32[1,2,1,64,256]{4,3,1,2,0:T(8,128)S(1)}, f32[1,2,1,64,256]{4,3,1,2,0:T(8,128)S(1)}, u32[]{:S(2)}, u32[]{:S(2)}) collective-permute-start(f32[1,2,1,64,256]{4,3,1,2,0:T(8,128)S(1)} %get-tuple-element.60), channel_id=1, source_target_pairs={{1,0},{2,1},{3,2},{0,3},{5,4},{6,5},{7,6},{4,7},{9,8},{10,9},{11,1... | collective-permute-start | bytes 393224 | tf_op jit(solution)/shard_map/ppermute | solution.py:34
  64.1 6.8 %collective-permute-start.4 = (f32[1,2,1,64,256]{4,3,1,2,0:T(8,128)S(1)}, f32[1,2,1,64,256]{4,3,1,2,0:T(8,128)S(1)}, u32[]{:S(2)}, u32[]{:S(2)}) collective-permute-start(f32[1,2,1,64,256]{4,3,1,2,0:T(8,128)S(1)} %get-tuple-element.61), channel_id=1, source_target_pairs={{0,1},{1,2},{2,3},{3,0},{4,5},{5,6},{6,7},{7,4},{8,9},{9,10},{10,1... | collective-permute-start | bytes 393224 | tf_op jit(solution)/shard_map/ppermute | solution.py:31
  72.8 5.3 %collective-permute-start.5 = (f32[1,2,1,64,256]{4,3,1,2,0:T(8,128)S(1)}, f32[1,2,1,64,256]{4,3,1,2,0:T(8,128)S(1)}, u32[]{:S(2)}, u32[]{:S(2)}) collective-permute-start(f32[1,2,1,64,256]{4,3,1,2,0:T(8,128)S(1)} %get-tuple-element.48), channel_id=1, source_target_pairs={{1,0},{2,1},{3,2},{0,3},{5,4},{6,5},{7,6},{4,7},{9,8},{10,9},{11,1... | collective-permute-start | bytes 393224 | tf_op jit(solution)/shard_map/ppermute | solution.py:34
  73.4 6.8 %collective-permute-start.6 = (f32[1,2,1,64,256]{4,3,1,2,0:T(8,128)S(1)}, f32[1,2,1,64,256]{4,3,1,2,0:T(8,128)S(1)}, u32[]{:S(2)}, u32[]{:S(2)}) collective-permute-start(f32[1,2,1,64,256]{4,3,1,2,0:T(8,128)S(1)} %get-tuple-element.49), channel_id=1, source_target_pairs={{0,1},{1,2},{2,3},{3,0},{4,5},{5,6},{6,7},{7,4},{8,9},{9,10},{10,1... | collective-permute-start | bytes 393224 | tf_op jit(solution)/shard_map/ppermute | solution.py:31
  82.3 5.0 %collective-permute-start.7 = (f32[1,2,1,64,256]{4,3,1,2,0:T(8,128)S(1)}, f32[1,2,1,64,256]{4,3,1,2,0:T(8,128)S(1)}, u32[]{:S(2)}, u32[]{:S(2)}) collective-permute-start(f32[1,2,1,64,256]{4,3,1,2,0:T(8,128)S(1)} %get-tuple-element.36), channel_id=1, source_target_pairs={{1,0},{2,1},{3,2},{0,3},{5,4},{6,5},{7,6},{4,7},{9,8},{10,9},{11,1... | collective-permute-start | bytes 393224 | tf_op jit(solution)/shard_map/ppermute | solution.py:34
  83.4 6.8 %collective-permute-start.8 = (f32[1,2,1,64,256]{4,3,1,2,0:T(8,128)S(1)}, f32[1,2,1,64,256]{4,3,1,2,0:T(8,128)S(1)}, u32[]{:S(2)}, u32[]{:S(2)}) collective-permute-start(f32[1,2,1,64,256]{4,3,1,2,0:T(8,128)S(1)} %get-tuple-element.37), channel_id=1, source_target_pairs={{0,1},{1,2},{2,3},{3,0},{4,5},{5,6},{6,7},{7,4},{8,9},{9,10},{10,1... | collective-permute-start | bytes 393224 | tf_op jit(solution)/shard_map/ppermute | solution.py:31
  92.4 7.0 %collective-permute-start.10 = (f32[1,2,1,64,256]{4,3,1,2,0:T(8,128)S(1)}, f32[1,2,1,64,256]{4,3,1,2,0:T(8,128)S(1)}, u32[]{:S(2)}, u32[]{:S(2)}) collective-permute-start(f32[1,2,1,64,256]{4,3,1,2,0:T(8,128)S(1)} %get-tuple-element.25), channel_id=1, source_target_pairs={{0,1},{1,2},{2,3},{3,0},{4,5},{5,6},{6,7},{7,4},{8,9},{9,10},{10,1... | collective-permute-start | bytes 393224 | tf_op jit(solution)/shard_map/ppermute | solution.py:31
  92.5 6.9 %collective-permute-start.9 = (f32[1,2,1,64,256]{4,3,1,2,0:T(8,128)S(1)}, f32[1,2,1,64,256]{4,3,1,2,0:T(8,128)S(1)}, u32[]{:S(2)}, u32[]{:S(2)}) collective-permute-start(f32[1,2,1,64,256]{4,3,1,2,0:T(8,128)S(1)} %get-tuple-element.24), channel_id=1, source_target_pairs={{1,0},{2,1},{3,2},{0,3},{5,4},{6,5},{7,6},{4,7},{9,8},{10,9},{11,1... | collective-permute-start | bytes 393224 | tf_op jit(solution)/shard_map/ppermute | solution.py:34
  101.8 6.7 %collective-permute-start.11 = (f32[1,2,1,64,256]{4,3,1,2,0:T(8,128)S(1)}, f32[1,2,1,64,256]{4,3,1,2,0:T(8,128)S(1)}, u32[]{:S(2)}, u32[]{:S(2)}) collective-permute-start(f32[1,2,1,64,256]{4,3,1,2,0:T(8,128)S(1)} %get-tuple-element.12), channel_id=1, source_target_pairs={{1,0},{2,1},{3,2},{0,3},{5,4},{6,5},{7,6},{4,7},{9,8},{10,9},{11,1... | collective-permute-start | bytes 393224 | tf_op jit(solution)/shard_map/ppermute | solution.py:34
  106.0 6.8 %collective-permute-start.12 = (f32[1,2,1,64,256]{4,3,1,2,0:T(8,128)S(1)}, f32[1,2,1,64,256]{4,3,1,2,0:T(8,128)S(1)}, u32[]{:S(2)}, u32[]{:S(2)}) collective-permute-start(f32[1,2,1,64,256]{4,3,1,2,0:T(8,128)S(1)} %get-tuple-element.13), channel_id=1, source_target_pairs={{0,1},{1,2},{2,3},{3,0},{4,5},{5,6},{6,7},{7,4},{8,9},{9,10},{10,1... | collective-permute-start | bytes 393224 | tf_op jit(solution)/shard_map/ppermute | solution.py:31
  116.3 20.4 %all-to-all-start.2 = ((f32[2,512,256]{2,0,1:T(2,128)}), f32[2,512,256]{2,0,1:T(2,128)S(1)}, u32[]{:S(2)}, u32[]{:S(2)}) async-start(f32[2,512,256]{2,0,1:T(2,128)} %copy.22), calls=%async_computation.2 | async-start | bytes 2097152 | tf_op jit(solution)/shard_map/all_to_all | solution.py:141
where the time goes:
time: 162 us; the launch traced here: 159 us
  waiting for transfers between devices  72.5 us (45%)
  starting transfers between devices  36 us (22%)
  local copies, waits for them, and re-layouts  18.5 us (11%)
  blocking collectives  17.8 us (11%)
  other arithmetic  10.6 us (7%)
  matrix products  2.16 us (1%)
    all_to_all x1, blocking collectives, body(): lax.all_to_all(restored, 'tm', split_axis=0, concat_axis=1, tiled=True)  17.8 us
    ppermute x6, waiting for transfers between devices, extended(): lax.ppermute(lax.slice_in_dim(block, block.shape[dim] - width, None, axis...  15.5 us
    ppermute x6, starting transfers between devices, extended(): lax.ppermute(lax.slice_in_dim(block, 0, width, axis=dim), axis, backward)  14.8 us
    all_to_all x1, waiting for transfers between devices, body(): lax.all_to_all(flattened, 'tm', split_axis=1, concat_axis=0, tiled=True)  13.9 us
    all_to_all x1, waiting for transfers between devices, body(): lax.all_to_all(solved_rows, 'tm', split_axis=1, concat_axis=0, tiled=True)  13.9 us
    all_to_all x1, waiting for transfers between devices, body(): lax.all_to_all(spectra, 'tm', split_axis=0, concat_axis=1, tiled=True)  13.7 us
    ppermute x6, waiting for transfers between devices, extended(): lax.ppermute(lax.slice_in_dim(block, 0, width, axis=dim), axis, backward)  12.7 us
    all_to_all x1, starting transfers between devices, body(): lax.all_to_all(solved_rows, 'tm', split_axis=1, concat_axis=0, tiled=True)  6.54 us
  transfers between devices with their start and end apart: 16, of which 14 were waited for; matrix products, arithmetic and copies ran while one was open for 3% of the time, Pallas kernels for 0%

commit v1 on v0

v1 whole, which is shorter than its diff:
```python
import functools
import math

import jax
import jax.numpy as jnp
import numpy as np
from jax import lax
from jax.experimental import pallas as pl
from jax.experimental.pallas import tpu as pltpu
from jax.sharding import PartitionSpec as P

SWEEPS = 6
EARLY = 3

alpha_value = 0.1
time_step = 0.1
couple_first = 0.4
couple_cross = 0.05
reaction_shift = 0.1
relaxation = 0.9

PAD = 8
VMEM_LIMIT = 60 * 1024 * 1024


def ring(axis, step):
    count = lax.axis_size(axis)
    return [(i, (i + step) % count) for i in range(count)]


def hop(block, step):
    return lax.ppermute(block, "space", ring("space", step))


def tile_of(low, high):
    return jnp.concatenate([low, high], axis=0).T


def windows(tile, count):
    third = tile.shape[0]
    size = third // count
    padded = jnp.concatenate([tile[third - PAD :], tile, tile[:PAD]], axis=0)
    return [padded[b * size : b * size + size + 2 * PAD] for b in range(count)]


def pack_own(position, state, initial, out, first, stage):
    count, steps, pairs, rows, lanes = out.shape
    width = state.shape[1]
    third = state.shape[3]
    size = third // count
    for pair in range(pairs):
        tile = tile_of(initial[pair], initial[width - 1 - pair])
        stage[:PAD] = tile[third - PAD :]
        stage[PAD : PAD + third] = tile
        stage[PAD + third :] = tile[:PAD]
        first[pair] = stage[pl.ds(pl.multiple_of(position[0] * size, 8), rows), :]
        for step in range(steps):
            tile = tile_of(state[step, pair], state[step, width - 1 - pair])
            for b, window in enumerate(windows(tile, count)):
                out[b, step, pair] = window


def pack_early(lower, upper, out):
    count, steps, depth, rows, lanes = out.shape
    for step in range(steps):
        for j in range(depth):
            tile = tile_of(lower[step, j], upper[step, depth - 1 - j])
            for b, window in enumerate(windows(tile, count)):
                out[b, step, j] = window


def swap(tile):
    return pltpu.roll(tile, tile.shape[-1] // 2, tile.ndim - 1)


def low_mask(tile):
    lanes = tile.shape[-1]
    return lax.broadcasted_iota(jnp.int32, tile.shape, tile.ndim - 1) < lanes // 2


def pack_late(skip, own, up, down):
    half, late, rows, lanes = up.shape
    pairs = own.shape[1]
    width = 2 * pairs
    depth = SWEEPS

    def step(t, carry):
        for j in range(late):
            a = depth - j
            for out, layer in ((up, width - a), (down, a - 1)):
                pair, in_low = (layer, True) if layer < pairs else (width - 1 - layer, False)
                early = own[t, pair, skip : skip + rows]
                later = own[t + half, pair, skip : skip + rows]
                if in_low:
                    out[t, j] = jnp.where(low_mask(early), early, swap(later))
                else:
                    out[t, j] = jnp.where(low_mask(early), swap(early), later)
        return carry

    lax.fori_loop(0, half, step, 0)


def real_forward(values):
    count = len(values)
    if count == 1:
        return [(values[0], None)]
    if count == 2:
        return [(values[0] + values[1], None), (values[0] - values[1], None)]
    even = real_forward(values[0::2])
    odd = real_forward(values[1::2])
    half = count // 2
    result = [None] * (half + 1)
    for k in range(count // 4 + 1):
        even_real, even_imag = even[k]
        odd_real, odd_imag = odd[k]
        if k == 0:
            result[0] = (even_real + odd_real, None)
            result[half] = (even_real - odd_real, None)
        elif 4 * k == count:
            result[k] = (even_real, -odd_real)
        else:
            cos, sin = math.cos(2 * math.pi * k / count), math.sin(2 * math.pi * k / count)
            if odd_imag is None:
                turned_real, turned_imag = cos * odd_real, -sin * odd_real
            else:
                turned_real = cos * odd_real + sin * odd_imag
                turned_imag = cos * odd_imag - sin * odd_real
            if even_imag is None:
                result[k] = (even_real + turned_real, turned_imag)
                result[half - k] = (even_real - turned_real, turned_imag)
            else:
                result[k] = (even_real + turned_real, even_imag + turned_imag)
                result[half - k] = (even_real - turned_real, turned_imag - even_imag)
    return result


def real_inverse(modes):
    half = len(modes) - 1
    count = 2 * half
    if count == 2:
        return [modes[0][0] + modes[1][0], modes[0][0] - modes[1][0]]
    even, odd = [], []
    for k in range(count // 4 + 1):
        real, imag = modes[k]
        other_real, other_imag = modes[half - k]
        if k == 0:
            even.append((real + other_real, None))
            odd.append((real - other_real, None))
        elif 4 * k == count:
            even.append((2.0 * real, None))
            odd.append((-2.0 * imag, None))
        else:
            cos, sin = math.cos(2 * math.pi * k / count), math.sin(2 * math.pi * k / count)
            even.append((real + other_real, imag - other_imag))
            minus_real, minus_imag = real - other_real, imag + other_imag
            odd.append((cos * minus_real - sin * minus_imag, sin * minus_real + cos * minus_imag))
    result = [None] * count
    result[0::2] = real_inverse(even)
    result[1::2] = real_inverse(odd)
    return result


def mode_inverses(horizon):
    rho = alpha_value ** (1.0 / horizon)
    angles = 2.0 * math.pi * np.arange(horizon // 2 + 1) / horizon
    shift = (
        1.0 + reaction_shift + 2.0 * couple_first + 4.0 * couple_cross - rho * np.cos(angles)
    ) + 1j * rho * np.sin(angles)
    return 1.0 / shift


def sweep_table(horizon):
    inverse = relaxation * mode_inverses(horizon)
    rows = [(inverse[0].real, 0.0, 0.0, inverse[-1].real)]
    rows += [(v.real, -v.imag, v.imag, v.real) for v in inverse[1:-1]]
    return couple_cross * np.array(rows, np.float32)


def second_sum(tile):
    lanes = tile.shape[-1]
    axis = tile.ndim - 1
    place = lax.broadcasted_iota(jnp.int32, tile.shape, axis) % (lanes // 2)
    before = jnp.where(
        place == 0, pltpu.roll(tile, lanes // 2 + 1, axis), pltpu.roll(tile, 1, axis)
    )
    after = jnp.where(
        place == lanes // 2 - 1,
        pltpu.roll(tile, lanes // 2 - 1, axis),
        pltpu.roll(tile, lanes - 1, axis),
    )
    return before + after


def solve(skip, table, up, down, first, first_low, first_high, own, early, out, state, base, ping, pong, sems):
    horizon, pairs = own.shape[:2]
    taken = early.shape[1]
    depth = SWEEPS
    late = depth - taken
    rows = own.shape[2]
    post_rows = up.shape[2]
    block = rows - 2 * PAD
    last = depth + pairs - 1
    half = horizon // 2
    at = PAD
    copies = [
        pltpu.make_async_copy(
            own, state.at[pl.ds(1, horizon), pl.ds(depth, pairs), pl.ds(at, rows)], sems.at[0]
        ),
        pltpu.make_async_copy(
            early, state.at[pl.ds(1, horizon), pl.ds(late, taken), pl.ds(at, rows)], sems.at[1]
        ),
    ]
    for copy in copies:
        copy.start()

    for i in range(pairs):
        state[0, depth + i, at : at + rows] = first[i]
    for a in range(1, depth):
        if a <= pairs:
            low, high = first_low[a - 1], first_high[a - 1]
            tile = swap(jnp.where(low_mask(low), high, low))
        else:
            low, high = first_low[2 * pairs - a], first_high[2 * pairs - a]
            tile = jnp.where(low_mask(low), low, high)
        state[0, depth - a, at : at + rows] = tile

    def place(t, carry):
        for j in range(late):
            low, high = up[t, j], down[t, j]
            mask = low_mask(low)
            here = slice(at + skip, at + skip + post_rows)
            state[1 + t, j, here] = jnp.where(mask, low, swap(high))
            state[1 + half + t, j, here] = jnp.where(mask, swap(low), high)
        return carry

    lax.fori_loop(0, half, place, 0)
    for copy in copies:
        copy.wait()

    def mirror(t, carry):
        state[t, last + 1, at : at + rows] = swap(state[t, last, at : at + rows])
        return carry

    lax.fori_loop(0, horizon + 1, mirror, 0)

    def weigh(t, carry):
        for x in range(1, last + 1):
            s = state[t + 1, x, at : at + rows]
            along = state[t + 1, x - 1, at : at + rows] + state[t + 1, x + 1, at : at + rows]
            across = (
                state[t + 1, x, at - 1 : at + rows - 1]
                + state[t + 1, x, at + 1 : at + rows + 1]
                + second_sum(s)
            )
            centre = time_step - 1.0 - 2.0 * couple_first - 4.0 * couple_cross
            ping[t, x, at : at + rows] = (
                (state[t, x, at : at + rows] + couple_first * along)
                + (couple_cross * across + s * (centre - time_step * (s * s)))
            )
        return carry

    lax.fori_loop(0, horizon, weigh, 0)

    inverses = mode_inverses(horizon)
    weights = [alpha_value ** (n / horizon) for n in range(horizon)]
    tiles = rows // 8

    def transform(index, carry):
        x = 1 + index // tiles
        r = pl.ds(pl.multiple_of(at + (index % tiles) * 8, 8), 8)
        spectrum = real_forward([weights[n] * ping[n, x, r, :] for n in range(horizon)])
        for k, (real, imag) in enumerate(spectrum):
            c = relaxation * inverses[k]
            if k == 0:
                base[0, x, r, :] = float(c.real) * real
            elif k == half:
                base[half, x, r, :] = float(c.real) * real
            else:
                base[k, x, r, :] = float(c.real) * real - float(c.imag) * imag
                base[half + k, x, r, :] = float(c.imag) * real + float(c.real) * imag
        return carry

    lax.fori_loop(0, last * tiles, transform, 0)

    def mirror_base(k, carry):
        base[k, last + 1, at : at + rows] = swap(base[k, last, at : at + rows])
        return carry

    lax.fori_loop(0, horizon, mirror_base, 0)

    def sweep(number, source, target):
        def pair(k, carry):
            a, b, c, d = [table[k, i] for i in range(4)]
            for x in range(number + 1, last + 1):
                near = []
                for m in (k, half + k):
                    v = source[m, x, at : at + rows]
                    along = source[m, x - 1, at : at + rows] + source[m, x + 1, at : at + rows]
                    across = (
                        source[m, x, at - 1 : at + rows - 1]
                        + source[m, x, at + 1 : at + rows + 1]
                        + second_sum(v)
                    )
                    near.append(
                        (
                            base[m, x, at : at + rows] + (1.0 - relaxation) * v,
                            (couple_first / couple_cross) * along + across,
                        )
                    )
                (rest_real, near_real), (rest_imag, near_imag) = near
                real = rest_real + (a * near_real + b * near_imag)
                imag = rest_imag + (c * near_real + d * near_imag)
                target[k, x, at : at + rows] = real
                target[half + k, x, at : at + rows] = imag
                if x == last:
                    target[k, last + 1, at : at + rows] = swap(real)
                    target[half + k, last + 1, at : at + rows] = swap(imag)
            return carry

        lax.fori_loop(0, half, pair, 0)

    source = base
    for number in range(1, SWEEPS):
        target = ping if number % 2 else pong
        sweep(number, source, target)
        source = target

    kept = block // 8

    def restore(index, carry):
        i = index // kept
        r = pl.ds(pl.multiple_of(at + PAD + (index % kept) * 8, 8), 8)
        modes = [(source[0, depth + i, r, :], None)]
        modes += [
            (source[k, depth + i, r, :], source[half + k, depth + i, r, :]) for k in range(1, half)
        ]
        modes += [(source[half, depth + i, r, :], None)]
        place_at = pl.ds(pl.multiple_of((index % kept) * 8, 8), 8)
        for n, value in enumerate(real_inverse(modes)):
            out[n, i, place_at, :] = (1.0 / (horizon * weights[n])) * value
        return carry

    lax.fori_loop(0, pairs * kept, restore, 0)


def finish(state, pieces, updated):
    count, steps, pairs, size, lanes = pieces.shape
    width = 2 * pairs
    second = lanes // 2
    for step in range(steps):
        for pair in range(pairs):
            tile = jnp.concatenate([pieces[b, step, pair] for b in range(count)], axis=0).T
            updated[step, pair] = state[step, pair] + tile[:second]
            updated[step, width - 1 - pair] = state[step, width - 1 - pair] + tile[second:]


def residual_of(state, carried, low, high, out):
    steps, width = state.shape[:2]
    for step in range(steps):
        for layer in range(width):
            s = state[step, layer]
            below = low[step] if layer == 0 else state[step, layer - 1]
            above = high[step] if layer == width - 1 else state[step, layer + 1]
            before = carried[layer] if step == 0 else state[step - 1, layer]
            across = (
                pltpu.roll(s, 1, 0)
                + pltpu.roll(s, s.shape[0] - 1, 0)
                + pltpu.roll(s, 1, 1)
                + pltpu.roll(s, s.shape[1] - 1, 1)
            )
            centre = time_step - 1.0 - 2.0 * couple_first - 4.0 * couple_cross
            out[step, layer] = (
                (before + couple_first * (below + above))
                + (couple_cross * across + s * (centre - time_step * (s * s)))
            )


def vmem(count):
    return [pl.BlockSpec(memory_space=pltpu.VMEM)] * count


def shape_of(*dims):
    return jax.ShapeDtypeStruct(dims, jnp.float32)


def params():
    return pltpu.CompilerParams(vmem_limit_bytes=VMEM_LIMIT)


def cost(flops, bytes_accessed):
    return pl.CostEstimate(flops=int(flops), bytes_accessed=int(bytes_accessed), transcendentals=0)


def body(state, initial):
    steps, width, second, third = state.shape
    count = lax.axis_size("tm")
    horizon = steps * count
    position = lax.axis_index("tm")
    depth, taken = SWEEPS, EARLY
    late = depth - taken
    pairs = width // 2
    size = third // count
    rows = size + 2 * PAD
    lanes = 2 * second
    skip = 4
    post_rows = rows - 2 * skip

    lower = hop(state[:, width - taken :], 1)
    upper = hop(state[:, :taken], -1)

    sent, first = pl.pallas_call(
        pack_own,
        out_shape=(shape_of(count, steps, pairs, rows, lanes), shape_of(pairs, rows, lanes)),
        in_specs=[pl.BlockSpec(memory_space=pltpu.SMEM)] + vmem(2),
        out_specs=vmem(2),
        scratch_shapes=[pltpu.VMEM((third + 2 * PAD, lanes), jnp.float32)],
        compiler_params=params(),
        cost_estimate=cost(4e6, 3e6),
        name="pack_own",
    )(position.reshape(1), state, initial)
    first_low = hop(first, 1)
    first_high = hop(first, -1)
    own = lax.all_to_all(sent, "tm", split_axis=0, concat_axis=0, tiled=True)
    own = own.reshape(horizon, pairs, rows, lanes)

    sent_early = pl.pallas_call(
        pack_early,
        out_shape=shape_of(count, steps, taken, rows, lanes),
        in_specs=vmem(2),
        out_specs=pl.BlockSpec(memory_space=pltpu.VMEM),
        compiler_params=params(),
        cost_estimate=cost(4e6, 3e6),
        name="pack_early",
    )(lower, upper)

    up, down = pl.pallas_call(
        functools.partial(pack_late, skip),
        out_shape=(shape_of(horizon // 2, late, post_rows, lanes),) * 2,
        in_specs=vmem(1),
        out_specs=vmem(2),
        compiler_params=params(),
        cost_estimate=cost(2e6, 2e6),
        name="pack_late",
    )(own)
    late_low = hop(up, 1)
    late_high = hop(down, -1)

    early = lax.all_to_all(sent_early, "tm", split_axis=0, concat_axis=0, tiled=True)
    early = early.reshape(horizon, taken, rows, lanes)

    carried = lax.ppermute(state[steps - 1], "tm", [(i, i + 1) for i in range(count - 1)])
    carried = jnp.where(position == 0, initial, carried)
    residual = pl.pallas_call(
        residual_of,
        out_shape=shape_of(*state.shape),
        in_specs=vmem(4),
        out_specs=pl.BlockSpec(memory_space=pltpu.VMEM),
        compiler_params=params(),
        cost_estimate=cost(6e6, 3e6),
        name="residual",
    )(state, carried, lower[:, taken - 1], upper[:, 0])

    scratch_rows = rows + 2 * PAD
    layers = depth + pairs + 1
    any_space = pl.BlockSpec(memory_space=pl.ANY)
    moved = pl.pallas_call(
        functools.partial(solve, skip),
        out_shape=shape_of(horizon, pairs, size, lanes),
        in_specs=[pl.BlockSpec(memory_space=pltpu.SMEM)] + vmem(5) + [any_space] * 2,
        out_specs=pl.BlockSpec(memory_space=pltpu.VMEM),
        scratch_shapes=[
            pltpu.VMEM((horizon + 1, layers, scratch_rows, lanes), jnp.float32),
            pltpu.VMEM((horizon, layers, scratch_rows, lanes), jnp.float32),
            pltpu.VMEM((horizon, layers, scratch_rows, lanes), jnp.float32),
            pltpu.VMEM((horizon, layers, scratch_rows, lanes), jnp.float32),
            pltpu.SemaphoreType.DMA((2,)),
        ],
        compiler_params=params(),
        cost_estimate=cost(1e8, 8e6),
        name="solve",
    )(jnp.asarray(sweep_table(horizon)), late_low, late_high, first, first_low, first_high, own, early)

    moved = moved.reshape(count, steps, pairs, size, lanes)
    pieces = lax.all_to_all(moved, "tm", split_axis=0, concat_axis=0, tiled=True)
    updated = pl.pallas_call(
        finish,
        out_shape=shape_of(*state.shape),
        in_specs=vmem(2),
        out_specs=pl.BlockSpec(memory_space=pltpu.VMEM),
        compiler_params=params(),
        cost_estimate=cost(2e6, 3e6),
        name="finish",
    )(state, pieces)
    return (updated, residual)


def solution(mesh):
    in_specs = (P("tm", "space", None, None), P("space", None, None))
    out_specs = (P("tm", "space", None, None), P("tm", "space", None, None))
    return jax.shard_map(body, mesh=mesh, in_specs=in_specs, out_specs=out_specs, check_vma=False)
```

time: 162 us -> 134 us (0.83); the launches traced: 159 us -> 133 us
  Pallas kernels: 0 us -> 46 us
  waiting for transfers between devices: 72.5 us -> 52.9 us
  blocking collectives: 17.8 us -> 0 us
  local copies, waits for them, and re-layouts: 18.5 us -> 5.75 us
  other arithmetic: 10.6 us -> 0.88 us
  starting transfers between devices: 36 us -> 27 us
  matrix products: 2.16 us -> 0 us
    pallas_call x0 -> x6, Pallas kernels: none -> 46 us  [the longest x1 31.5 us: body(): pl.pallas_call(functools.partial(solve, skip), out_shape=shape_of(horizon...]
    all_to_all x3, waiting for transfers between devices: 41.4 us -> 0.01 us  [the longest x1 0.01 us: body(): lax.all_to_all(moved, 'tm', split_axis=0, concat_axis=0, tiled=True)]
    ppermute x13 -> x7, waiting for transfers between devices: 31.1 us -> 52.9 us  [the longest x6 37.6 us: hop(): return lax.ppermute(block, 'space', ring('space', step))]
    all_to_all x1 -> x0, blocking collectives: 17.8 us -> none  [body(): lax.all_to_all(restored, 'tm', split_axis=0, concat_axis=1, tiled=True)]
    add x18 -> x0, other arithmetic: 9.31 us -> none  [the longest x5 3.99 us: body(): fields + nearby]
    slice x30 -> x1, local copies, waits for them, and re-layouts: 7.36 us -> 0.05 us  [body(): upper = hop(state[:, :taken], -1)]
    ppermute x13 -> x7, starting transfers between devices: 19.8 us -> 13.6 us  [the longest x6 11.6 us: hop(): return lax.ppermute(block, 'space', ring('space', step))]
    add x2 -> x0, local copies, waits for them, and re-layouts: 3.56 us -> none  [the longest x1 1.78 us: body(): before - state + laplace + time_step * (state - state * state * state)]
  transfers between devices with their start and end apart: 16 -> 10, of which waited for: 14 -> 5; matrix products, arithmetic and copies ran while one was open for 3% -> 4% of each run, Pallas kernels for 0% -> 7%
where the time goes in v1:
time: 134 us; the launch traced here: 133 us
  waiting for transfers between devices  52.9 us (39%)
  Pallas kernels  46 us (34%)
  starting transfers between devices  27 us (20%)
  local copies, waits for them, and re-layouts  5.75 us (4%)
    ppermute x6, waiting for transfers between devices, hop(): return lax.ppermute(block, 'space', ring('space', step))  37.6 us
    pallas_call x1, Pallas kernels, body(): pl.pallas_call(functools.partial(solve, skip), out_shape=shape_of(horizon...  31.5 us
    ppermute x1, waiting for transfers between devices, body(): lax.ppermute(state[steps - 1], 'tm', [(i, i + 1) for i in range(count - 1)])  15.3 us
    ppermute x6, starting transfers between devices, hop(): return lax.ppermute(block, 'space', ring('space', step))  11.6 us
    all_to_all x1, starting transfers between devices, body(): lax.all_to_all(sent_early, 'tm', split_axis=0, concat_axis=0, tiled=True)  4.68 us
    all_to_all x1, starting transfers between devices, body(): lax.all_to_all(moved, 'tm', split_axis=0, concat_axis=0, tiled=True)  4.36 us
    all_to_all x1, starting transfers between devices, body(): own = lax.all_to_all(sent, 'tm', split_axis=0, concat_axis=0, tiled=True)  4.35 us
    pallas_call x1, Pallas kernels, body(): pl.pallas_call(functools.partial(pack_late, skip), out_shape=(shape_of(ho...  3.14 us
  transfers between devices with their start and end apart: 10, of which 5 were waited for; matrix products, arithmetic and copies ran while one was open for 4% of the time, Pallas kernels for 7%

profile of v1, /device:TPU:4, one launch (start us, length us, event | category | flops | bytes accessed | tf_op | source)
XLA Modules:
  0.0 133.3 jit_solution(13882098792651892215)
XLA Ops:
  0.6 3.0 %pack_own.1 = (f32[8,2,4,48,128]{4,3,2,1,0:T(8,128)}, f32[4,48,128]{2,1,0:T(8,128)}) custom-call(s32[1]{0:T(128)} %bitcast.position, f32[2,8,64,256]{3,2,1,0:T(8,128)} %state.5, f32[8,64,256]{2,1,0:T(8,128)} %initial.1), custom_call_target="tpu_custom_call" | custom-call | flops 4000000 | bytes 3000000 | tf_op jit(solution)/shard_map/pack_own/pallas_call | solution.py:411
  3.6 0.0 copy-start
  3.6 4.3 %all-to-all-start = ((f32[8,2,4,48,128]{4,3,2,1,0:T(8,128)}), f32[8,2,4,48,128]{4,3,2,1,0:T(8,128)S(1)}, u32[]{:S(2)}, u32[]{:S(2)}) async-start(f32[8,2,4,48,128]{4,3,2,1,0:T(8,128)} %get-tuple-element.6), calls=%async_computation | async-start | bytes 3145728 | tf_op jit(solution)/shard_map/all_to_all | solution.py:423
  8.0 0.0 copy-done
  8.0 0.1 fusion
  8.1 1.6 %collective-permute-start.4 = (f32[2,3,64,256]{3,2,0,1:T(8,128)S(1)}, f32[2,3,64,256]{3,2,0,1:T(8,128)S(1)}, u32[]{:S(2)}, u32[]{:S(2)}) collective-permute-start(f32[2,3,64,256]{3,2,0,1:T(8,128)S(1)} %copy.9), channel_id=1, source_target_pairs={{0,1},{1,2},{2,3},{3,0},{4,5},{5,6},{6,7},{7,4},{8,9},{9,10},{10,1... | collective-permute-start | bytes 1179656 | tf_op jit(solution)/shard_map/ppermute | solution.py:32
  9.7 2.3 %collective-permute-start.5 = (f32[2,3,64,256]{3,2,0,1:T(8,128)S(1)}, f32[2,3,64,256]{3,2,0,1:T(8,128)S(1)}, u32[]{:S(2)}, u32[]{:S(2)}) collective-permute-start(f32[2,3,64,256]{3,2,0,1:T(8,128)S(1)} %copy.10), channel_id=1, source_target_pairs={{0,3},{1,0},{2,1},{3,2},{4,7},{5,4},{6,5},{7,6},{8,11},{9,8},{10,9... | collective-permute-start | bytes 1179656 | tf_op jit(solution)/shard_map/ppermute | solution.py:32
  12.0 9.9 %collective-permute-done.4 = f32[2,3,64,256]{3,2,0,1:T(8,128)S(1)} collective-permute-done((f32[2,3,64,256]{3,2,0,1:T(8,128)S(1)}, f32[2,3,64,256]{3,2,0,1:T(8,128)S(1)}, u32[]{:S(2)}, u32[]{:S(2)}) %collective-permute-start.4) | collective-permute-done | bytes 393248 | tf_op jit(solution)/shard_map/ppermute | solution.py:32
  22.0 0.8 copy.7.lower
  22.7 6.3 %collective-permute-done.5 = f32[2,3,64,256]{3,2,0,1:T(8,128)S(1)} collective-permute-done((f32[2,3,64,256]{3,2,0,1:T(8,128)S(1)}, f32[2,3,64,256]{3,2,0,1:T(8,128)S(1)}, u32[]{:S(2)}, u32[]{:S(2)}) %collective-permute-start.5) | collective-permute-done | bytes 393248 | tf_op jit(solution)/shard_map/ppermute | solution.py:32
  29.1 0.8 copy.8.upper
  29.8 2.4 %pack_early.1 = f32[8,2,3,48,128]{4,3,2,1,0:T(8,128)} custom-call(f32[2,3,64,256]{3,2,1,0:T(8,128)} %copy.7.lower, f32[2,3,64,256]{3,2,1,0:T(8,128)} %copy.8.upper), custom_call_target="tpu_custom_call" | custom-call | flops 4000000 | bytes 3000000 | tf_op jit(solution)/shard_map/pack_early/pallas_call | solution.py:426
  32.2 0.0 copy-start.6
  32.3 0.0 all-to-all-done
  32.3 0.0 copy-start.1
  32.3 4.7 %all-to-all-start.1 = ((f32[8,2,3,48,128]{4,3,2,1,0:T(8,128)}), f32[8,2,3,48,128]{4,3,2,1,0:T(8,128)}, u32[]{:S(2)}, u32[]{:S(2)}) async-start(f32[8,2,3,48,128]{4,3,2,1,0:T(8,128)} %pack_early.1), calls=%async_computation.1 | async-start | bytes 2359296 | tf_op jit(solution)/shard_map/all_to_all | solution.py:448
  36.9 0.0 copy-done.1
  36.9 3.1 %pack_late.1 = (f32[8,3,40,128]{3,2,1,0:T(8,128)}, f32[8,3,40,128]{3,2,1,0:T(8,128)}) custom-call(f32[16,4,48,128]{3,2,1,0:T(8,128)} %bitcast.10), custom_call_target="tpu_custom_call" | custom-call | flops 2000000 | bytes 2000000 | tf_op jit(solution)/shard_map/pack_late/pallas_call | solution.py:436
  40.1 1.0 collective-permute-start
  41.1 2.8 %collective-permute-start.1 = (f32[8,3,40,128]{3,2,1,0:T(8,128)}, f32[8,3,40,128]{3,2,1,0:T(8,128)S(1)}, u32[]{:S(2)}, u32[]{:S(2)}) collective-permute-start(f32[8,3,40,128]{3,2,1,0:T(8,128)} %get-tuple-element.8), channel_id=1, source_target_pairs={{0,3},{1,0},{2,1},{3,2},{4,7},{5,4},{6,5},{7,6},{8,11},{9,8},{10,9... | collective-permute-start | bytes 1474568 | tf_op jit(solution)/shard_map/ppermute | solution.py:32
  43.9 0.0 copy-done.6
  43.9 0.0 collective-permute-start.2
  43.9 3.8 %collective-permute-start.3 = (f32[4,48,128]{2,1,0:T(8,128)S(1)}, f32[4,48,128]{2,1,0:T(8,128)S(1)}, u32[]{:S(2)}, u32[]{:S(2)}) collective-permute-start(f32[4,48,128]{2,1,0:T(8,128)S(1)} %copy-done.6), channel_id=1, source_target_pairs={{0,3},{1,0},{2,1},{3,2},{4,7},{5,4},{6,5},{7,6},{8,11},{9,8},{10,9... | collective-permute-start | bytes 294920 | tf_op jit(solution)/shard_map/ppermute | solution.py:32
  47.7 21.1 %collective-permute-done.2.first_low = f32[4,48,128]{2,1,0:T(8,128)S(1)} collective-permute-done((f32[4,48,128]{2,1,0:T(8,128)S(1)}, f32[4,48,128]{2,1,0:T(8,128)S(1)}, u32[]{:S(2)}, u32[]{:S(2)}) %collective-permute-start.2) | collective-permute-done | bytes 98336 | tf_op jit(solution)/shard_map/ppermute | solution.py:32
  68.9 0.2 collective-permute-done.3.first_high
  69.1 0.0 all-to-all-done.1
  69.1 0.0 collective-permute-done.up
  69.1 0.0 copy-start.4
  69.1 0.0 collective-permute-done.1.down
  69.1 0.0 copy-start.5
  69.1 0.4 copy-done.7
  69.5 0.2 copy-done.8
  69.7 0.2 copy-done.4
  69.9 0.2 copy-done.5
  70.0 31.5 %solve.1 = f32[16,4,32,128]{3,2,1,0:T(8,128)} custom-call(f32[8,4]{1,0:T(8,128)} %constant.10.clone.table, f32[8,3,40,128]{3,2,1,0:T(8,128)} %copy-done.4, f32[8,3,40,128]{3,2,1,0:T(8,128)} %copy-done.5, f32[4,48,128]{2,1,0:T(8,128)} %get-tuple-element.9.first, f32[4,48,128]{2,1,0:T(8,128)} %copy-done.7, f32[4,48,128]{2,1,0:T(8,128)} %copy-done.8, ...), custom_call_target="tpu_custom_call" | custom-call | flops 100000000 | bytes 8000000 | tf_op jit(solution)/shard_map/solve/pallas_call | solution.py:466
  101.6 0.0 copy-start.3
  101.6 4.4 %all-to-all-start.2 = ((f32[8,2,4,32,128]{4,3,2,1,0:T(8,128)}), f32[8,2,4,32,128]{4,3,2,1,0:T(8,128)S(1)}, u32[]{:S(2)}, u32[]{:S(2)}) async-start(f32[8,2,4,32,128]{4,3,2,1,0:T(8,128)} %bitcast.12), calls=%async_computation.2 | async-start | bytes 2097152 | tf_op jit(solution)/shard_map/all_to_all | solution.py:484
  105.9 0.8 slice_bitcast_fusion
  106.8 2.0 %collective-permute-start.6 = (f32[8,64,256]{2,1,0:T(8,128)}, f32[8,64,256]{2,1,0:T(8,128)S(1)}, u32[]{:S(2)}, u32[]{:S(2)}) collective-permute-start(f32[8,64,256]{2,1,0:T(8,128)} %slice_bitcast_fusion), channel_id=1, source_target_pairs={{0,4},{4,8},{8,12},{12,16},{16,20},{20,24},{24,28},{1,5},{5,9},{9,... | collective-permute-start | bytes 1572872 | tf_op jit(solution)/shard_map/ppermute | solution.py:451
  108.8 0.7 slice_bitcast_fusion.1.high
  109.4 0.7 slice_bitcast_fusion.2.low
  110.1 15.3 %collective-permute-done.6 = f32[8,64,256]{2,1,0:T(8,128)S(1)} collective-permute-done((f32[8,64,256]{2,1,0:T(8,128)}, f32[8,64,256]{2,1,0:T(8,128)S(1)}, u32[]{:S(2)}, u32[]{:S(2)}) %collective-permute-start.6) | collective-permute-done | bytes 524320 | tf_op jit(solution)/shard_map/ppermute | solution.py:451
  125.4 0.0 copy-done.3
  125.5 0.9 broadcast_select_fusion.carried
  126.3 3.1 %residual.1 = f32[2,8,64,256]{3,2,1,0:T(8,128)} custom-call(f32[2,8,64,256]{3,2,1,0:T(8,128)} %state.5, f32[8,64,256]{2,1,0:T(8,128)} %broadcast_select_fusion.carried, f32[2,64,256]{2,1,0:T(8,128)} %slice_bitcast_fusion.2.low, f32[2,64,256]{2,1,0:T(8,128)} %slice_bitcast_fusion.1.high), custom_call_target="tpu_custom_call" | custom-call | flops 6000000 | bytes 3000000 | tf_op jit(solution)/shard_map/residual/pallas_call | solution.py:453
  129.5 0.0 all-to-all-done.2.pieces
  129.5 1.0 copy-done.2
  130.5 2.8 %finish.1 = f32[2,8,64,256]{3,2,1,0:T(8,128)} custom-call(f32[2,8,64,256]{3,2,1,0:T(8,128)} %state.5, f32[8,2,4,32,128]{4,3,2,1,0:T(8,128)} %copy-done.2), custom_call_target="tpu_custom_call" | custom-call | flops 2000000 | bytes 3000000 | tf_op jit(solution)/shard_map/finish/pallas_call | solution.py:485
  (5 shorter events, 0.1 us)
Async XLA Ops:
  3.6 4.4 %copy-start = (f32[2,8,64,256]{3,2,1,0:T(8,128)S(1)}, f32[2,8,64,256]{3,2,1,0:T(8,128)}, u32[]{:S(2)}) copy-start(f32[2,8,64,256]{3,2,1,0:T(8,128)} %state.5) | copy-start | bytes 3145732
  3.6 28.6 %all-to-all-start = ((f32[8,2,4,48,128]{4,3,2,1,0:T(8,128)}), f32[8,2,4,48,128]{4,3,2,1,0:T(8,128)S(1)}, u32[]{:S(2)}, u32[]{:S(2)}) async-start(f32[8,2,4,48,128]{4,3,2,1,0:T(8,128)} %get-tuple-element.6), calls=%async_computation | async-start | bytes 3145728 | tf_op jit(solution)/shard_map/all_to_all | solution.py:423
  8.1 13.9 %collective-permute-start.4 = (f32[2,3,64,256]{3,2,0,1:T(8,128)S(1)}, f32[2,3,64,256]{3,2,0,1:T(8,128)S(1)}, u32[]{:S(2)}, u32[]{:S(2)}) collective-permute-start(f32[2,3,64,256]{3,2,0,1:T(8,128)S(1)} %copy.9), channel_id=1, source_target_pairs={{0,1},{1,2},{2,3},{3,0},{4,5},{5,6},{6,7},{7,4},{8,9},{9,10},{10,1... | collective-permute-start | bytes 1179656 | tf_op jit(solution)/shard_map/ppermute | solution.py:32
  9.7 19.3 %collective-permute-start.5 = (f32[2,3,64,256]{3,2,0,1:T(8,128)S(1)}, f32[2,3,64,256]{3,2,0,1:T(8,128)S(1)}, u32[]{:S(2)}, u32[]{:S(2)}) collective-permute-start(f32[2,3,64,256]{3,2,0,1:T(8,128)S(1)} %copy.10), channel_id=1, source_target_pairs={{0,3},{1,0},{2,1},{3,2},{4,7},{5,4},{6,5},{7,6},{8,11},{9,8},{10,9... | collective-permute-start | bytes 1179656 | tf_op jit(solution)/shard_map/ppermute | solution.py:32
  32.2 11.7 %copy-start.6 = (f32[4,48,128]{2,1,0:T(8,128)S(1)}, f32[4,48,128]{2,1,0:T(8,128)}, u32[]{:S(2)}) copy-start(f32[4,48,128]{2,1,0:T(8,128)} %get-tuple-element.9.first) | copy-start | bytes 294916
  32.3 4.7 %copy-start.1 = (f32[8,2,4,48,128]{4,3,2,1,0:T(8,128)}, f32[8,2,4,48,128]{4,3,2,1,0:T(8,128)S(1)}, u32[]{:S(2)}) copy-start(f32[8,2,4,48,128]{4,3,2,1,0:T(8,128)S(1)} %all-to-all-done) | copy-start | bytes 4718596
  32.3 36.8 %all-to-all-start.1 = ((f32[8,2,3,48,128]{4,3,2,1,0:T(8,128)}), f32[8,2,3,48,128]{4,3,2,1,0:T(8,128)}, u32[]{:S(2)}, u32[]{:S(2)}) async-start(f32[8,2,3,48,128]{4,3,2,1,0:T(8,128)} %pack_early.1), calls=%async_computation.1 | async-start | bytes 2359296 | tf_op jit(solution)/shard_map/all_to_all | solution.py:448
  40.1 29.0 %collective-permute-start = (f32[8,3,40,128]{3,2,1,0:T(8,128)}, f32[8,3,40,128]{3,2,1,0:T(8,128)S(1)}, u32[]{:S(2)}, u32[]{:S(2)}) collective-permute-start(f32[8,3,40,128]{3,2,1,0:T(8,128)} %get-tuple-element.7), channel_id=1, source_target_pairs={{0,1},{1,2},{2,3},{3,0},{4,5},{5,6},{6,7},{7,4},{8,9},{9,10},{10,1... | collective-permute-start | bytes 1474568 | tf_op jit(solution)/shard_map/ppermute | solution.py:32
  41.1 28.0 %collective-permute-start.1 = (f32[8,3,40,128]{3,2,1,0:T(8,128)}, f32[8,3,40,128]{3,2,1,0:T(8,128)S(1)}, u32[]{:S(2)}, u32[]{:S(2)}) collective-permute-start(f32[8,3,40,128]{3,2,1,0:T(8,128)} %get-tuple-element.8), channel_id=1, source_target_pairs={{0,3},{1,0},{2,1},{3,2},{4,7},{5,4},{6,5},{7,6},{8,11},{9,8},{10,9... | collective-permute-start | bytes 1474568 | tf_op jit(solution)/shard_map/ppermute | solution.py:32
  43.9 25.0 %collective-permute-start.2 = (f32[4,48,128]{2,1,0:T(8,128)S(1)}, f32[4,48,128]{2,1,0:T(8,128)S(1)}, u32[]{:S(2)}, u32[]{:S(2)}) collective-permute-start(f32[4,48,128]{2,1,0:T(8,128)S(1)} %copy-done.6), channel_id=1, source_target_pairs={{0,1},{1,2},{2,3},{3,0},{4,5},{5,6},{6,7},{7,4},{8,9},{9,10},{10,1... | collective-permute-start | bytes 294920 | tf_op jit(solution)/shard_map/ppermute | solution.py:32
  43.9 25.1 %collective-permute-start.3 = (f32[4,48,128]{2,1,0:T(8,128)S(1)}, f32[4,48,128]{2,1,0:T(8,128)S(1)}, u32[]{:S(2)}, u32[]{:S(2)}) collective-permute-start(f32[4,48,128]{2,1,0:T(8,128)S(1)} %copy-done.6), channel_id=1, source_target_pairs={{0,3},{1,0},{2,1},{3,2},{4,7},{5,4},{6,5},{7,6},{8,11},{9,8},{10,9... | collective-permute-start | bytes 294920 | tf_op jit(solution)/shard_map/ppermute | solution.py:32
  68.9 0.6 copy-start.7
  69.1 0.6 copy-start.8
  69.1 0.8 copy-start.4
  69.1 0.9 copy-start.5
  101.6 23.9 %copy-start.3 = (f32[8,64,256]{2,1,0:T(8,128)S(1)}, f32[8,64,256]{2,1,0:T(8,128)}, u32[]{:S(2)}) copy-start(f32[8,64,256]{2,1,0:T(8,128)} %initial.1) | copy-start | bytes 1572868
  101.6 27.9 %all-to-all-start.2 = ((f32[8,2,4,32,128]{4,3,2,1,0:T(8,128)}), f32[8,2,4,32,128]{4,3,2,1,0:T(8,128)S(1)}, u32[]{:S(2)}, u32[]{:S(2)}) async-start(f32[8,2,4,32,128]{4,3,2,1,0:T(8,128)} %bitcast.12), calls=%async_computation.2 | async-start | bytes 2097152 | tf_op jit(solution)/shard_map/all_to_all | solution.py:484
  106.8 18.7 %collective-permute-start.6 = (f32[8,64,256]{2,1,0:T(8,128)}, f32[8,64,256]{2,1,0:T(8,128)S(1)}, u32[]{:S(2)}, u32[]{:S(2)}) collective-permute-start(f32[8,64,256]{2,1,0:T(8,128)} %slice_bitcast_fusion), channel_id=1, source_target_pairs={{0,4},{4,8},{8,12},{12,16},{16,20},{20,24},{24,28},{1,5},{5,9},{9,... | collective-permute-start | bytes 1572872 | tf_op jit(solution)/shard_map/ppermute | solution.py:451
  129.5 1.0 copy-start.2

commit v2 on v1

--- a/solution.py
+++ b/solution.py
@@ -9,6 +9,7 @@
 from jax.experimental.pallas import tpu as pltpu
 from jax.sharding import PartitionSpec as P
 
+
 SWEEPS = 6
 EARLY = 3
 
@@ -19,8 +20,10 @@
 reaction_shift = 0.1
 relaxation = 0.9
 
+CHUNK = 16
+LANES = 128
 PAD = 8
-VMEM_LIMIT = 60 * 1024 * 1024
+MIB = 1024 * 1024
 
 
 def ring(axis, step):
@@ -32,8 +35,15 @@
     return lax.ppermute(block, "space", ring("space", step))
 
 
-def tile_of(low, high):
-    return jnp.concatenate([low, high], axis=0).T
+def tile_of(low, high, mix):
+    second, third = low.shape
+    parts = []
+    for part in range(third // LANES):
+        here = slice(part * LANES, (part + 1) * LANES)
+        mix[part, pl.ds(0, second, stride=2), :] = low[:, here]
+        mix[part, pl.ds(1, second, stride=2), :] = high[:, here]
+        parts.append(mix[part].T)
+    return jnp.concatenate(parts, axis=0)
 
 
 def windows(tile, count):
@@ -43,44 +53,50 @@
     return [padded[b * size : b * size + size + 2 * PAD] for b in range(count)]
 
 
-def pack_own(position, state, initial, out, first, stage):
-    count, steps, pairs, rows, lanes = out.shape
+def pack_inner(start, state, out, mix):
+    count, steps, pairs, _, _ = out.shape
+    width = state.shape[1]
+    for pair in range(pairs):
+        for step in range(steps):
+            low, high = state[step, start + pair], state[step, width - 1 - start - pair]
+            for b, window in enumerate(windows(tile_of(low, high, mix.at[step % 2]), count)):
+                out[b, step, pair] = window
+
+
+def pack_outer(position, state, initial, out, first, stage, mix):
+    count, rows = out.shape[0], out.shape[3]
     width = state.shape[1]
     third = state.shape[3]
     size = third // count
-    for pair in range(pairs):
-        tile = tile_of(initial[pair], initial[width - 1 - pair])
+    pack_inner(0, state, out, mix)
+    for pair in range(first.shape[0]):
+        tile = tile_of(initial[pair], initial[width - 1 - pair], mix.at[0])
         stage[:PAD] = tile[third - PAD :]
         stage[PAD : PAD + third] = tile
         stage[PAD + third :] = tile[:PAD]
         first[pair] = stage[pl.ds(pl.multiple_of(position[0] * size, 8), rows), :]
-        for step in range(steps):
-            tile = tile_of(state[step, pair], state[step, width - 1 - pair])
-            for b, window in enumerate(windows(tile, count)):
-                out[b, step, pair] = window
-
-
-def pack_early(lower, upper, out):
-    count, steps, depth, rows, lanes = out.shape
+
+
+def pack_early(lower, upper, out, mix):
+    count, steps, depth, _, _ = out.shape
     for step in range(steps):
         for j in range(depth):
-            tile = tile_of(lower[step, j], upper[step, depth - 1 - j])
+            tile = tile_of(lower[step, j], upper[step, depth - 1 - j], mix.at[j % 2])
             for b, window in enumerate(windows(tile, count)):
                 out[b, step, j] = window
 
 
+def low_mask(tile):
+    return lax.broadcasted_iota(jnp.int32, tile.shape, tile.ndim - 1) % 2 == 0
+
+
 def swap(tile):
-    return pltpu.roll(tile, tile.shape[-1] // 2, tile.ndim - 1)
-
-
-def low_mask(tile):
-    lanes = tile.shape[-1]
-    return lax.broadcasted_iota(jnp.int32, tile.shape, tile.ndim - 1) < lanes // 2
-
-
-def pack_late(skip, own, up, down):
-    half, late, rows, lanes = up.shape
-    pairs = own.shape[1]
+    lanes, axis = tile.shape[-1], tile.ndim - 1
+    return jnp.where(low_mask(tile), pltpu.roll(tile, lanes - 1, axis), pltpu.roll(tile, 1, axis))
+
+
+def pack_late(skip, pairs, start, own, up, down):
+    half, late, rows, _ = up.shape
     width = 2 * pairs
     depth = SWEEPS
 
@@ -89,8 +105,8 @@
             a = depth - j
             for out, layer in ((up, width - a), (down, a - 1)):
                 pair, in_low = (layer, True) if layer < pairs else (width - 1 - layer, False)
-                early = own[t, pair, skip : skip + rows]
-                later = own[t + half, pair, skip : skip + rows]
+                early = own[t, pair - start, skip : skip + rows]
+                later = own[t + half, pair - start, skip : skip + rows]
                 if in_low:
                     out[t, j] = jnp.where(low_mask(early), early, swap(later))
                 else:
@@ -177,26 +193,20 @@
 
 
 def second_sum(tile):
-    lanes = tile.shape[-1]
-    axis = tile.ndim - 1
-    place = lax.broadcasted_iota(jnp.int32, tile.shape, axis) % (lanes // 2)
-    before = jnp.where(
-        place == 0, pltpu.roll(tile, lanes // 2 + 1, axis), pltpu.roll(tile, 1, axis)
-    )
-    after = jnp.where(
-        place == lanes // 2 - 1,
-        pltpu.roll(tile, lanes // 2 - 1, axis),
-        pltpu.roll(tile, lanes - 1, axis),
-    )
-    return before + after
-
-
-def solve(skip, table, up, down, first, first_low, first_high, own, early, out, state, base, ping, pong, sems):
-    horizon, pairs = own.shape[:2]
+    lanes, axis = tile.shape[-1], tile.ndim - 1
+    return pltpu.roll(tile, 2, axis) + pltpu.roll(tile, lanes - 2, axis)
+
+
+def solve(
+    skip, table, up, down, first, first_low, first_high, outer, inner, early, out, state, base, ping, pong, sems
+):
+    horizon = inner.shape[0]
+    pairs = first.shape[0]
+    start = outer.shape[1]
     taken = early.shape[1]
     depth = SWEEPS
     late = depth - taken
-    rows = own.shape[2]
+    rows = inner.shape[2]
     post_rows = up.shape[2]
     block = rows - 2 * PAD
     last = depth + pairs - 1
@@ -204,7 +214,12 @@
     at = PAD
     copies = [
         pltpu.make_async_copy(
-            own, state.at[pl.ds(1, horizon), pl.ds(depth, pairs), pl.ds(at, rows)], sems.at[0]
+            outer, state.at[pl.ds(1, horizon), pl.ds(depth, start), pl.ds(at, rows)], sems.at[0]
+        ),
+        pltpu.make_async_copy(
+            inner,
+            state.at[pl.ds(1, horizon), pl.ds(depth + start, pairs - start), pl.ds(at, rows)],
+            sems.at[2],
         ),
         pltpu.make_async_copy(
             early, state.at[pl.ds(1, horizon), pl.ds(late, taken), pl.ds(at, rows)], sems.at[1]
@@ -244,19 +259,20 @@
     lax.fori_loop(0, horizon + 1, mirror, 0)
 
     def weigh(t, carry):
+        centre = time_step - 1.0 - 2.0 * couple_first - 4.0 * couple_cross
         for x in range(1, last + 1):
-            s = state[t + 1, x, at : at + rows]
-            along = state[t + 1, x - 1, at : at + rows] + state[t + 1, x + 1, at : at + rows]
-            across = (
-                state[t + 1, x, at - 1 : at + rows - 1]
-                + state[t + 1, x, at + 1 : at + rows + 1]
-                + second_sum(s)
-            )
-            centre = time_step - 1.0 - 2.0 * couple_first - 4.0 * couple_cross
-            ping[t, x, at : at + rows] = (
-                (state[t, x, at : at + rows] + couple_first * along)
-                + (couple_cross * across + s * (centre - time_step * (s * s)))
-            )
+            for r in range(at, at + rows, CHUNK):
+                s = state[t + 1, x, r : r + CHUNK]
+                along = state[t + 1, x - 1, r : r + CHUNK] + state[t + 1, x + 1, r : r + CHUNK]
+                across = (
+                    state[t + 1, x, r - 1 : r + CHUNK - 1]
+                    + state[t + 1, x, r + 1 : r + CHUNK + 1]
+                    + second_sum(s)
+                )
+                ping[t, x, r : r + CHUNK] = (
+                    (state[t, x, r : r + CHUNK] + couple_first * along)
+                    + (couple_cross * across + s * (centre - time_step * (s * s)))
+                )
         return carry
 
     lax.fori_loop(0, horizon, weigh, 0)
@@ -289,32 +305,38 @@
     lax.fori_loop(0, horizon, mirror_base, 0)
 
     def sweep(number, source, target):
+        reach = SWEEPS - 1 - number
+        begin = at + PAD - 8 * (-(-reach // 8))
+        chunks = (block + 2 * (at + PAD - begin)) // CHUNK
+
         def pair(k, carry):
             a, b, c, d = [table[k, i] for i in range(4)]
             for x in range(number + 1, last + 1):
-                near = []
-                for m in (k, half + k):
-                    v = source[m, x, at : at + rows]
-                    along = source[m, x - 1, at : at + rows] + source[m, x + 1, at : at + rows]
-                    across = (
-                        source[m, x, at - 1 : at + rows - 1]
-                        + source[m, x, at + 1 : at + rows + 1]
-                        + second_sum(v)
-                    )
-                    near.append(
-                        (
-                            base[m, x, at : at + rows] + (1.0 - relaxation) * v,
-                            (couple_first / couple_cross) * along + across,
+                for chunk in range(chunks):
+                    r = begin + chunk * CHUNK
+                    near = []
+                    for m in (k, half + k):
+                        v = source[m, x, r : r + CHUNK]
+                        along = source[m, x - 1, r : r + CHUNK] + source[m, x + 1, r : r + CHUNK]
+                        across = (
+                            source[m, x, r - 1 : r + CHUNK - 1]
+                            + source[m, x, r + 1 : r + CHUNK + 1]
+                            + second_sum(v)
                         )
-                    )
-                (rest_real, near_real), (rest_imag, near_imag) = near
-                real = rest_real + (a * near_real + b * near_imag)
-                imag = rest_imag + (c * near_real + d * near_imag)
-                target[k, x, at : at + rows] = real
-                target[half + k, x, at : at + rows] = imag
-                if x == last:
-                    target[k, last + 1, at : at + rows] = swap(real)
-                    target[half + k, last + 1, at : at + rows] = swap(imag)
+                        near.append(
+                            (
+                                base[m, x, r : r + CHUNK] + (1.0 - relaxation) * v,
+                                (couple_first / couple_cross) * along + across,
+                            )
+                        )
+                    (rest_real, near_real), (rest_imag, near_imag) = near
+                    real = rest_real + (a * near_real + b * near_imag)
+                    imag = rest_imag + (c * near_real + d * near_imag)
+                    target[k, x, r : r + CHUNK] = real
+                    target[half + k, x, r : r + CHUNK] = imag
+                    if x == last:
+                        target[k, last + 1, r : r + CHUNK] = swap(real)
+                        target[half + k, last + 1, r : r + CHUNK] = swap(imag)
             return carry
 
         lax.fori_loop(0, half, pair, 0)
@@ -343,15 +365,21 @@
     lax.fori_loop(0, pairs * kept, restore, 0)
 
 
-def finish(state, pieces, updated):
-    count, steps, pairs, size, lanes = pieces.shape
+def finish(state, pieces, updated, mix):
+    count, steps, pairs, _, lanes = pieces.shape
     width = 2 * pairs
     second = lanes // 2
     for step in range(steps):
         for pair in range(pairs):
             tile = jnp.concatenate([pieces[b, step, pair] for b in range(count)], axis=0).T
-            updated[step, pair] = state[step, pair] + tile[:second]
-            updated[step, width - 1 - pair] = state[step, width - 1 - pair] + tile[second:]
+            mirror = width - 1 - pair
+            for part in range(tile.shape[1] // LANES):
+                here = slice(part * LANES, (part + 1) * LANES)
+                piece = mix.at[pair % 2, part]
+                piece[...] = tile[:, here]
+                low, high = piece[pl.ds(0, second, stride=2), :], piece[pl.ds(1, second, stride=2), :]
+                updated[step, pair, :, here] = state[step, pair, :, here] + low
+                updated[step, mirror, :, here] = state[step, mirror, :, here] + high
 
 
 def residual_of(state, carried, low, high, out):
@@ -383,15 +411,20 @@
     return jax.ShapeDtypeStruct(dims, jnp.float32)
 
 
-def params():
-    return pltpu.CompilerParams(vmem_limit_bytes=VMEM_LIMIT)
+def params(*arrays):
+    held = sum(4 * math.prod(getattr(a, "shape", a)) for a in arrays)
+    return pltpu.CompilerParams(vmem_limit_bytes=held + 2 * MIB)
 
 
 def cost(flops, bytes_accessed):
     return pl.CostEstimate(flops=int(flops), bytes_accessed=int(bytes_accessed), transcendentals=0)
 
 
-def body(state, initial):
+def exchange(block):
+    return lax.all_to_all(block, "tm", split_axis=0, concat_axis=0, tiled=True)
+
+
+def iteration(state, initial):
     steps, width, second, third = state.shape
     count = lax.axis_size("tm")
     horizon = steps * count
@@ -399,54 +432,66 @@
     depth, taken = SWEEPS, EARLY
     late = depth - taken
     pairs = width // 2
+    start = min(taken, width - depth)
     size = third // count
     rows = size + 2 * PAD
     lanes = 2 * second
     skip = 4
     post_rows = rows - 2 * skip
+    mixer = pltpu.VMEM((2, third // LANES, lanes, LANES), jnp.float32)
 
     lower = hop(state[:, width - taken :], 1)
     upper = hop(state[:, :taken], -1)
 
-    sent, first = pl.pallas_call(
-        pack_own,
-        out_shape=(shape_of(count, steps, pairs, rows, lanes), shape_of(pairs, rows, lanes)),
+    sent_inner = pl.pallas_call(
+        functools.partial(pack_inner, start),
+        out_shape=shape_of(count, steps, pairs - start, rows, lanes),
+        in_specs=vmem(1),
+        out_specs=pl.BlockSpec(memory_space=pltpu.VMEM),
+        scratch_shapes=[mixer],
+        compiler_params=params(state, state, state),
+        cost_estimate=cost(4e6, 3e6),
+        name="pack_inner",
+    )(state)
+    inner = exchange(sent_inner).reshape(horizon, pairs - start, rows, lanes)
+
+    sent_outer, first = pl.pallas_call(
+        pack_outer,
+        out_shape=(shape_of(count, steps, start, rows, lanes), shape_of(pairs, rows, lanes)),
         in_specs=[pl.BlockSpec(memory_space=pltpu.SMEM)] + vmem(2),
         out_specs=vmem(2),
-        scratch_shapes=[pltpu.VMEM((third + 2 * PAD, lanes), jnp.float32)],
-        compiler_params=params(),
+        scratch_shapes=[pltpu.VMEM((third + 2 * PAD, lanes), jnp.float32), mixer],
+        compiler_params=params(state, state, initial, state),
         cost_estimate=cost(4e6, 3e6),
-        name="pack_own",
+        name="pack_outer",
     )(position.reshape(1), state, initial)
+    outer = exchange(sent_outer).reshape(horizon, start, rows, lanes)
     first_low = hop(first, 1)
     first_high = hop(first, -1)
-    own = lax.all_to_all(sent, "tm", split_axis=0, concat_axis=0, tiled=True)
-    own = own.reshape(horizon, pairs, rows, lanes)
+
+    up, down = pl.pallas_call(
+        functools.partial(pack_late, skip, pairs, start),
+        out_shape=(shape_of(horizon // 2, late, post_rows, lanes),) * 2,
+        in_specs=vmem(1),
+        out_specs=vmem(2),
+        compiler_params=params(inner, inner),
+        cost_estimate=cost(2e6, 2e6),
+        name="pack_late",
+    )(inner)
+    late_low = hop(up, 1)
+    late_high = hop(down, -1)
 
     sent_early = pl.pallas_call(
         pack_early,
         out_shape=shape_of(count, steps, taken, rows, lanes),
         in_specs=vmem(2),
         out_specs=pl.BlockSpec(memory_space=pltpu.VMEM),
-        compiler_params=params(),
+        scratch_shapes=[mixer],
+        compiler_params=params(lower, upper, sent_inner, sent_outer),
         cost_estimate=cost(4e6, 3e6),
         name="pack_early",
     )(lower, upper)
-
-    up, down = pl.pallas_call(
-        functools.partial(pack_late, skip),
-        out_shape=(shape_of(horizon // 2, late, post_rows, lanes),) * 2,
-        in_specs=vmem(1),
-        out_specs=vmem(2),
-        compiler_params=params(),
-        cost_estimate=cost(2e6, 2e6),
-        name="pack_late",
-    )(own)
-    late_low = hop(up, 1)
-    late_high = hop(down, -1)
-
-    early = lax.all_to_all(sent_early, "tm", split_axis=0, concat_axis=0, tiled=True)
-    early = early.reshape(horizon, taken, rows, lanes)
+    early = exchange(sent_early).reshape(horizon, taken, rows, lanes)
 
     carried = lax.ppermute(state[steps - 1], "tm", [(i, i + 1) for i in range(count - 1)])
     carried = jnp.where(position == 0, initial, carried)
@@ -455,7 +500,7 @@
         out_shape=shape_of(*state.shape),
         in_specs=vmem(4),
         out_specs=pl.BlockSpec(memory_space=pltpu.VMEM),
-        compiler_params=params(),
+        compiler_params=params(state, state, carried, lower),
         cost_estimate=cost(6e6, 3e6),
         name="residual",
     )(state, carried, lower[:, taken - 1], upper[:, 0])
@@ -466,28 +511,39 @@
     moved = pl.pallas_call(
         functools.partial(solve, skip),
         out_shape=shape_of(horizon, pairs, size, lanes),
-        in_specs=[pl.BlockSpec(memory_space=pltpu.SMEM)] + vmem(5) + [any_space] * 2,
+        in_specs=[pl.BlockSpec(memory_space=pltpu.SMEM)] + vmem(5) + [any_space] * 3,
         out_specs=pl.BlockSpec(memory_space=pltpu.VMEM),
         scratch_shapes=[
             pltpu.VMEM((horizon + 1, layers, scratch_rows, lanes), jnp.float32),
             pltpu.VMEM((horizon, layers, scratch_rows, lanes), jnp.float32),
             pltpu.VMEM((horizon, layers, scratch_rows, lanes), jnp.float32),
             pltpu.VMEM((horizon, layers, scratch_rows, lanes), jnp.float32),
-            pltpu.SemaphoreType.DMA((2,)),
+            pltpu.SemaphoreType.DMA((3,)),
         ],
-        compiler_params=params(),
+        compiler_params=params((4 * MIB,), *[(horizon + 1, layers, scratch_rows, lanes)] * 4),
         cost_estimate=cost(1e8, 8e6),
         name="solve",
-    )(jnp.asarray(sweep_table(horizon)), late_low, late_high, first, first_low, first_high, own, early)
+    )(
+        jnp.asarray(sweep_table(horizon)),
+        late_low,
+        late_high,
+        first,
+        first_low,
+        first_high,
+        outer,
+        inner,
+        early,
+    )
 
     moved = moved.reshape(count, steps, pairs, size, lanes)
-    pieces = lax.all_to_all(moved, "tm", split_axis=0, concat_axis=0, tiled=True)
+    pieces = exchange(moved)
     updated = pl.pallas_call(
         finish,
         out_shape=shape_of(*state.shape),
         in_specs=vmem(2),
         out_specs=pl.BlockSpec(memory_space=pltpu.VMEM),
-        compiler_params=params(),
+        scratch_shapes=[mixer],
+        compiler_params=params(state, state, state),
         cost_estimate=cost(2e6, 3e6),
         name="finish",
     )(state, pieces)
@@ -497,4 +553,4 @@
 def solution(mesh):
     in_specs = (P("tm", "space", None, None), P("space", None, None))
     out_specs = (P("tm", "space", None, None), P("tm", "space", None, None))
-    return jax.shard_map(body, mesh=mesh, in_specs=in_specs, out_specs=out_specs, check_vma=False)
+    return jax.shard_map(iteration, mesh=mesh, in_specs=in_specs, out_specs=out_specs, check_vma=False)

time: 134 us -> 140 us (1.045)
  Pallas kernels: 46 us -> 27.2 us
  local copies, waits for them, and re-layouts: 5.75 us -> 16.7 us
  waiting for transfers between devices: 52.9 us -> 62.1 us
  starting transfers between devices: 27 us -> 31.4 us
    pallas_call x6 -> x7, Pallas kernels: 46 us -> 27.2 us  [the longest x1 20.5 us: iteration(): pl.pallas_call(functools.partial(solve, skip), out_shape=shape_of(horizon...]
    unnamed x20 -> x42, local copies, waits for them, and re-layouts: 1.99 us -> 14.8 us
    all_to_all x3 -> x4, waiting for transfers between devices: 0.01 us -> 9.2 us  [exchange(): return lax.all_to_all(block, 'tm', split_axis=0, concat_axis=0, tiled=True)]
    all_to_all x3 -> x4, starting transfers between devices: 13.4 us -> 17.7 us  [exchange(): return lax.all_to_all(block, 'tm', split_axis=0, concat_axis=0, tiled=True)]
    ppermute x2, local copies, waits for them, and re-layouts: 1.55 us -> 0.05 us  [hop(): return lax.ppermute(block, 'space', ring('space', step))]
  transfers between devices with their start and end apart: 10 -> 11, of which waited for: 5 -> 5; matrix products, arithmetic and copies ran while one was open for 4% -> 2% of each run, Pallas kernels for 7% -> 3%
where the time goes in v2:
time: 140 us; the launch traced here: 139 us
  waiting for transfers between devices  62.1 us (44%)
  starting transfers between devices  31.4 us (22%)
  Pallas kernels  27.2 us (19%)
  local copies, waits for them, and re-layouts  16.7 us (12%)
    ppermute x6, waiting for transfers between devices, hop(): return lax.ppermute(block, 'space', ring('space', step))  37.2 us
    pallas_call x1, Pallas kernels, iteration(): pl.pallas_call(functools.partial(solve, skip), out_shape=shape_of(horizon...  20.5 us
    all_to_all x4, starting transfers between devices, exchange(): return lax.all_to_all(block, 'tm', split_axis=0, concat_axis=0, tiled=True)  17.7 us
    ppermute x1, waiting for transfers between devices, iteration(): lax.ppermute(state[steps - 1], 'tm', [(i, i + 1) for i in range(count - 1)])  15.7 us
    unnamed x42, local copies, waits for them, and re-layouts  14.8 us
    ppermute x6, starting transfers between devices, hop(): return lax.ppermute(block, 'space', ring('space', step))  11.6 us
    all_to_all x4, waiting for transfers between devices, exchange(): return lax.all_to_all(block, 'tm', split_axis=0, concat_axis=0, tiled=True)  9.2 us
  transfers between devices with their start and end apart: 11, of which 5 were waited for; matrix products, arithmetic and copies ran while one was open for 2% of the time, Pallas kernels for 3%

profile of v2, /device:TPU:4, one launch (start us, length us, event | category | flops | bytes accessed | tf_op | source)
XLA Modules:
  0.0 139.3 jit_solution(4892010484063225924)
XLA Ops:
  0.6 0.0 copy-start
  0.6 1.2 copy-done
  1.9 1.1 pack_inner.1
  3.0 4.4 %all-to-all-start = ((f32[8,2,2,48,128]{4,3,2,1,0:T(8,128)}), f32[8,2,2,48,128]{4,3,2,1,0:T(8,128)S(1)}, u32[]{:S(2)}, u32[]{:S(2)}) async-start(f32[8,2,2,48,128]{4,3,2,1,0:T(8,128)} %pack_inner.1), calls=%async_computation | async-start | bytes 1572864 | tf_op jit(solution)/shard_map/all_to_all | solution.py:424
  7.3 0.4 pack_outer.1
  7.7 0.0 copy-start.6
  7.7 0.9 copy-done.6
  8.6 0.6 copy-done.11
  9.2 9.2 %all-to-all-done = f32[8,2,2,48,128]{4,3,2,1,0:T(8,128)S(1)} async-done(((f32[8,2,2,48,128]{4,3,2,1,0:T(8,128)}), f32[8,2,2,48,128]{4,3,2,1,0:T(8,128)S(1)}, u32[]{:S(2)}, u32[]{:S(2)}) %all-to-all-start) | async-done | bytes 786464 | tf_op jit(solution)/shard_map/all_to_all | solution.py:424
  18.4 4.9 %all-to-all-start.1 = ((f32[8,2,2,48,128]{4,3,2,1,0:T(8,128)}), f32[8,2,2,48,128]{4,3,2,1,0:T(8,128)S(1)}, u32[]{:S(2)}, u32[]{:S(2)}) async-start(f32[8,2,2,48,128]{4,3,2,1,0:T(8,128)} %copy-done.6), calls=%async_computation.1 | async-start | bytes 1572864 | tf_op jit(solution)/shard_map/all_to_all | solution.py:424
  23.4 0.1 fusion
  23.5 1.6 %collective-permute-start.4 = (f32[2,3,64,256]{3,2,0,1:T(8,128)S(1)}, f32[2,3,64,256]{3,2,0,1:T(8,128)S(1)}, u32[]{:S(2)}, u32[]{:S(2)}) collective-permute-start(f32[2,3,64,256]{3,2,0,1:T(8,128)S(1)} %copy.9), channel_id=1, source_target_pairs={{0,1},{1,2},{2,3},{3,0},{4,5},{5,6},{6,7},{7,4},{8,9},{9,10},{10,1... | collective-permute-start | bytes 1179656 | tf_op jit(solution)/shard_map/ppermute | solution.py:35
  25.1 2.3 %collective-permute-start.5 = (f32[2,3,64,256]{3,2,0,1:T(8,128)S(1)}, f32[2,3,64,256]{3,2,0,1:T(8,128)S(1)}, u32[]{:S(2)}, u32[]{:S(2)}) collective-permute-start(f32[2,3,64,256]{3,2,0,1:T(8,128)S(1)} %copy.10), channel_id=1, source_target_pairs={{0,3},{1,0},{2,1},{3,2},{4,7},{5,4},{6,5},{7,6},{8,11},{9,8},{10,9... | collective-permute-start | bytes 1179656 | tf_op jit(solution)/shard_map/ppermute | solution.py:35
  27.4 9.9 %collective-permute-done.4 = f32[2,3,64,256]{3,2,0,1:T(8,128)S(1)} collective-permute-done((f32[2,3,64,256]{3,2,0,1:T(8,128)S(1)}, f32[2,3,64,256]{3,2,0,1:T(8,128)S(1)}, u32[]{:S(2)}, u32[]{:S(2)}) %collective-permute-start.4) | collective-permute-done | bytes 393248 | tf_op jit(solution)/shard_map/ppermute | solution.py:35
  37.4 0.7 copy-done.18
  38.1 6.4 %collective-permute-done.5 = f32[2,3,64,256]{3,2,0,1:T(8,128)S(1)} collective-permute-done((f32[2,3,64,256]{3,2,0,1:T(8,128)S(1)}, f32[2,3,64,256]{3,2,0,1:T(8,128)S(1)}, u32[]{:S(2)}, u32[]{:S(2)}) %collective-permute-start.5) | collective-permute-done | bytes 393248 | tf_op jit(solution)/shard_map/ppermute | solution.py:35
  44.5 0.7 copy-done.19
  45.2 1.4 pack_early.1
  46.6 0.0 all-to-all-done.1
  46.6 0.9 copy-done.3
  47.5 4.2 %all-to-all-start.2 = ((f32[8,2,3,48,128]{4,3,2,1,0:T(8,128)}), f32[8,2,3,48,128]{4,3,2,1,0:T(8,128)S(1)}, u32[]{:S(2)}, u32[]{:S(2)}) async-start(f32[8,2,3,48,128]{4,3,2,1,0:T(8,128)} %pack_early.1), calls=%async_computation.2 | async-start | bytes 2359296 | tf_op jit(solution)/shard_map/all_to_all | solution.py:424
  51.7 0.8 pack_late.1
  52.5 1.1 collective-permute-start
  53.6 2.8 %collective-permute-start.1 = (f32[8,3,40,128]{3,2,1,0:T(8,128)S(1)}, f32[8,3,40,128]{3,2,1,0:T(8,128)S(1)}, u32[]{:S(2)}, u32[]{:S(2)}) collective-permute-start(f32[8,3,40,128]{3,2,1,0:T(8,128)S(1)} %get-tuple-element.7), channel_id=1, source_target_pairs={{0,3},{1,0},{2,1},{3,2},{4,7},{5,4},{6,5},{7,6},{8,11},{9,8},{10,9... | collective-permute-start | bytes 1474568 | tf_op jit(solution)/shard_map/ppermute | solution.py:35
  56.3 0.0 collective-permute-start.2
  56.3 3.8 %collective-permute-start.3 = (f32[4,48,128]{2,1,0:T(8,128)}, f32[4,48,128]{2,1,0:T(8,128)S(1)}, u32[]{:S(2)}, u32[]{:S(2)}) collective-permute-start(f32[4,48,128]{2,1,0:T(8,128)} %copy-done.11), channel_id=1, source_target_pairs={{0,3},{1,0},{2,1},{3,2},{4,7},{5,4},{6,5},{7,6},{8,11},{9,8},{10,9... | collective-permute-start | bytes 294920 | tf_op jit(solution)/shard_map/ppermute | solution.py:35
  60.2 20.9 %collective-permute-done.2.first_low = f32[4,48,128]{2,1,0:T(8,128)S(1)} collective-permute-done((f32[4,48,128]{2,1,0:T(8,128)}, f32[4,48,128]{2,1,0:T(8,128)S(1)}, u32[]{:S(2)}, u32[]{:S(2)}) %collective-permute-start.2) | collective-permute-done | bytes 98336 | tf_op jit(solution)/shard_map/ppermute | solution.py:35
  81.1 0.6 copy-done.13
  81.7 0.6 copy-done.15
  82.4 0.8 copy-done.7
  83.2 0.8 copy-done.9
  83.9 1.1 copy-done.4
  85.1 1.0 copy-done.8
  86.1 1.0 copy-done.10
  87.1 0.9 copy-done.12
  88.0 0.9 copy-done.14
  88.9 0.9 copy-done.16
  89.8 20.5 %solve.1 = f32[16,4,32,128]{3,2,1,0:T(8,128)S(1)} custom-call(f32[8,4]{1,0:T(8,128)S(1)} %copy-done.17, f32[8,3,40,128]{3,2,1,0:T(8,128)S(1)} %copy-done.8, f32[8,3,40,128]{3,2,1,0:T(8,128)S(1)} %copy-done.10, f32[4,48,128]{2,1,0:T(8,128)S(1)} %copy-done.12, f32[4,48,128]{2,1,0:T(8,128)S(1)} %copy-done.14, f32[4,48,128]{2,1,0:T(8,128)S(1)} %copy-done.16, ...), custom_call_target="tpu_custom_call" | custom-call | flops 100000000 | bytes 8000000 | tf_op jit(solution)/shard_map/solve/pallas_call | solution.py:511
  110.3 0.0 copy-start.2
  110.3 1.0 copy-done.2
  111.3 4.2 %all-to-all-start.3 = ((f32[8,2,4,32,128]{4,3,2,1,0:T(8,128)}), f32[8,2,4,32,128]{4,3,2,1,0:T(8,128)S(1)}, u32[]{:S(2)}, u32[]{:S(2)}) async-start(f32[8,2,4,32,128]{4,3,2,1,0:T(8,128)} %bitcast.14), calls=%async_computation.3 | async-start | bytes 2097152 | tf_op jit(solution)/shard_map/all_to_all | solution.py:424
  115.5 2.0 %collective-permute-start.6 = (f32[8,64,256]{2,1,0:T(8,128)S(1)}, f32[8,64,256]{2,1,0:T(8,128)}, u32[]{:S(2)}, u32[]{:S(2)}) collective-permute-start(f32[8,64,256]{2,1,0:T(8,128)S(1)} %slice_bitcast_fusion), channel_id=1, source_target_pairs={{0,4},{4,8},{8,12},{12,16},{16,20},{20,24},{24,28},{1,5},{5,9},{9,... | collective-permute-start | bytes 1572872 | tf_op jit(solution)/shard_map/ppermute | solution.py:496
  117.6 0.9 slice_bitcast_fusion.1.high
  118.5 0.9 slice_bitcast_fusion.2.low
  119.4 15.7 %collective-permute-done.6 = f32[8,64,256]{2,1,0:T(8,128)} collective-permute-done((f32[8,64,256]{2,1,0:T(8,128)S(1)}, f32[8,64,256]{2,1,0:T(8,128)}, u32[]{:S(2)}, u32[]{:S(2)}) %collective-permute-start.6) | collective-permute-done | bytes 524320 | tf_op jit(solution)/shard_map/ppermute | solution.py:496
  135.1 1.1 broadcast_select_fusion.carried
  136.2 1.7 %residual.1 = f32[2,8,64,256]{3,2,1,0:T(8,128)} custom-call(f32[2,8,64,256]{3,2,1,0:T(8,128)S(1)} %copy-done.1, f32[8,64,256]{2,1,0:T(8,128)S(1)} %broadcast_select_fusion.carried, f32[2,64,256]{2,1,0:T(8,128)S(1)} %slice_bitcast_fusion.2.low, f32[2,64,256]{2,1,0:T(8,128)S(1)} %slice_bitcast_fusion.1.high), custom_call_target="tpu_custom_call" | custom-call | flops 6000000 | bytes 3000000 | tf_op jit(solution)/shard_map/residual/pallas_call | solution.py:498
  137.9 1.4 %finish.1 = f32[2,8,64,256]{3,2,1,0:T(8,128)} custom-call(f32[2,8,64,256]{3,2,1,0:T(8,128)S(1)} %copy-done.1, f32[8,2,4,32,128]{4,3,2,1,0:T(8,128)S(1)} %all-to-all-done.3.pieces), custom_call_target="tpu_custom_call" | custom-call | flops 2000000 | bytes 3000000 | tf_op jit(solution)/shard_map/finish/pallas_call | solution.py:540
  (30 shorter events, 0.2 us)
Async XLA Ops:
  0.6 1.2 copy-start
  3.0 4.4 %copy-start.1 = (f32[2,8,64,256]{3,2,1,0:T(8,128)S(1)}, f32[2,8,64,256]{3,2,1,0:T(8,128)}, u32[]{:S(2)}) copy-start(f32[2,8,64,256]{3,2,1,0:T(8,128)} %state.7) | copy-start | bytes 3145732
  3.0 4.4 %copy-start.5 = (f32[8,64,256]{2,1,0:T(8,128)S(1)}, f32[8,64,256]{2,1,0:T(8,128)}, u32[]{:S(2)}) copy-start(f32[8,64,256]{2,1,0:T(8,128)} %initial.1) | copy-start | bytes 1572868
  3.0 15.5 %all-to-all-start = ((f32[8,2,2,48,128]{4,3,2,1,0:T(8,128)}), f32[8,2,2,48,128]{4,3,2,1,0:T(8,128)S(1)}, u32[]{:S(2)}, u32[]{:S(2)}) async-start(f32[8,2,2,48,128]{4,3,2,1,0:T(8,128)} %pack_inner.1), calls=%async_computation | async-start | bytes 1572864 | tf_op jit(solution)/shard_map/all_to_all | solution.py:424
  7.7 0.9 copy-start.6
  8.6 0.6 copy-start.11
  18.4 28.2 %all-to-all-start.1 = ((f32[8,2,2,48,128]{4,3,2,1,0:T(8,128)}), f32[8,2,2,48,128]{4,3,2,1,0:T(8,128)S(1)}, u32[]{:S(2)}, u32[]{:S(2)}) async-start(f32[8,2,2,48,128]{4,3,2,1,0:T(8,128)} %copy-done.6), calls=%async_computation.1 | async-start | bytes 1572864 | tf_op jit(solution)/shard_map/all_to_all | solution.py:424
  23.5 13.9 %collective-permute-start.4 = (f32[2,3,64,256]{3,2,0,1:T(8,128)S(1)}, f32[2,3,64,256]{3,2,0,1:T(8,128)S(1)}, u32[]{:S(2)}, u32[]{:S(2)}) collective-permute-start(f32[2,3,64,256]{3,2,0,1:T(8,128)S(1)} %copy.9), channel_id=1, source_target_pairs={{0,1},{1,2},{2,3},{3,0},{4,5},{5,6},{6,7},{7,4},{8,9},{9,10},{10,1... | collective-permute-start | bytes 1179656 | tf_op jit(solution)/shard_map/ppermute | solution.py:35
  25.1 19.3 %collective-permute-start.5 = (f32[2,3,64,256]{3,2,0,1:T(8,128)S(1)}, f32[2,3,64,256]{3,2,0,1:T(8,128)S(1)}, u32[]{:S(2)}, u32[]{:S(2)}) collective-permute-start(f32[2,3,64,256]{3,2,0,1:T(8,128)S(1)} %copy.10), channel_id=1, source_target_pairs={{0,3},{1,0},{2,1},{3,2},{4,7},{5,4},{6,5},{7,6},{8,11},{9,8},{10,9... | collective-permute-start | bytes 1179656 | tf_op jit(solution)/shard_map/ppermute | solution.py:35
  37.3 0.8 copy-start.18
  44.5 0.8 copy-start.19
  46.6 37.4 %copy-start.17 = (f32[8,4]{1,0:T(8,128)S(1)}, f32[8,4]{1,0:T(8,128)}, u32[]{:S(2)}) copy-start(f32[8,4]{1,0:T(8,128)} %constant.10.clone.table) | copy-start | bytes 388
  46.6 0.9 copy-start.3
  47.5 36.5 %all-to-all-start.2 = ((f32[8,2,3,48,128]{4,3,2,1,0:T(8,128)}), f32[8,2,3,48,128]{4,3,2,1,0:T(8,128)S(1)}, u32[]{:S(2)}, u32[]{:S(2)}) async-start(f32[8,2,3,48,128]{4,3,2,1,0:T(8,128)} %pack_early.1), calls=%async_computation.2 | async-start | bytes 2359296 | tf_op jit(solution)/shard_map/all_to_all | solution.py:424
  52.5 29.9 %collective-permute-start = (f32[8,3,40,128]{3,2,1,0:T(8,128)S(1)}, f32[8,3,40,128]{3,2,1,0:T(8,128)S(1)}, u32[]{:S(2)}, u32[]{:S(2)}) collective-permute-start(f32[8,3,40,128]{3,2,1,0:T(8,128)S(1)} %get-tuple-element.6), channel_id=1, source_target_pairs={{0,1},{1,2},{2,3},{3,0},{4,5},{5,6},{6,7},{7,4},{8,9},{9,10},{10,1... | collective-permute-start | bytes 1474568 | tf_op jit(solution)/shard_map/ppermute | solution.py:35
  53.6 29.6 %collective-permute-start.1 = (f32[8,3,40,128]{3,2,1,0:T(8,128)S(1)}, f32[8,3,40,128]{3,2,1,0:T(8,128)S(1)}, u32[]{:S(2)}, u32[]{:S(2)}) collective-permute-start(f32[8,3,40,128]{3,2,1,0:T(8,128)S(1)} %get-tuple-element.7), channel_id=1, source_target_pairs={{0,3},{1,0},{2,1},{3,2},{4,7},{5,4},{6,5},{7,6},{8,11},{9,8},{10,9... | collective-permute-start | bytes 1474568 | tf_op jit(solution)/shard_map/ppermute | solution.py:35
  56.3 24.8 %collective-permute-start.2 = (f32[4,48,128]{2,1,0:T(8,128)}, f32[4,48,128]{2,1,0:T(8,128)S(1)}, u32[]{:S(2)}, u32[]{:S(2)}) collective-permute-start(f32[4,48,128]{2,1,0:T(8,128)} %copy-done.11), channel_id=1, source_target_pairs={{0,1},{1,2},{2,3},{3,0},{4,5},{5,6},{6,7},{7,4},{8,9},{9,10},{10,1... | collective-permute-start | bytes 294920 | tf_op jit(solution)/shard_map/ppermute | solution.py:35
  56.3 25.4 %collective-permute-start.3 = (f32[4,48,128]{2,1,0:T(8,128)}, f32[4,48,128]{2,1,0:T(8,128)S(1)}, u32[]{:S(2)}, u32[]{:S(2)}) collective-permute-start(f32[4,48,128]{2,1,0:T(8,128)} %copy-done.11), channel_id=1, source_target_pairs={{0,3},{1,0},{2,1},{3,2},{4,7},{5,4},{6,5},{7,6},{8,11},{9,8},{10,9... | collective-permute-start | bytes 294920 | tf_op jit(solution)/shard_map/ppermute | solution.py:35
  81.1 0.6 copy-start.13
  81.7 0.6 copy-start.15
  82.4 0.8 copy-start.7
  83.2 0.8 copy-start.9
  83.9 1.1 copy-start.4
  85.1 1.0 copy-start.8
  86.1 1.0 copy-start.10
  87.1 0.9 copy-start.12
  88.0 0.9 copy-start.14
  88.9 0.9 copy-start.16
  110.3 1.0 copy-start.2
  111.3 26.6 %all-to-all-start.3 = ((f32[8,2,4,32,128]{4,3,2,1,0:T(8,128)}), f32[8,2,4,32,128]{4,3,2,1,0:T(8,128)S(1)}, u32[]{:S(2)}, u32[]{:S(2)}) async-start(f32[8,2,4,32,128]{4,3,2,1,0:T(8,128)} %bitcast.14), calls=%async_computation.3 | async-start | bytes 2097152 | tf_op jit(solution)/shard_map/all_to_all | solution.py:424
  115.5 19.6 %collective-permute-start.6 = (f32[8,64,256]{2,1,0:T(8,128)S(1)}, f32[8,64,256]{2,1,0:T(8,128)}, u32[]{:S(2)}, u32[]{:S(2)}) collective-permute-start(f32[8,64,256]{2,1,0:T(8,128)S(1)} %slice_bitcast_fusion), channel_id=1, source_target_pairs={{0,4},{4,8},{8,12},{12,16},{16,20},{20,24},{24,28},{1,5},{5,9},{9,... | collective-permute-start | bytes 1572872 | tf_op jit(solution)/shard_map/ppermute | solution.py:496

commit v3 on v0

v3 whole, which is shorter than its diff:
```python
import functools
import math

import jax
import jax.numpy as jnp
import numpy as np
from jax import lax
from jax.experimental import pallas as pl
from jax.experimental.pallas import tpu as pltpu
from jax.sharding import PartitionSpec as P


SWEEPS = 6
EARLY = 3

alpha_value = 0.1
time_step = 0.1
couple_first = 0.4
couple_cross = 0.05
reaction_shift = 0.1
relaxation = 0.9

CHUNK = 8
LANES = 128
PAD = 8
EDGE = 12
MIB = 1024 * 1024


def reach(depth):
    return SWEEPS - max(depth, 0)


def ring(axis, step):
    count = lax.axis_size(axis)
    return [(i, (i + step) % count) for i in range(count)]


def hop(block, step):
    return lax.ppermute(block, "space", ring("space", step))


def low_mask(tile):
    return lax.broadcasted_iota(jnp.int32, tile.shape, tile.ndim - 1) % 2 == 0


def first_mask(tile):
    return lax.broadcasted_iota(jnp.int32, tile.shape, tile.ndim - 1) // 2 % 2 == 0


def turn(tile, step):
    return pltpu.roll(tile, step % tile.shape[-1], tile.ndim - 1)


def merge(low, high, low_at=0, high_at=1):
    low = turn(low, -1) if low_at else low
    high = high if high_at else turn(high, 1)
    return jnp.where(low_mask(low), low, high)


def swap(tile):
    return jnp.where(low_mask(tile), turn(tile, -1), turn(tile, 1))


def stage_tile(mix, stage):
    third = mix.shape[0] * LANES
    for part in range(mix.shape[0]):
        stage[PAD + part * LANES : PAD + (part + 1) * LANES] = mix[part].T
    stage[:PAD] = stage[third : third + PAD]
    stage[third + PAD :] = stage[PAD : 2 * PAD]


def layer_half(layer, width):
    return (layer, True) if 2 * layer < width else (width - 1 - layer, False)


def copy_in(sems, pairs):
    copies = [pltpu.make_async_copy(a, b, sems.at[i]) for i, (a, b) in enumerate(pairs)]
    for copy in copies:
        copy.start()
    return copies


def pack_own(
    position, state_hbm, initial_hbm, out_hbm, first_hbm, up, down, state, initial, out, first, stage, mix, sems, out_sems
):
    count, steps = out.shape[:2]
    width, second, third = state.shape[1:]
    size = third // count
    pairs = width // 2
    rows = size + 2 * SWEEPS
    parts = third // LANES
    loads = []
    for pair in range(pairs):
        for i, layer in enumerate((pair, width - 1 - pair)):
            loads += copy_in(
                sems.at[pl.ds(4 * pair + 2 * i, 2)],
                [(state_hbm.at[:, layer], state.at[:, layer]), (initial_hbm.at[layer], initial.at[layer])],
            )
    stores = []
    for pair in range(pairs):
        for load in loads[4 * pair : 4 * pair + 4]:
            load.wait()
        for step in range(steps + 1):
            slot = step % 2
            for part in range(parts):
                here = slice(part * LANES, (part + 1) * LANES)
                for half, layer in enumerate((pair, width - 1 - pair)):
                    source = state[step, layer, :, here] if step < steps else initial[layer, :, here]
                    mix[slot, part, pl.ds(half, second, stride=2), :] = source
            stage_tile(mix.at[slot], stage.at[slot])
            if step < steps:
                for b in range(count):
                    begin = PAD - SWEEPS + b * size
                    out[b, step, pair * rows : (pair + 1) * rows] = stage[slot, begin : begin + rows]
            else:
                begin = pl.multiple_of(position[0] * size, 8)
                first[pair] = stage[slot, pl.ds(begin, size + 2 * PAD), :]
        if pair % 2:
            here = pl.ds((pair - 1) * rows, 2 * rows)
            stores += copy_in(
                out_sems.at[pl.ds(pair // 2, 1)], [(out.at[:, :, here], out_hbm.at[:, :, here])]
            )
    stores += copy_in(out_sems.at[pl.ds(pairs // 2, 1)], [(first, first_hbm)])
    at = 0
    for step in range(steps):
        for j in range(EARLY):
            for part in range(parts):
                here = slice(part * LANES, (part + 1) * LANES)
                up[at : at + second] = state[step, width - EARLY + j, :, here]
                down[at : at + second] = state[step, j, :, here]
                at += second
    short = size + 2 * (SWEEPS - 2)
    begin = PAD - SWEEPS + 2
    for slot in range(SWEEPS // 2):
        for out_ref, layers in (
            (up, [width - a for a in (2 * slot + 1, 2 * slot + 2)]),
            (down, [a - 1 for a in (2 * slot + 1, 2 * slot + 2)]),
        ):
            (one, one_low), (two, two_low) = [layer_half(layer, width) for layer in layers]
            out_ref[at : at + short] = merge(
                first[one, begin : begin + short],
                first[two, begin : begin + short],
                0 if one_low else 1,
                0 if two_low else 1,
            )
        at += short
    for store in stores:
        store.wait()


def early_rows(size):
    return [size + 2 * reach(EARLY - j) for j in range(EARLY)]


def late_rows(size):
    return [size + 2 * reach(SWEEPS - j) for j in range(SWEEPS - EARLY)]


def offsets(sizes):
    return [sum(sizes[:i]) for i in range(len(sizes))]


def pack_early(after, lower_hbm, upper_hbm, out_hbm, lower, upper, out, stage, mix, sems):
    count, steps = out.shape[:2]
    used = lower.shape[0] // steps
    loads = []
    for step in range(steps):
        here = pl.ds(step * used, used)
        loads += copy_in(
            sems.at[pl.ds(2 * step, 2)],
            [(lower_hbm.at[here], lower.at[here]), (upper_hbm.at[here], upper.at[here])],
        )
    parts = mix.shape[1]
    second = mix.shape[2] // 2
    size = parts * LANES // count
    sizes = early_rows(size)
    stores = []
    for step in range(steps):
        for load in loads[2 * step : 2 * step + 2]:
            load.wait()
        for j, (rows, at) in enumerate(zip(sizes, offsets(sizes))):
            slot = j % 2
            for part in range(parts):
                low = ((step * EARLY + j) * parts + part) * second
                high = ((step * EARLY + EARLY - 1 - j) * parts + part) * second
                mix[slot, part, pl.ds(0, second, stride=2), :] = lower[low : low + second]
                mix[slot, part, pl.ds(1, second, stride=2), :] = upper[high : high + second]
            stage_tile(mix.at[slot], stage.at[slot])
            for b in range(count):
                begin = PAD - (rows - size) // 2 + b * size
                out[b, step, at : at + rows] = stage[slot, begin : begin + rows]
        stores += copy_in(
            sems.at[pl.ds(2 * steps + step, 1)], [(out.at[:, step], out_hbm.at[:, step])]
        )
    for store in stores:
        store.wait()


def pack_late(pairs, size, own, up, down):
    horizon = own.shape[0]
    half = horizon // 2
    width = 2 * pairs
    stride = size + 2 * SWEEPS
    at = 0
    for j, rows in enumerate(late_rows(size)):
        a = SWEEPS - j
        for t in range(half):
            for out, layer in ((up, width - a), (down, a - 1)):
                pair, low = layer_half(layer, width)
                begin = pair * stride + (stride - rows) // 2
                before = own[t, begin : begin + rows]
                after = own[t + half, begin : begin + rows]
                here = 0 if low else 1
                out[at : at + rows] = merge(before, after, here, here)
            at += rows


def real_forward(values):
    count = len(values)
    if count == 1:
        return [(values[0], None)]
    if count == 2:
        return [(values[0] + values[1], None), (values[0] - values[1], None)]
    even = real_forward(values[0::2])
    odd = real_forward(values[1::2])
    half = count // 2
    result = [None] * (half + 1)
    for k in range(count // 4 + 1):
        even_real, even_imag = even[k]
        odd_real, odd_imag = odd[k]
        if k == 0:
            result[0] = (even_real + odd_real, None)
            result[half] = (even_real - odd_real, None)
        elif 4 * k == count:
            result[k] = (even_real, -odd_real)
        else:
            cos, sin = math.cos(2 * math.pi * k / count), math.sin(2 * math.pi * k / count)
            if odd_imag is None:
                turned_real, turned_imag = cos * odd_real, -sin * odd_real
            else:
                turned_real = cos * odd_real + sin * odd_imag
                turned_imag = cos * odd_imag - sin * odd_real
            if even_imag is None:
                result[k] = (even_real + turned_real, turned_imag)
                result[half - k] = (even_real - turned_real, turned_imag)
            else:
                result[k] = (even_real + turned_real, even_imag + turned_imag)
                result[half - k] = (even_real - turned_real, turned_imag - even_imag)
    return result


def real_inverse(modes):
    half = len(modes) - 1
    count = 2 * half
    if count == 2:
        return [modes[0][0] + modes[1][0], modes[0][0] - modes[1][0]]
    even, odd = [], []
    for k in range(count // 4 + 1):
        real, imag = modes[k]
        other_real, other_imag = modes[half - k]
        if k == 0:
            even.append((real + other_real, None))
            odd.append((real - other_real, None))
        elif 4 * k == count:
            even.append((2.0 * real, None))
            odd.append((-2.0 * imag, None))
        else:
            cos, sin = math.cos(2 * math.pi * k / count), math.sin(2 * math.pi * k / count)
            even.append((real + other_real, imag - other_imag))
            minus_real, minus_imag = real - other_real, imag + other_imag
            odd.append((cos * minus_real - sin * minus_imag, sin * minus_real + cos * minus_imag))
    result = [None] * count
    result[0::2] = real_inverse(even)
    result[1::2] = real_inverse(odd)
    return result


def mode_inverses(horizon):
    rho = alpha_value ** (1.0 / horizon)
    angles = 2.0 * math.pi * np.arange(horizon // 2 + 1) / horizon
    shift = (
        1.0 + reaction_shift + 2.0 * couple_first + 4.0 * couple_cross - rho * np.cos(angles)
    ) + 1j * rho * np.sin(angles)
    return 1.0 / shift


def sweep_table(horizon, lanes):
    inverse = relaxation * mode_inverses(horizon)
    rows = [(inverse[0].real, 0.0, 0.0, inverse[-1].real)]
    rows += [(v.real, -v.imag, v.imag, v.real) for v in inverse[1:-1]]
    table = couple_cross * np.array(rows)
    quarter = horizon // 4
    mode = np.arange(quarter)[:, None] + quarter * (np.arange(lanes) // 2 % 2)[None, :]
    spread = np.moveaxis(table[mode], -1, 1)[:, :, None, :]
    return np.broadcast_to(spread, (quarter, 4, 8, lanes)).astype(np.float32)


class Plan:
    def __init__(self, pairs):
        self.last = SWEEPS + pairs - 1
        self.begins = [SWEEPS, SWEEPS - EARLY, 0]

    def fresh(self, phase):
        end = self.last if phase == 0 else self.begins[phase - 1]
        return range(self.begins[phase] + 1, end + 1)

    def rows(self, phase, level):
        fresh = self.fresh(phase)
        return range(fresh.start + level, min(fresh.stop - 1 + level, self.last) + 1)

    def arrays(self, phase):
        return [(phase, level) for level in range(SWEEPS) if self.rows(phase, level)]

    def find(self, phase, level, row):
        for p in range(phase, -1, -1):
            if row in self.rows(p, level):
                return (p, level), row - self.rows(p, level).start
        raise ValueError((phase, level, row))

    def needed(self, phase):
        keys = set()
        for level in range(1, SWEEPS):
            for row in self.rows(phase, level):
                keys.add(self.find(phase, 0, row)[0])
                for x in (row - 1, row, min(row + 1, self.last)):
                    keys.add(self.find(phase, level - 1, x)[0])
        if phase == 2:
            for row in range(SWEEPS, self.last + 1):
                keys.add(self.find(phase, SWEEPS - 1, row)[0])
        return sorted(k for k in keys if k[0] < phase)

    def shape(self, key, horizon, size, lanes):
        rows = size + 2 * EDGE
        return (horizon, len(self.rows(*key)), rows, lanes)


def loop(count, copies, step):
    while count % copies:
        copies -= 1

    def several(index, carry):
        for i in range(copies):
            step(index * copies + i, 0)
        return carry

    lax.fori_loop(0, count // copies, several, 0)


def second_sum(tile):
    return turn(tile, 2) + turn(tile, -2)


def solve(phase, plan, pairs, size, names, far, *refs):
    named = dict(zip(names, refs))
    outs = refs[len(names) :]
    state, weighted, sems = refs[-3:]
    near = refs[-3 - len(far) : -3]
    halo = (SWEEPS // 2) * (size + 2 * (SWEEPS - 2))
    sources = {}
    for name in far:
        sources[name] = named[name]
        if name in ("first_low", "first_high"):
            sources[name] = named[name].at[pl.ds(named[name].shape[0] - halo, halo)]
    loads = dict(zip(far, copy_in(sems, [(sources[n], r) for n, r in zip(far, near)])))
    named |= dict(zip(far, near))
    horizon = weighted.shape[0]
    half, quarter = horizon // 2, horizon // 4
    last = plan.last
    window = size + 2 * EDGE
    at = PAD
    fresh = plan.fresh(phase)
    held = range(fresh.start - 1, fresh.stop + 1)
    keys = plan.arrays(phase)
    count = len(keys)
    results = outs[:1] if phase == 2 else outs[:count]
    inner_refs = refs[len(names) + len(results) :][:count] if phase != 1 else results
    final = refs[len(names) + 1 + count] if phase == 2 else None
    arrays = dict(zip(keys, inner_refs))
    for key in plan.needed(phase):
        arrays[key] = named[key]

    own, early, first = named["own"], named.get("early"), named["first"]
    early_sizes, late_sizes = early_rows(size), late_rows(size)
    early_at, late_at = offsets(early_sizes), offsets([half * rows for rows in late_sizes])
    late_count = SWEEPS - EARLY
    own_rows = size + 2 * SWEEPS

    def fill(t, carry):
        for x in held:
            if x > last:
                continue
            if x >= SWEEPS:
                begin = at + EDGE - SWEEPS
                state[1 + t, x - held.start, begin : begin + own_rows] = own[
                    t, (x - SWEEPS) * own_rows : (x - SWEEPS + 1) * own_rows
                ]
            elif x >= late_count:
                j = x - late_count
                begin = at + EDGE - (early_sizes[j] - size) // 2
                state[1 + t, x - held.start, begin : begin + early_sizes[j]] = early[
                    t, early_at[j] : early_at[j] + early_sizes[j]
                ]
        return carry

    loop(horizon, 4, fill)
    for x in held:
        if x < late_count:
            rows, where = late_sizes[x], late_at[x]
            begin = at + EDGE - (rows - size) // 2
            for t in range(half):
                low = named["late_low"][where + t * rows : where + (t + 1) * rows]
                high = named["late_high"][where + t * rows : where + (t + 1) * rows]
                state[1 + t, x - held.start, begin : begin + rows] = merge(low, high, 0, 0)
                state[1 + half + t, x - held.start, begin : begin + rows] = merge(low, high, 1, 1)
    for name in ("first", "first_low", "first_high"):
        if name in loads:
            loads.pop(name).wait()
    for x in fresh:
        if x >= SWEEPS:
            begin = at + EDGE - PAD
            state[0, x - held.start, begin : begin + size + 2 * PAD] = first[x - SWEEPS]
        else:
            a = SWEEPS - x
            rows = size + 2 * (SWEEPS - 2)
            total = named["first_low"].shape[0]
            where = total - (SWEEPS // 2 - (a - 1) // 2) * rows
            low, high = named["first_low"][where : where + rows], named["first_high"][where : where + rows]
            slot = (a - 1) % 2
            tile = merge(low, high, slot, slot)
            begin = at + EDGE - SWEEPS + 2
            state[0, x - held.start, begin : begin + rows] = tile

    def weigh(t, carry):
        centre = time_step - 1.0 - 2.0 * couple_first - 4.0 * couple_cross
        for i in range(len(fresh)):
            for r in range(at, at + window, CHUNK):
                s = state[t + 1, i + 1, r : r + CHUNK]
                outer = state[t + 1, i, r : r + CHUNK]
                along = outer + (swap(s) if fresh[i] == last else state[t + 1, i + 2, r : r + CHUNK])
                across = (
                    state[t + 1, i + 1, r - 1 : r + CHUNK - 1]
                    + state[t + 1, i + 1, r + 1 : r + CHUNK + 1]
                    + second_sum(s)
                )
                weighted[t, i, r - at : r - at + CHUNK] = (
                    (state[t, i + 1, r : r + CHUNK] + couple_first * along)
                    + (couple_cross * across + s * (centre - time_step * (s * s)))
                )
        return carry

    loop(horizon, 4, weigh)

    inverses = mode_inverses(horizon)
    weights = [alpha_value ** (n / horizon) for n in range(horizon)]
    tiles = window // 8
    base = arrays[(phase, 0)]

    def transform(index, carry):
        i = index // tiles
        r = pl.ds(pl.multiple_of((index % tiles) * 8, 8), 8)
        spectrum = real_forward([weights[n] * weighted[n, i, r, :] for n in range(horizon)])
        reals, imags = [None] * half, [None] * half
        for k, (real, imag) in enumerate(spectrum):
            c = relaxation * inverses[k]
            if k == 0:
                reals[0] = float(c.real) * real
            elif k == half:
                imags[0] = float(c.real) * real
            else:
                reals[k] = float(c.real) * real - float(c.imag) * imag
                imags[k] = float(c.imag) * real + float(c.real) * imag
        for part, values in enumerate((reals, imags)):
            for k in range(quarter):
                one, two = values[k], values[k + quarter]
                mask = first_mask(one)
                base[part * half + 2 * k, i, r, :] = jnp.where(mask, one, turn(two, 2))
                base[part * half + 2 * k + 1, i, r, :] = jnp.where(mask, turn(one, -2), two)
        return carry

    loop(len(fresh) * tiles, 3, transform)

    table = named["table"]
    for load in loads.values():
        load.wait()

    def sweep(level):
        rows = plan.rows(phase, level)
        span = size + PAD
        begin = EDGE - PAD // 2
        target = arrays[(phase, level)]

        def read(level_, part, k, parity, x, r):
            key, i = plan.find(phase, level_, x)
            return arrays[key][part * half + 2 * k + parity, i, r : r + CHUNK]

        def mode(k, carry):
            a, b, c, d = [table[k, i] for i in range(4)]
            for x in rows:
                for r in range(begin, begin + span, CHUNK):
                    for parity in (0, 1):
                        near = []
                        for part in (0, 1):
                            v = read(level - 1, part, k, parity, x, r)
                            other = read(level - 1, part, k, 1 - parity, x, r)
                            inner = (
                                swap(v)
                                if x == last
                                else read(level - 1, part, k, parity, x + 1, r)
                            )
                            along = read(level - 1, part, k, parity, x - 1, r) + inner
                            across = (
                                read(level - 1, part, k, parity, x, r - 1)
                                + read(level - 1, part, k, parity, x, r + 1)
                            ) + (other + turn(other, 4 if parity == 0 else -4))
                            near.append(
                                (
                                    read(0, part, k, parity, x, r) + (1.0 - relaxation) * v,
                                    (couple_first / couple_cross) * along + across,
                                )
                            )
                        (rest_real, near_real), (rest_imag, near_imag) = near
                        values = (
                            rest_real + (a * near_real + b * near_imag),
                            rest_imag + (c * near_real + d * near_imag),
                        )
                        here = slice(r, r + CHUNK)
                        for part, value in enumerate(values):
                            m = part * half + 2 * k + parity
                            target[m, x - rows.start, here] = value
            return carry

        loop(quarter, 2, mode)

    for key in keys:
        if key[1]:
            sweep(key[1])
    if phase == 0:
        for store in copy_in(sems, [(arrays[key], ref) for key, ref in zip(keys, results)]):
            store.wait()
    if phase < 2:
        return

    kept = size // 8
    done = [plan.find(phase, SWEEPS - 1, SWEEPS + i) for i in range(pairs)]
    stores = []
    for i, (key, row) in enumerate(done):

        for index in range(kept):
            source = arrays[key]
            r = slice(EDGE + index * 8, EDGE + index * 8 + 8)
            parts = []
            for part in (0, 1):
                values = [None] * half
                for k in range(quarter):
                    even = source[part * half + 2 * k, row, r, :]
                    odd = source[part * half + 2 * k + 1, row, r, :]
                    mask = first_mask(even)
                    values[k] = jnp.where(mask, even, turn(odd, 2))
                    values[k + quarter] = jnp.where(mask, turn(even, -2), odd)
                parts.append(values)
            reals, imags = parts
            modes = [(reals[0], None)] + list(zip(reals[1:], imags[1:])) + [(imags[0], None)]
            for n, value in enumerate(real_inverse(modes)):
                final[n, i, index * 8 : index * 8 + 8] = (1.0 / (horizon * weights[n])) * value
        stores += copy_in(sems.at[pl.ds(i, 1)], [(final.at[:, i], results[0].at[:, i])])
    for store in stores:
        store.wait()


def finish(state, pieces, updated, mix):
    count, steps, pairs, size, lanes = pieces.shape
    width = 2 * pairs
    second = lanes // 2
    per = LANES // size
    for step in range(steps):
        for pair in range(pairs):
            mirror = width - 1 - pair
            for part in range(count // per):
                here = slice(part * LANES, (part + 1) * LANES)
                piece = mix.at[pair % 2, part]
                piece[...] = jnp.concatenate(
                    [pieces[part * per + b, step, pair] for b in range(per)], axis=0
                ).T
                low, high = piece[pl.ds(0, second, stride=2), :], piece[pl.ds(1, second, stride=2), :]
                updated[step, pair, :, here] = state[step, pair, :, here] + low
                updated[step, mirror, :, here] = state[step, mirror, :, here] + high


def residual_of(state, carried, lower_hbm, upper_hbm, out, lower, upper, sems):
    steps, width, second, third = state.shape
    parts = third // LANES
    used = pl.ds(0, lower.shape[0])
    loads = copy_in(sems, [(lower_hbm.at[used], lower), (upper_hbm.at[used], upper)])
    for load in loads:
        load.wait()

    def outside(ref, step, j):
        at = (step * EARLY + j) * parts * second
        return jnp.concatenate(
            [ref[at + part * second : at + (part + 1) * second] for part in range(parts)], axis=1
        )

    for step in range(steps):
        for layer in range(width):
            s = state[step, layer]
            below = outside(lower, step, EARLY - 1) if layer == 0 else state[step, layer - 1]
            above = outside(upper, step, 0) if layer == width - 1 else state[step, layer + 1]
            before = carried[layer] if step == 0 else state[step - 1, layer]
            across = (
                pltpu.roll(s, 1, 0)
                + pltpu.roll(s, s.shape[0] - 1, 0)
                + pltpu.roll(s, 1, 1)
                + pltpu.roll(s, s.shape[1] - 1, 1)
            )
            centre = time_step - 1.0 - 2.0 * couple_first - 4.0 * couple_cross
            out[step, layer] = (
                (before + couple_first * (below + above))
                + (couple_cross * across + s * (centre - time_step * (s * s)))
            )


def shape_of(*dims):
    return jax.ShapeDtypeStruct(dims, jnp.float32)


def padded_bytes(shape):
    *major, rows, lanes = (1, 1, *shape)
    return 4 * math.prod(major) * (-(-rows // 8) * 8) * (-(-lanes // 128) * 128)


def call(kernel, outs, args, scratch=(), flops=2e6, scalars=0, far=(), far_outs=()):
    spaces = [
        pltpu.SMEM if i < scalars else pltpu.HBM if i in far else pltpu.VMEM for i in range(len(args))
    ]
    out_spaces = [pltpu.HBM if i in far_outs else pltpu.VMEM for i in range(len(outs))]
    held = [a.shape for i, a in enumerate(args) if i not in far]
    held += [o.shape for i, o in enumerate(outs) if i not in far_outs]
    held += [r.shape for r in scratch if len(r.shape) > 1]
    moved = sum(padded_bytes(a.shape) for a in (*args, *outs))
    args = [
        pltpu.with_memory_space_constraint(a, pltpu.HBM) if i in far else a for i, a in enumerate(args)
    ]
    outs = [pltpu.HBM(o.shape, o.dtype) if i in far_outs else o for i, o in enumerate(outs)]
    return pl.pallas_call(
        kernel,
        out_shape=tuple(outs),
        in_specs=[pl.BlockSpec(memory_space=space) for space in spaces],
        out_specs=tuple(pl.BlockSpec(memory_space=space) for space in out_spaces),
        scratch_shapes=list(scratch),
        compiler_params=pltpu.CompilerParams(
            vmem_limit_bytes=sum(padded_bytes(s) for s in held) + 2 * MIB
        ),
        cost_estimate=pl.CostEstimate(
            flops=int(flops), bytes_accessed=int(moved), transcendentals=0
        ),
    )(*args)


def vmem(*shape):
    return pltpu.VMEM(shape, jnp.float32)


def semaphores(count):
    return pltpu.SemaphoreType.DMA((count,))


def exchange(block):
    return lax.all_to_all(block, "tm", split_axis=0, concat_axis=0, tiled=True)


def iteration(state, initial):
    steps, width, second, third = state.shape
    count = lax.axis_size("tm")
    horizon = steps * count
    half = horizon // 2
    position = lax.axis_index("tm")
    pairs = width // 2
    size = third // count
    lanes = 2 * second
    stage = vmem(2, third + 2 * PAD, lanes)
    mixer = vmem(2, third // LANES, lanes, LANES)

    raw_rows = EARLY * steps * second * (third // LANES)
    sent_rows = raw_rows + (SWEEPS // 2) * (size + 2 * SWEEPS - 4)
    own_shape = (count, steps, pairs * (size + 2 * SWEEPS), lanes)
    first_shape = (pairs, size + 2 * PAD, lanes)
    sent, first, up, down = call(
        pack_own,
        [
            shape_of(*own_shape),
            shape_of(*first_shape),
            shape_of(sent_rows, LANES),
            shape_of(sent_rows, LANES),
        ],
        [position.reshape(1), state, initial],
        [
            vmem(*state.shape),
            vmem(*initial.shape),
            vmem(*own_shape),
            vmem(*first_shape),
            stage,
            mixer,
            semaphores(4 * pairs),
            semaphores(pairs // 2 + 1),
        ],
        scalars=1,
        far=(1, 2),
        far_outs=(0, 1),
    )
    own = exchange(sent).reshape(horizon, -1, lanes)

    lower = hop(up, 1)
    upper = hop(down, -1)

    late_shape = shape_of(half * sum(late_rows(size)), lanes)
    late_up, late_down = call(functools.partial(pack_late, pairs, size), [late_shape] * 2, [own])
    late_low = hop(late_up, 1)
    late_high = hop(late_down, -1)

    early_shape = (count, steps, sum(early_rows(size)), lanes)
    (sent_early,) = call(
        pack_early,
        [shape_of(*early_shape)],
        [late_up, lower, upper],
        [
            vmem(raw_rows, LANES),
            vmem(raw_rows, LANES),
            vmem(*early_shape),
            stage,
            mixer,
            semaphores(3 * steps),
        ],
        far=(0, 1, 2),
        far_outs=(0,),
    )
    early = exchange(sent_early).reshape(horizon, -1, lanes)

    carried = lax.ppermute(state[steps - 1], "tm", [(i, i + 1) for i in range(count - 1)])
    carried = jnp.where(position == 0, initial, carried)
    (residual,) = call(
        residual_of,
        [shape_of(*state.shape)],
        [state, carried, lower, upper],
        [vmem(raw_rows, LANES), vmem(raw_rows, LANES), semaphores(2)],
        flops=6e6,
        far=(2, 3),
    )

    plan = Plan(pairs)
    table = jnp.asarray(sweep_table(horizon, lanes))
    arrays = {}
    for phase in range(3):
        inputs = {"table": table, "own": own, "first": first}
        if phase:
            inputs |= {"early": early, "first_low": lower, "first_high": upper}
        if phase == 2:
            inputs |= {"late_low": late_low, "late_high": late_high}
        inputs |= {key: arrays[key] for key in plan.needed(phase)}
        keys = plan.arrays(phase)
        outs = [shape_of(*plan.shape(key, horizon, size, lanes)) for key in keys]
        fresh = len(plan.fresh(phase))
        halo = vmem((SWEEPS // 2) * (size + 2 * (SWEEPS - 2)), lanes)
        far = [n for n in inputs if n in ("first", "first_low", "first_high") or n[0] == 0]
        near = [halo if n[:6] == "first_" else vmem(*inputs[n].shape) for n in far]
        scratch = near + [
            vmem(horizon + 1, fresh + 2, size + 2 * EDGE + 2 * PAD, lanes),
            vmem(horizon, fresh, size + 2 * EDGE, lanes),
            semaphores(max(len(far), len(keys), pairs)),
        ]
        inner = [vmem(*o.shape) for o in outs]
        if phase == 0:
            scratch = inner + scratch
        if phase == 2:
            scratch = inner + [vmem(horizon, pairs, size, lanes)] + scratch
            outs = [shape_of(horizon, pairs, size, lanes)]
        results = call(
            functools.partial(solve, phase, plan, pairs, size, list(inputs), far),
            outs,
            list(inputs.values()),
            scratch,
            flops=3e7,
            far=[i for i, n in enumerate(inputs) if n in far],
            far_outs=() if phase == 1 else range(len(outs)),
        )
        arrays |= dict(zip(keys, results)) if phase < 2 else {}
    moved = results[0].reshape(count, steps, pairs, size, lanes)

    pieces = exchange(moved)
    (updated,) = call(finish, [shape_of(*state.shape)], [state, pieces], [mixer])
    return (updated, residual)


def solution(mesh):
    in_specs = (P("tm", "space", None, None), P("space", None, None))
    out_specs = (P("tm", "space", None, None), P("tm", "space", None, None))
    return jax.shard_map(iteration, mesh=mesh, in_specs=in_specs, out_specs=out_specs, check_vma=False)
```

time: 162 us -> 97.7 us (0.60); the launches traced: 159 us -> 97.2 us
  waiting for transfers between devices: 72.5 us -> 41 us
  Pallas kernels: 0 us -> 29.6 us
  blocking collectives: 17.8 us -> 0 us
  local copies, waits for them, and re-layouts: 18.5 us -> 3.17 us
  starting transfers between devices: 36 us -> 22.6 us
  other arithmetic: 10.6 us -> 0.07 us
  matrix products: 2.16 us -> 0 us
    pallas_call x0 -> x8, Pallas kernels: none -> 29.6 us  [call(): pl.pallas_call(kernel, out_shape=tuple(outs), in_specs=[pl.BlockSpec(memo...]
    all_to_all x3, waiting for transfers between devices: 41.4 us -> 18.3 us  [exchange(): return lax.all_to_all(block, 'tm', split_axis=0, concat_axis=0, tiled=True)]
    all_to_all x1 -> x0, blocking collectives: 17.8 us -> none  [body(): lax.all_to_all(restored, 'tm', split_axis=0, concat_axis=1, tiled=True)]
    ppermute x13 -> x5, starting transfers between devices: 19.8 us -> 9.66 us  [the longest x4 7.65 us: hop(): return lax.ppermute(block, 'space', ring('space', step))]
    add x18 -> x0, other arithmetic: 9.31 us -> none  [the longest x5 3.99 us: body(): fields + nearby]
    ppermute x13 -> x5, waiting for transfers between devices: 31.1 us -> 22.7 us  [the longest x1 16.7 us: iteration(): lax.ppermute(state[steps - 1], 'tm', [(i, i + 1) for i in range(count - 1)])]
    slice x30 -> x0, local copies, waits for them, and re-layouts: 7.36 us -> none  [the longest x12 5.18 us: cross_sum(): jnp.roll(field, -1, -1)]
    add x2 -> x0, local copies, waits for them, and re-layouts: 3.56 us -> none  [the longest x1 1.78 us: body(): before - state + laplace + time_step * (state - state * state * state)]
  transfers between devices with their start and end apart: 16 -> 8, of which waited for: 14 -> 5; matrix products, arithmetic and copies ran while one was open for 3% -> 1% of each run, Pallas kernels for 0% -> 15%
where the time goes in v3:
time: 97.7 us; the launch traced here: 97.2 us
  waiting for transfers between devices  41 us (42%)
  Pallas kernels  29.6 us (30%)
  starting transfers between devices  22.6 us (23%)
  local copies, waits for them, and re-layouts  3.17 us (3%)
    pallas_call x8, Pallas kernels, call(): pl.pallas_call(kernel, out_shape=tuple(outs), in_specs=[pl.BlockSpec(memo...  29.6 us
    all_to_all x3, waiting for transfers between devices, exchange(): return lax.all_to_all(block, 'tm', split_axis=0, concat_axis=0, tiled=True)  18.3 us
    ppermute x1, waiting for transfers between devices, iteration(): lax.ppermute(state[steps - 1], 'tm', [(i, i + 1) for i in range(count - 1)])  16.7 us
    all_to_all x3, starting transfers between devices, exchange(): return lax.all_to_all(block, 'tm', split_axis=0, concat_axis=0, tiled=True)  12.9 us
    ppermute x4, starting transfers between devices, hop(): return lax.ppermute(block, 'space', ring('space', step))  7.65 us
    ppermute x4, waiting for transfers between devices, hop(): return lax.ppermute(block, 'space', ring('space', step))  6.03 us
    unnamed x16, local copies, waits for them, and re-layouts  2.33 us
    ppermute x1, starting transfers between devices, iteration(): lax.ppermute(state[steps - 1], 'tm', [(i, i + 1) for i in range(count - 1)])  2.01 us
  transfers between devices with their start and end apart: 8, of which 5 were waited for; matrix products, arithmetic and copies ran while one was open for 1% of the time, Pallas kernels for 15%

profile of v3, /device:TPU:4, one launch (start us, length us, event | category | flops | bytes accessed | tf_op | source)
XLA Modules:
  0.0 97.2 jit_solution(2728483125692524571)
XLA Ops:
  0.6 3.0 %shard_map.50 = (f32[8,2,176,128]{3,2,1,0:T(8,128)}, f32[4,48,128]{2,1,0:T(8,128)}, f32[888,128]{1,0:T(8,128)S(1)}, f32[888,128]{1,0:T(8,128)S(1)}) custom-call(s32[1]{0:T(128)} %bitcast.position, f32[2,8,64,256]{3,2,1,0:T(8,128)} %state.3, f32[8,64,256]{2,1,0:T(8,128)} %initial_hbm.1), custom_call_target="tpu_custom_call" | custom-call | flops 2000000 | bytes 4026368 | tf_op jit(solution)/shard_map/pallas_call | solution.py:645
  3.6 4.2 %all-to-all-start = ((f32[8,2,176,128]{3,2,1,0:T(8,128)}), f32[8,2,176,128]{3,2,1,0:T(8,128)S(1)}, u32[]{:S(2)}, u32[]{:S(2)}) async-start(f32[8,2,176,128]{3,2,1,0:T(8,128)} %get-tuple-element.17), calls=%async_computation | async-start | bytes 2883584 | tf_op jit(solution)/shard_map/all_to_all | solution.py:669
  7.9 1.6 %collective-permute-start = (f32[888,128]{1,0:T(8,128)S(1)}, f32[888,128]{1,0:T(8,128)S(1)}, u32[]{:S(2)}, u32[]{:S(2)}) collective-permute-start(f32[888,128]{1,0:T(8,128)S(1)} %get-tuple-element.20), channel_id=1, source_target_pairs={{0,1},{1,2},{2,3},{3,0},{4,5},{5,6},{6,7},{7,4},{8,9},{9,10},{10,1... | collective-permute-start | bytes 1363976 | tf_op jit(solution)/shard_map/ppermute | solution.py:40
  9.4 2.2 %collective-permute-start.1 = (f32[888,128]{1,0:T(8,128)S(1)}, f32[888,128]{1,0:T(8,128)S(1)}, u32[]{:S(2)}, u32[]{:S(2)}) collective-permute-start(f32[888,128]{1,0:T(8,128)S(1)} %get-tuple-element.21), channel_id=1, source_target_pairs={{0,3},{1,0},{2,1},{3,2},{4,7},{5,4},{6,5},{7,6},{8,11},{9,8},{10,9... | collective-permute-start | bytes 1363976 | tf_op jit(solution)/shard_map/ppermute | solution.py:40
  11.7 14.3 %all-to-all-done = f32[8,2,176,128]{3,2,1,0:T(8,128)S(1)} async-done(((f32[8,2,176,128]{3,2,1,0:T(8,128)}), f32[8,2,176,128]{3,2,1,0:T(8,128)S(1)}, u32[]{:S(2)}, u32[]{:S(2)}) %all-to-all-start) | async-done | bytes 1441824 | tf_op jit(solution)/shard_map/all_to_all | solution.py:669
  26.0 0.3 shard_map.51
  26.3 0.0 copy-start.2
  26.3 0.7 copy-done.2
  27.0 0.0 copy-start.4
  27.0 0.8 copy-done.4
  27.8 0.0 collective-permute-done.lower_hbm.refs_4_
  27.8 0.0 copy-start.5
  27.8 3.5 %collective-permute-done.1.upper_hbm.refs_5_ = f32[888,128]{1,0:T(8,128)S(1)} collective-permute-done((f32[888,128]{1,0:T(8,128)S(1)}, f32[888,128]{1,0:T(8,128)S(1)}, u32[]{:S(2)}, u32[]{:S(2)}) %collective-permute-start.1) | collective-permute-done | bytes 454688 | tf_op jit(solution)/shard_map/ppermute | solution.py:40
  31.4 0.0 copy-start.6
  31.4 0.0 copy-done.5
  31.4 0.8 copy-done.6
  32.1 2.3 %shard_map.52 = f32[8,2,120,128]{3,2,1,0:T(8,128)} custom-call(f32[816,128]{1,0:T(8,128)} %copy-done.2, f32[888,128]{1,0:T(8,128)} %copy-done.5, f32[888,128]{1,0:T(8,128)} %copy-done.6), custom_call_target="tpu_custom_call" | custom-call | flops 2000000 | bytes 2310144 | tf_op jit(solution)/shard_map/pallas_call | solution.py:645
  34.5 0.0 copy-start.3
  34.5 0.0 copy-start.1
  34.5 4.3 %all-to-all-start.1 = ((f32[8,2,120,128]{3,2,1,0:T(8,128)}), f32[8,2,120,128]{3,2,1,0:T(8,128)S(1)}, u32[]{:S(2)}, u32[]{:S(2)}) async-start(f32[8,2,120,128]{3,2,1,0:T(8,128)} %shard_map.52), calls=%async_computation.1 | async-start | bytes 1966080 | tf_op jit(solution)/shard_map/all_to_all | solution.py:669
  38.8 0.0 copy-done.3
  38.8 1.1 %collective-permute-start.2 = (f32[816,128]{1,0:T(8,128)S(1)}, f32[816,128]{1,0:T(8,128)S(1)}, u32[]{:S(2)}, u32[]{:S(2)}) collective-permute-start(f32[816,128]{1,0:T(8,128)S(1)} %copy-done.3), channel_id=1, source_target_pairs={{0,1},{1,2},{2,3},{3,0},{4,5},{5,6},{6,7},{7,4},{8,9},{9,10},{10,1... | collective-permute-start | bytes 1253384 | tf_op jit(solution)/shard_map/ppermute | solution.py:40
  40.0 2.7 %collective-permute-start.3 = (f32[816,128]{1,0:T(8,128)}, f32[816,128]{1,0:T(8,128)}, u32[]{:S(2)}, u32[]{:S(2)}) collective-permute-start(f32[816,128]{1,0:T(8,128)} %copy-done.4), channel_id=1, source_target_pairs={{0,3},{1,0},{2,1},{3,2},{4,7},{5,4},{6,5},{7,6},{8,11},{9,8},{10,9... | collective-permute-start | bytes 1253384 | tf_op jit(solution)/shard_map/ppermute | solution.py:40
  42.7 0.0 copy-done.1
  42.7 5.4 %shard_map.53 = (f32[16,3,56,128]{3,2,1,0:T(8,128)}, f32[16,2,56,128]{3,2,1,0:T(8,128)}, f32[16,1,56,128]{3,2,1,0:T(8,128)}) custom-call(f32[4,4,8,128]{3,2,1,0:T(8,128)S(1)} %copy-done.1, f32[16,176,128]{2,1,0:T(8,128)S(1)} %bitcast.7, f32[4,48,128]{2,1,0:T(8,128)} %get-tuple-element.18.refs_2_), custom_call_target="tpu_custom_call" | custom-call | flops 30000000 | bytes 4358144 | tf_op jit(solution)/shard_map/pallas_call | solution.py:645
  48.1 4.0 %all-to-all-done.1 = f32[8,2,120,128]{3,2,1,0:T(8,128)S(1)} async-done(((f32[8,2,120,128]{3,2,1,0:T(8,128)}), f32[8,2,120,128]{3,2,1,0:T(8,128)S(1)}, u32[]{:S(2)}, u32[]{:S(2)}) %all-to-all-start.1) | async-done | bytes 983072 | tf_op jit(solution)/shard_map/all_to_all | solution.py:669
  52.0 6.1 %shard_map.54 = (f32[16,3,56,128]{3,2,1,0:T(8,128)S(1)}, f32[16,3,56,128]{3,2,1,0:T(8,128)S(1)}, f32[16,3,56,128]{3,2,1,0:T(8,128)S(1)}, f32[16,3,56,128]{3,2,1,...) custom-call(f32[4,4,8,128]{3,2,1,0:T(8,128)S(1)} %copy-done.1, ...), custom_call_target="tpu_custom_call" | custom-call | flops 30000000 | bytes 13131776 | tf_op jit(solution)/shard_map/pallas_call | solution.py:645
  58.1 0.0 collective-permute-done.2.refs_6_
  58.1 2.5 %collective-permute-done.3.refs_7_ = f32[816,128]{1,0:T(8,128)} collective-permute-done((f32[816,128]{1,0:T(8,128)}, f32[816,128]{1,0:T(8,128)}, u32[]{:S(2)}, u32[]{:S(2)}) %collective-permute-start.3) | collective-permute-done | bytes 417824 | tf_op jit(solution)/shard_map/ppermute | solution.py:40
  60.6 8.3 %shard_map.55 = f32[16,4,32,128]{3,2,1,0:T(8,128)} custom-call(f32[4,4,8,128]{3,2,1,0:T(8,128)S(1)} %copy-done.1, f32[16,176,128]{2,1,0:T(8,128)S(1)} %bitcast.9, f32[4,48,128]{2,1,0:T(8,128)} %get-tuple-element.18.refs_2_, f32[16,120,128]{2,1,0:T(8,128)S(1)} %bitcast.11, f32[888,128]{1,0:T(8,128)} %copy-done.5, f32[888,128]{1,0:T(8,128)} %copy-done.6, ...), custom_call_target="tpu_custom_call" | custom-call | flops 30000000 | bytes 13639680 | tf_op jit(solution)/shard_map/pallas_call | solution.py:645
  69.0 0.0 copy-start
  69.0 0.0 copy-start.7
  69.0 4.3 %all-to-all-start.2 = ((f32[8,2,4,32,128]{4,3,2,1,0:T(8,128)}), f32[8,2,4,32,128]{4,3,2,1,0:T(8,128)S(1)}, u32[]{:S(2)}, u32[]{:S(2)}) async-start(f32[8,2,4,32,128]{4,3,2,1,0:T(8,128)} %bitcast.12), calls=%async_computation.2 | async-start | bytes 2097152 | tf_op jit(solution)/shard_map/all_to_all | solution.py:669
  73.3 0.0 copy-done
  73.3 0.8 slice_bitcast_fusion
  74.2 2.0 %collective-permute-start.4 = (f32[8,64,256]{2,1,0:T(8,128)}, f32[8,64,256]{2,1,0:T(8,128)S(1)}, u32[]{:S(2)}, u32[]{:S(2)}) collective-permute-start(f32[8,64,256]{2,1,0:T(8,128)} %slice_bitcast_fusion), channel_id=1, source_target_pairs={{0,4},{4,8},{8,12},{12,16},{16,20},{20,24},{24,28},{1,5},{5,9},{9,... | collective-permute-start | bytes 1572872 | tf_op jit(solution)/shard_map/ppermute | solution.py:739
  76.2 16.7 %collective-permute-done.4 = f32[8,64,256]{2,1,0:T(8,128)S(1)} collective-permute-done((f32[8,64,256]{2,1,0:T(8,128)}, f32[8,64,256]{2,1,0:T(8,128)S(1)}, u32[]{:S(2)}, u32[]{:S(2)}) %collective-permute-start.4) | collective-permute-done | bytes 524320 | tf_op jit(solution)/shard_map/ppermute | solution.py:739
  92.8 0.0 copy-done.7
  92.9 0.1 broadcast_select_fusion.carried
  92.9 2.8 %shard_map.57 = f32[2,8,64,256]{3,2,1,0:T(8,128)} custom-call(f32[2,8,64,256]{3,2,1,0:T(8,128)S(1)} %copy-done, f32[8,64,256]{2,1,0:T(8,128)S(1)} %broadcast_select_fusion.carried, f32[888,128]{1,0:T(8,128)} %copy-done.5, f32[888,128]{1,0:T(8,128)} %copy-done.6), custom_call_target="tpu_custom_call" | custom-call | flops 6000000 | bytes 3530752 | tf_op jit(solution)/shard_map/pallas_call | solution.py:645
  95.7 0.0 all-to-all-done.2.pieces
  95.8 1.4 %shard_map.56 = f32[2,8,64,256]{3,2,1,0:T(8,128)} custom-call(f32[2,8,64,256]{3,2,1,0:T(8,128)S(1)} %copy-done, f32[8,2,4,32,128]{4,3,2,1,0:T(8,128)S(1)} %all-to-all-done.2.pieces), custom_call_target="tpu_custom_call" | custom-call | flops 2000000 | bytes 3145728 | tf_op jit(solution)/shard_map/pallas_call | solution.py:645
Async XLA Ops:
  3.6 22.4 %all-to-all-start = ((f32[8,2,176,128]{3,2,1,0:T(8,128)}), f32[8,2,176,128]{3,2,1,0:T(8,128)S(1)}, u32[]{:S(2)}, u32[]{:S(2)}) async-start(f32[8,2,176,128]{3,2,1,0:T(8,128)} %get-tuple-element.17), calls=%async_computation | async-start | bytes 2883584 | tf_op jit(solution)/shard_map/all_to_all | solution.py:669
  7.9 20.0 %collective-permute-start = (f32[888,128]{1,0:T(8,128)S(1)}, f32[888,128]{1,0:T(8,128)S(1)}, u32[]{:S(2)}, u32[]{:S(2)}) collective-permute-start(f32[888,128]{1,0:T(8,128)S(1)} %get-tuple-element.20), channel_id=1, source_target_pairs={{0,1},{1,2},{2,3},{3,0},{4,5},{5,6},{6,7},{7,4},{8,9},{9,10},{10,1... | collective-permute-start | bytes 1363976 | tf_op jit(solution)/shard_map/ppermute | solution.py:40
  9.4 21.9 %collective-permute-start.1 = (f32[888,128]{1,0:T(8,128)S(1)}, f32[888,128]{1,0:T(8,128)S(1)}, u32[]{:S(2)}, u32[]{:S(2)}) collective-permute-start(f32[888,128]{1,0:T(8,128)S(1)} %get-tuple-element.21), channel_id=1, source_target_pairs={{0,3},{1,0},{2,1},{3,2},{4,7},{5,4},{6,5},{7,6},{8,11},{9,8},{10,9... | collective-permute-start | bytes 1363976 | tf_op jit(solution)/shard_map/ppermute | solution.py:40
  26.3 0.8 copy-start.2
  27.0 0.8 copy-start.4
  27.8 3.5 %copy-start.5 = (f32[888,128]{1,0:T(8,128)}, f32[888,128]{1,0:T(8,128)S(1)}, u32[]{:S(2)}) copy-start(f32[888,128]{1,0:T(8,128)S(1)} %collective-permute-done.lower_hbm.refs_4_) | copy-start | bytes 1363972
  31.4 0.8 copy-start.6
  34.5 4.4 %copy-start.3 = (f32[816,128]{1,0:T(8,128)S(1)}, f32[816,128]{1,0:T(8,128)}, u32[]{:S(2)}) copy-start(f32[816,128]{1,0:T(8,128)} %copy-done.2) | copy-start | bytes 1253380
  34.5 8.2 %copy-start.1 = (f32[4,4,8,128]{3,2,1,0:T(8,128)S(1)}, f32[4,4,8,128]{3,2,1,0:T(8,128)}, u32[]{:S(2)}) copy-start(f32[4,4,8,128]{3,2,1,0:T(8,128)} %constant.10.clone.refs_0_) | copy-start | bytes 196612
  34.5 17.6 %all-to-all-start.1 = ((f32[8,2,120,128]{3,2,1,0:T(8,128)}), f32[8,2,120,128]{3,2,1,0:T(8,128)S(1)}, u32[]{:S(2)}, u32[]{:S(2)}) async-start(f32[8,2,120,128]{3,2,1,0:T(8,128)} %shard_map.52), calls=%async_computation.1 | async-start | bytes 1966080 | tf_op jit(solution)/shard_map/all_to_all | solution.py:669
  38.8 19.3 %collective-permute-start.2 = (f32[816,128]{1,0:T(8,128)S(1)}, f32[816,128]{1,0:T(8,128)S(1)}, u32[]{:S(2)}, u32[]{:S(2)}) collective-permute-start(f32[816,128]{1,0:T(8,128)S(1)} %copy-done.3), channel_id=1, source_target_pairs={{0,1},{1,2},{2,3},{3,0},{4,5},{5,6},{6,7},{7,4},{8,9},{9,10},{10,1... | collective-permute-start | bytes 1253384 | tf_op jit(solution)/shard_map/ppermute | solution.py:40
  40.0 20.7 %collective-permute-start.3 = (f32[816,128]{1,0:T(8,128)}, f32[816,128]{1,0:T(8,128)}, u32[]{:S(2)}, u32[]{:S(2)}) collective-permute-start(f32[816,128]{1,0:T(8,128)} %copy-done.4), channel_id=1, source_target_pairs={{0,3},{1,0},{2,1},{3,2},{4,7},{5,4},{6,5},{7,6},{8,11},{9,8},{10,9... | collective-permute-start | bytes 1253384 | tf_op jit(solution)/shard_map/ppermute | solution.py:40
  69.0 4.4 %copy-start = (f32[2,8,64,256]{3,2,1,0:T(8,128)S(1)}, f32[2,8,64,256]{3,2,1,0:T(8,128)}, u32[]{:S(2)}) copy-start(f32[2,8,64,256]{3,2,1,0:T(8,128)} %state.3) | copy-start | bytes 3145732
  69.0 23.9 %copy-start.7 = (f32[8,64,256]{2,1,0:T(8,128)S(1)}, f32[8,64,256]{2,1,0:T(8,128)}, u32[]{:S(2)}) copy-start(f32[8,64,256]{2,1,0:T(8,128)} %initial_hbm.1) | copy-start | bytes 1572868
  69.0 26.8 %all-to-all-start.2 = ((f32[8,2,4,32,128]{4,3,2,1,0:T(8,128)}), f32[8,2,4,32,128]{4,3,2,1,0:T(8,128)S(1)}, u32[]{:S(2)}, u32[]{:S(2)}) async-start(f32[8,2,4,32,128]{4,3,2,1,0:T(8,128)} %bitcast.12), calls=%async_computation.2 | async-start | bytes 2097152 | tf_op jit(solution)/shard_map/all_to_all | solution.py:669
  74.2 18.7 %collective-permute-start.4 = (f32[8,64,256]{2,1,0:T(8,128)}, f32[8,64,256]{2,1,0:T(8,128)S(1)}, u32[]{:S(2)}, u32[]{:S(2)}) collective-permute-start(f32[8,64,256]{2,1,0:T(8,128)} %slice_bitcast_fusion), channel_id=1, source_target_pairs={{0,4},{4,8},{8,12},{12,16},{16,20},{20,24},{24,28},{1,5},{5,9},{9,... | collective-permute-start | bytes 1572872 | tf_op jit(solution)/shard_map/ppermute | solution.py:739

commit v4 on v3

--- a/solution.py
+++ b/solution.py
@@ -20,6 +20,7 @@
 reaction_shift = 0.1
 relaxation = 0.9
 
+SPLIT = 4
 CHUNK = 8
 LANES = 128
 PAD = 8
@@ -79,6 +80,14 @@
     for copy in copies:
         copy.start()
     return copies
+
+
+def split(source, target, step):
+    some = source.shape[0] // SPLIT
+    return [
+        (source.at[pl.ds(i * some, some), step], target.at[pl.ds(i * some, some), step])
+        for i in range(SPLIT)
+    ]
 
 
 def pack_own(
@@ -119,7 +128,8 @@
         if pair % 2:
             here = pl.ds((pair - 1) * rows, 2 * rows)
             stores += copy_in(
-                out_sems.at[pl.ds(pair // 2, 1)], [(out.at[:, :, here], out_hbm.at[:, :, here])]
+                out_sems.at[pl.ds(pair // 2, 1)],
+                [(out.at[:, :, here], out_hbm.at[:, :, here])],
             )
     stores += copy_in(out_sems.at[pl.ds(pairs // 2, 1)], [(first, first_hbm)])
     at = 0
@@ -161,24 +171,26 @@
     return [sum(sizes[:i]) for i in range(len(sizes))]
 
 
-def pack_early(after, lower_hbm, upper_hbm, out_hbm, lower, upper, out, stage, mix, sems):
+def pack_early(after, lower, upper, out_hbm, kept_low, kept_high, out, stage, mix, sems):
     count, steps = out.shape[:2]
-    used = lower.shape[0] // steps
-    loads = []
-    for step in range(steps):
-        here = pl.ds(step * used, used)
-        loads += copy_in(
-            sems.at[pl.ds(2 * step, 2)],
-            [(lower_hbm.at[here], lower.at[here]), (upper_hbm.at[here], upper.at[here])],
-        )
     parts = mix.shape[1]
     second = mix.shape[2] // 2
     size = parts * LANES // count
     sizes = early_rows(size)
+    layer = parts * second
+    raw = EARLY * steps * layer
     stores = []
+    for i, (source, target, nearest) in enumerate(
+        ((lower, kept_low, EARLY - 1), (upper, kept_high, 0))
+    ):
+        pieces = [
+            (source.at[pl.ds((step * EARLY + nearest) * layer, layer)], target.at[pl.ds(step * layer, layer)])
+            for step in range(steps)
+        ]
+        rest = source.shape[0] - raw
+        pieces.append((source.at[pl.ds(raw, rest)], target.at[pl.ds(steps * layer, rest)]))
+        stores += copy_in(sems.at[pl.ds(i * (steps + 1), steps + 1)], pieces)
     for step in range(steps):
-        for load in loads[2 * step : 2 * step + 2]:
-            load.wait()
         for j, (rows, at) in enumerate(zip(sizes, offsets(sizes))):
             slot = j % 2
             for part in range(parts):
@@ -191,7 +203,7 @@
                 begin = PAD - (rows - size) // 2 + b * size
                 out[b, step, at : at + rows] = stage[slot, begin : begin + rows]
         stores += copy_in(
-            sems.at[pl.ds(2 * steps + step, 1)], [(out.at[:, step], out_hbm.at[:, step])]
+            sems.at[pl.ds(2 * steps + 2 + step * SPLIT, SPLIT)], split(out, out_hbm, step)
         )
     for store in stores:
         store.wait()
@@ -299,7 +311,8 @@
 class Plan:
     def __init__(self, pairs):
         self.last = SWEEPS + pairs - 1
-        self.begins = [SWEEPS, SWEEPS - EARLY, 0]
+        self.begins = [SWEEPS, 0]
+        self.final = len(self.begins) - 1
 
     def fresh(self, phase):
         end = self.last if phase == 0 else self.begins[phase - 1]
@@ -325,7 +338,7 @@
                 keys.add(self.find(phase, 0, row)[0])
                 for x in (row - 1, row, min(row + 1, self.last)):
                     keys.add(self.find(phase, level - 1, x)[0])
-        if phase == 2:
+        if phase == self.final:
             for row in range(SWEEPS, self.last + 1):
                 keys.add(self.find(phase, SWEEPS - 1, row)[0])
         return sorted(k for k in keys if k[0] < phase)
@@ -373,9 +386,10 @@
     held = range(fresh.start - 1, fresh.stop + 1)
     keys = plan.arrays(phase)
     count = len(keys)
-    results = outs[:1] if phase == 2 else outs[:count]
-    inner_refs = refs[len(names) + len(results) :][:count] if phase != 1 else results
-    final = refs[len(names) + 1 + count] if phase == 2 else None
+    ends = phase == plan.final
+    results = outs[:1] if ends else outs[:count]
+    inner_refs = refs[len(names) + len(results) :][:count] if ends or phase == 0 else results
+    final = refs[len(names) + 1 + count] if ends else None
     arrays = dict(zip(keys, inner_refs))
     for key in plan.needed(phase):
         arrays[key] = named[key]
@@ -449,7 +463,7 @@
                 )
         return carry
 
-    loop(horizon, 4, weigh)
+    loop(horizon, 8, weigh)
 
     inverses = mode_inverses(horizon)
     weights = [alpha_value ** (n / horizon) for n in range(horizon)]
@@ -478,7 +492,7 @@
                 base[part * half + 2 * k + 1, i, r, :] = jnp.where(mask, turn(one, -2), two)
         return carry
 
-    loop(len(fresh) * tiles, 3, transform)
+    loop(len(fresh) * tiles, 7, transform)
 
     table = named["table"]
     for load in loads.values():
@@ -530,7 +544,7 @@
                             target[m, x - rows.start, here] = value
             return carry
 
-        loop(quarter, 2, mode)
+        loop(quarter, 4, mode)
 
     for key in keys:
         if key[1]:
@@ -538,7 +552,7 @@
     if phase == 0:
         for store in copy_in(sems, [(arrays[key], ref) for key, ref in zip(keys, results)]):
             store.wait()
-    if phase < 2:
+    if not ends:
         return
 
     kept = size // 8
@@ -568,11 +582,12 @@
         store.wait()
 
 
-def finish(state, pieces, updated, mix):
+def finish(state, pieces, out, updated, mix, sems):
     count, steps, pairs, size, lanes = pieces.shape
     width = 2 * pairs
     second = lanes // 2
     per = LANES // size
+    stores = []
     for step in range(steps):
         for pair in range(pairs):
             mirror = width - 1 - pair
@@ -585,6 +600,13 @@
                 low, high = piece[pl.ds(0, second, stride=2), :], piece[pl.ds(1, second, stride=2), :]
                 updated[step, pair, :, here] = state[step, pair, :, here] + low
                 updated[step, mirror, :, here] = state[step, mirror, :, here] + high
+            first = 2 * (step * pairs + pair)
+            stores += copy_in(
+                sems.at[pl.ds(first, 2)],
+                [(updated.at[step, layer], out.at[step, layer]) for layer in (pair, mirror)],
+            )
+    for store in stores:
+        store.wait()
 
 
 def residual_of(state, carried, lower_hbm, upper_hbm, out, lower, upper, sems):
@@ -595,8 +617,8 @@
     for load in loads:
         load.wait()
 
-    def outside(ref, step, j):
-        at = (step * EARLY + j) * parts * second
+    def outside(ref, step):
+        at = step * parts * second
         return jnp.concatenate(
             [ref[at + part * second : at + (part + 1) * second] for part in range(parts)], axis=1
         )
@@ -604,8 +626,8 @@
     for step in range(steps):
         for layer in range(width):
             s = state[step, layer]
-            below = outside(lower, step, EARLY - 1) if layer == 0 else state[step, layer - 1]
-            above = outside(upper, step, 0) if layer == width - 1 else state[step, layer + 1]
+            below = outside(lower, step) if layer == 0 else state[step, layer - 1]
+            above = outside(upper, step) if layer == width - 1 else state[step, layer + 1]
             before = carried[layer] if step == 0 else state[step - 1, layer]
             across = (
                 pltpu.roll(s, 1, 0)
@@ -719,20 +741,14 @@
     late_high = hop(late_down, -1)
 
     early_shape = (count, steps, sum(early_rows(size)), lanes)
-    (sent_early,) = call(
+    kept = shape_of(steps * second * (third // LANES) + sent_rows - raw_rows, LANES)
+    sent_early, kept_low, kept_high = call(
         pack_early,
-        [shape_of(*early_shape)],
+        [shape_of(*early_shape), kept, kept],
         [late_up, lower, upper],
-        [
-            vmem(raw_rows, LANES),
-            vmem(raw_rows, LANES),
-            vmem(*early_shape),
-            stage,
-            mixer,
-            semaphores(3 * steps),
-        ],
-        far=(0, 1, 2),
-        far_outs=(0,),
+        [vmem(*early_shape), stage, mixer, semaphores(2 * steps + 2 + SPLIT * steps)],
+        far=(0,),
+        far_outs=(0, 1, 2),
     )
     early = exchange(sent_early).reshape(horizon, -1, lanes)
 
@@ -741,8 +757,8 @@
     (residual,) = call(
         residual_of,
         [shape_of(*state.shape)],
-        [state, carried, lower, upper],
-        [vmem(raw_rows, LANES), vmem(raw_rows, LANES), semaphores(2)],
+        [state, carried, kept_low, kept_high],
+        [vmem(raw_rows // EARLY, LANES), vmem(raw_rows // EARLY, LANES), semaphores(2)],
         flops=6e6,
         far=(2, 3),
     )
@@ -750,11 +766,12 @@
     plan = Plan(pairs)
     table = jnp.asarray(sweep_table(horizon, lanes))
     arrays = {}
-    for phase in range(3):
+    for phase in range(plan.final + 1):
+        ends = phase == plan.final
         inputs = {"table": table, "own": own, "first": first}
         if phase:
-            inputs |= {"early": early, "first_low": lower, "first_high": upper}
-        if phase == 2:
+            inputs |= {"early": early, "first_low": kept_low, "first_high": kept_high}
+        if ends:
             inputs |= {"late_low": late_low, "late_high": late_high}
         inputs |= {key: arrays[key] for key in plan.needed(phase)}
         keys = plan.arrays(phase)
@@ -771,7 +788,7 @@
         inner = [vmem(*o.shape) for o in outs]
         if phase == 0:
             scratch = inner + scratch
-        if phase == 2:
+        if ends:
             scratch = inner + [vmem(horizon, pairs, size, lanes)] + scratch
             outs = [shape_of(horizon, pairs, size, lanes)]
         results = call(
@@ -781,13 +798,19 @@
             scratch,
             flops=3e7,
             far=[i for i, n in enumerate(inputs) if n in far],
-            far_outs=() if phase == 1 else range(len(outs)),
+            far_outs=range(len(outs)) if ends or phase == 0 else (),
         )
-        arrays |= dict(zip(keys, results)) if phase < 2 else {}
+        arrays |= {} if ends else dict(zip(keys, results))
     moved = results[0].reshape(count, steps, pairs, size, lanes)
 
     pieces = exchange(moved)
-    (updated,) = call(finish, [shape_of(*state.shape)], [state, pieces], [mixer])
+    (updated,) = call(
+        finish,
+        [shape_of(*state.shape)],
+        [state, pieces],
+        [vmem(*state.shape), mixer, semaphores(steps * width)],
+        far_outs=(0,),
+    )
     return (updated, residual)
 
 

time: 97.7 us -> 97.7 us (level)
  Pallas kernels: 29.6 us -> 22.4 us
  waiting for transfers between devices: 41 us -> 48.2 us
    ppermute x4, waiting for transfers between devices: 6.03 us -> 17.3 us  [hop(): return lax.ppermute(block, 'space', ring('space', step))]
    pallas_call x8 -> x7, Pallas kernels: 29.6 us -> 22.4 us  [call(): pl.pallas_call(kernel, out_shape=tuple(outs), in_specs=[pl.BlockSpec(memo...]
    all_to_all x3, waiting for transfers between devices: 18.3 us -> 14.3 us  [exchange(): return lax.all_to_all(block, 'tm', split_axis=0, concat_axis=0, tiled=True)]
  transfers between devices with their start and end apart: 8 -> 8, of which waited for: 5 -> 5; matrix products, arithmetic and copies ran while one was open for 1% -> 1% of each run, Pallas kernels for 15% -> 8%
where the time goes in v4:
time: 97.7 us; the launch traced here: 97.2 us
  waiting for transfers between devices  48.2 us (49%)
  Pallas kernels  22.4 us (23%)
  starting transfers between devices  22.4 us (23%)
  local copies, waits for them, and re-layouts  3.38 us (3%)
    pallas_call x7, Pallas kernels, call(): pl.pallas_call(kernel, out_shape=tuple(outs), in_specs=[pl.BlockSpec(memo...  22.4 us
    ppermute x4, waiting for transfers between devices, hop(): return lax.ppermute(block, 'space', ring('space', step))  17.3 us
    ppermute x1, waiting for transfers between devices, iteration(): lax.ppermute(state[steps - 1], 'tm', [(i, i + 1) for i in range(count - 1)])  16.7 us
    all_to_all x3, waiting for transfers between devices, exchange(): return lax.all_to_all(block, 'tm', split_axis=0, concat_axis=0, tiled=True)  14.3 us
    all_to_all x3, starting transfers between devices, exchange(): return lax.all_to_all(block, 'tm', split_axis=0, concat_axis=0, tiled=True)  12.8 us
    ppermute x4, starting transfers between devices, hop(): return lax.ppermute(block, 'space', ring('space', step))  7.65 us
    unnamed x16, local copies, waits for them, and re-layouts  2.53 us
    ppermute x1, starting transfers between devices, iteration(): lax.ppermute(state[steps - 1], 'tm', [(i, i + 1) for i in range(count - 1)])  2.01 us
  transfers between devices with their start and end apart: 8, of which 5 were waited for; matrix products, arithmetic and copies ran while one was open for 1% of the time, Pallas kernels for 8%

profile of v4, /device:TPU:4, one launch (start us, length us, event | category | flops | bytes accessed | tf_op | source)
XLA Modules:
  0.0 97.2 jit_solution(3909438375180692173)
XLA Ops:
  0.6 3.0 %shard_map.50 = (f32[8,2,176,128]{3,2,1,0:T(8,128)}, f32[4,48,128]{2,1,0:T(8,128)}, f32[888,128]{1,0:T(8,128)S(1)}, f32[888,128]{1,0:T(8,128)S(1)}) custom-call(s32[1]{0:T(128)} %bitcast.position, f32[2,8,64,256]{3,2,1,0:T(8,128)} %state.3, f32[8,64,256]{2,1,0:T(8,128)} %initial_hbm.1), custom_call_target="tpu_custom_call" | custom-call | flops 2000000 | bytes 4026368 | tf_op jit(solution)/shard_map/pallas_call | solution.py:667
  3.6 4.2 %all-to-all-start = ((f32[8,2,176,128]{3,2,1,0:T(8,128)}), f32[8,2,176,128]{3,2,1,0:T(8,128)S(1)}, u32[]{:S(2)}, u32[]{:S(2)}) async-start(f32[8,2,176,128]{3,2,1,0:T(8,128)} %get-tuple-element.14), calls=%async_computation | async-start | bytes 2883584 | tf_op jit(solution)/shard_map/all_to_all | solution.py:691
  7.8 1.6 %collective-permute-start = (f32[888,128]{1,0:T(8,128)S(1)}, f32[888,128]{1,0:T(8,128)S(1)}, u32[]{:S(2)}, u32[]{:S(2)}) collective-permute-start(f32[888,128]{1,0:T(8,128)S(1)} %get-tuple-element.17), channel_id=1, source_target_pairs={{0,1},{1,2},{2,3},{3,0},{4,5},{5,6},{6,7},{7,4},{8,9},{9,10},{10,1... | collective-permute-start | bytes 1363976 | tf_op jit(solution)/shard_map/ppermute | solution.py:41
  9.4 2.2 %collective-permute-start.1 = (f32[888,128]{1,0:T(8,128)S(1)}, f32[888,128]{1,0:T(8,128)S(1)}, u32[]{:S(2)}, u32[]{:S(2)}) collective-permute-start(f32[888,128]{1,0:T(8,128)S(1)} %get-tuple-element.18), channel_id=1, source_target_pairs={{0,3},{1,0},{2,1},{3,2},{4,7},{5,4},{6,5},{7,6},{8,11},{9,8},{10,9... | collective-permute-start | bytes 1363976 | tf_op jit(solution)/shard_map/ppermute | solution.py:41
  11.7 14.3 %all-to-all-done = f32[8,2,176,128]{3,2,1,0:T(8,128)S(1)} async-done(((f32[8,2,176,128]{3,2,1,0:T(8,128)}), f32[8,2,176,128]{3,2,1,0:T(8,128)S(1)}, u32[]{:S(2)}, u32[]{:S(2)}) %all-to-all-start) | async-done | bytes 1441824 | tf_op jit(solution)/shard_map/all_to_all | solution.py:691
  26.0 0.3 shard_map.51
  26.3 0.0 copy-start.1
  26.3 0.7 copy-done.1
  27.0 0.0 copy-start.6
  27.0 0.0 collective-permute-done.lower
  27.0 4.3 %collective-permute-done.1.upper = f32[888,128]{1,0:T(8,128)S(1)} collective-permute-done((f32[888,128]{1,0:T(8,128)S(1)}, f32[888,128]{1,0:T(8,128)S(1)}, u32[]{:S(2)}, u32[]{:S(2)}) %collective-permute-start.1) | collective-permute-done | bytes 454688 | tf_op jit(solution)/shard_map/ppermute | solution.py:41
  31.3 0.0 copy-start.2
  31.3 0.0 copy-start.5
  31.3 1.3 %shard_map.52 = (f32[8,2,120,128]{3,2,1,0:T(8,128)}, f32[376,128]{1,0:T(8,128)}, f32[376,128]{1,0:T(8,128)}) custom-call(f32[816,128]{1,0:T(8,128)} %copy-done.1, f32[888,128]{1,0:T(8,128)S(1)} %collective-permute-done.lower, f32[888,128]{1,0:T(8,128)S(1)} %collective-permute-done.1.upper), custom_call_target="tpu_custom_call" | custom-call | flops 2000000 | bytes 2695168 | tf_op jit(solution)/shard_map/pallas_call | solution.py:667
  32.7 0.0 copy-done.6
  32.7 4.2 %all-to-all-start.1 = ((f32[8,2,120,128]{3,2,1,0:T(8,128)}), f32[8,2,120,128]{3,2,1,0:T(8,128)S(1)}, u32[]{:S(2)}, u32[]{:S(2)}) async-start(f32[8,2,120,128]{3,2,1,0:T(8,128)} %get-tuple-element.19), calls=%async_computation.1 | async-start | bytes 1966080 | tf_op jit(solution)/shard_map/all_to_all | solution.py:691
  36.9 0.0 copy-done.2
  36.9 1.1 %collective-permute-start.2 = (f32[816,128]{1,0:T(8,128)S(1)}, f32[816,128]{1,0:T(8,128)S(1)}, u32[]{:S(2)}, u32[]{:S(2)}) collective-permute-start(f32[816,128]{1,0:T(8,128)S(1)} %copy-done.2), channel_id=1, source_target_pairs={{0,1},{1,2},{2,3},{3,0},{4,5},{5,6},{6,7},{7,4},{8,9},{9,10},{10,1... | collective-permute-start | bytes 1253384 | tf_op jit(solution)/shard_map/ppermute | solution.py:41
  38.0 2.7 %collective-permute-start.3 = (f32[816,128]{1,0:T(8,128)}, f32[816,128]{1,0:T(8,128)S(1)}, u32[]{:S(2)}, u32[]{:S(2)}) collective-permute-start(f32[816,128]{1,0:T(8,128)} %copy-done.6), channel_id=1, source_target_pairs={{0,3},{1,0},{2,1},{3,2},{4,7},{5,4},{6,5},{7,6},{8,11},{9,8},{10,9... | collective-permute-start | bytes 1253384 | tf_op jit(solution)/shard_map/ppermute | solution.py:41
  40.7 0.0 copy-done.5
  40.7 4.9 %shard_map.53 = (f32[16,3,56,128]{3,2,1,0:T(8,128)}, f32[16,2,56,128]{3,2,1,0:T(8,128)}, f32[16,1,56,128]{3,2,1,0:T(8,128)}) custom-call(f32[4,4,8,128]{3,2,1,0:T(8,128)S(1)} %copy-done.5, f32[16,176,128]{2,1,0:T(8,128)S(1)} %bitcast.7, f32[4,48,128]{2,1,0:T(8,128)} %get-tuple-element.15.refs_2_), custom_call_target="tpu_custom_call" | custom-call | flops 30000000 | bytes 4358144 | tf_op jit(solution)/shard_map/pallas_call | solution.py:667
  45.6 5.6 %collective-permute-done.2.refs_6_ = f32[816,128]{1,0:T(8,128)S(1)} collective-permute-done((f32[816,128]{1,0:T(8,128)S(1)}, f32[816,128]{1,0:T(8,128)S(1)}, u32[]{:S(2)}, u32[]{:S(2)}) %collective-permute-start.2) | collective-permute-done | bytes 417824 | tf_op jit(solution)/shard_map/ppermute | solution.py:41
  51.2 7.3 %collective-permute-done.3.refs_7_ = f32[816,128]{1,0:T(8,128)S(1)} collective-permute-done((f32[816,128]{1,0:T(8,128)}, f32[816,128]{1,0:T(8,128)S(1)}, u32[]{:S(2)}, u32[]{:S(2)}) %collective-permute-start.3) | collective-permute-done | bytes 417824 | tf_op jit(solution)/shard_map/ppermute | solution.py:41
  58.5 0.0 copy-start.3
  58.5 0.8 copy-done.3
  59.3 0.0 all-to-all-done.1
  59.3 0.0 copy-start.4
  59.3 1.0 %copy-done.4 = f32[816,128]{1,0:T(8,128)S(1)} copy-done((f32[816,128]{1,0:T(8,128)S(1)}, f32[816,128]{1,0:T(8,128)}, u32[]{:S(2)}) %copy-start.4) | copy-done | bytes 417816
  60.3 9.0 %shard_map.54 = f32[16,4,32,128]{3,2,1,0:T(8,128)} custom-call(f32[4,4,8,128]{3,2,1,0:T(8,128)S(1)} %copy-done.5, f32[16,176,128]{2,1,0:T(8,128)S(1)} %bitcast.8, f32[4,48,128]{2,1,0:T(8,128)} %get-tuple-element.15.refs_2_, f32[16,120,128]{2,1,0:T(8,128)S(1)} %bitcast.9, f32[376,128]{1,0:T(8,128)} %get-tuple-element.20.refs_4_.lower_hbm, ...), custom_call_target="tpu_custom_call" | custom-call | flops 30000000 | bytes 7610368 | tf_op jit(solution)/shard_map/pallas_call | solution.py:667
  69.3 0.0 copy-start
  69.4 0.0 copy-start.7
  69.4 4.3 %all-to-all-start.2 = ((f32[8,2,4,32,128]{4,3,2,1,0:T(8,128)}), f32[8,2,4,32,128]{4,3,2,1,0:T(8,128)S(1)}, u32[]{:S(2)}, u32[]{:S(2)}) async-start(f32[8,2,4,32,128]{4,3,2,1,0:T(8,128)} %bitcast.10), calls=%async_computation.2 | async-start | bytes 2097152 | tf_op jit(solution)/shard_map/all_to_all | solution.py:691
  73.7 0.0 copy-done
  73.7 0.8 slice_bitcast_fusion
  74.6 2.0 %collective-permute-start.4 = (f32[8,64,256]{2,1,0:T(8,128)}, f32[8,64,256]{2,1,0:T(8,128)S(1)}, u32[]{:S(2)}, u32[]{:S(2)}) collective-permute-start(f32[8,64,256]{2,1,0:T(8,128)} %slice_bitcast_fusion), channel_id=1, source_target_pairs={{0,4},{4,8},{8,12},{12,16},{16,20},{20,24},{24,28},{1,5},{5,9},{9,... | collective-permute-start | bytes 1572872 | tf_op jit(solution)/shard_map/ppermute | solution.py:755
  76.6 16.7 %collective-permute-done.4 = f32[8,64,256]{2,1,0:T(8,128)S(1)} collective-permute-done((f32[8,64,256]{2,1,0:T(8,128)}, f32[8,64,256]{2,1,0:T(8,128)S(1)}, u32[]{:S(2)}, u32[]{:S(2)}) %collective-permute-start.4) | collective-permute-done | bytes 524320 | tf_op jit(solution)/shard_map/ppermute | solution.py:755
  93.2 0.0 copy-done.7
  93.2 0.1 broadcast_select_fusion.carried
  93.3 2.7 %shard_map.56 = f32[2,8,64,256]{3,2,1,0:T(8,128)} custom-call(f32[2,8,64,256]{3,2,1,0:T(8,128)S(1)} %copy-done, f32[8,64,256]{2,1,0:T(8,128)S(1)} %broadcast_select_fusion.carried, f32[376,128]{1,0:T(8,128)} %get-tuple-element.20.refs_4_.lower_hbm, f32[376,128]{1,0:T(8,128)} %get-tuple-element.21.refs_5_.upper_hbm), custom_call_target="tpu_custom_call" | custom-call | flops 6000000 | bytes 3006464 | tf_op jit(solution)/shard_map/pallas_call | solution.py:667
  96.0 0.0 all-to-all-done.2.pieces
  96.0 1.2 %shard_map.55 = f32[2,8,64,256]{3,2,1,0:T(8,128)} custom-call(f32[2,8,64,256]{3,2,1,0:T(8,128)S(1)} %copy-done, f32[8,2,4,32,128]{4,3,2,1,0:T(8,128)S(1)} %all-to-all-done.2.pieces), custom_call_target="tpu_custom_call" | custom-call | flops 2000000 | bytes 3145728 | tf_op jit(solution)/shard_map/pallas_call | solution.py:667
Async XLA Ops:
  3.6 22.4 %all-to-all-start = ((f32[8,2,176,128]{3,2,1,0:T(8,128)}), f32[8,2,176,128]{3,2,1,0:T(8,128)S(1)}, u32[]{:S(2)}, u32[]{:S(2)}) async-start(f32[8,2,176,128]{3,2,1,0:T(8,128)} %get-tuple-element.14), calls=%async_computation | async-start | bytes 2883584 | tf_op jit(solution)/shard_map/all_to_all | solution.py:691
  7.8 19.2 %collective-permute-start = (f32[888,128]{1,0:T(8,128)S(1)}, f32[888,128]{1,0:T(8,128)S(1)}, u32[]{:S(2)}, u32[]{:S(2)}) collective-permute-start(f32[888,128]{1,0:T(8,128)S(1)} %get-tuple-element.17), channel_id=1, source_target_pairs={{0,1},{1,2},{2,3},{3,0},{4,5},{5,6},{6,7},{7,4},{8,9},{9,10},{10,1... | collective-permute-start | bytes 1363976 | tf_op jit(solution)/shard_map/ppermute | solution.py:41
  9.4 21.9 %collective-permute-start.1 = (f32[888,128]{1,0:T(8,128)S(1)}, f32[888,128]{1,0:T(8,128)S(1)}, u32[]{:S(2)}, u32[]{:S(2)}) collective-permute-start(f32[888,128]{1,0:T(8,128)S(1)} %get-tuple-element.18), channel_id=1, source_target_pairs={{0,3},{1,0},{2,1},{3,2},{4,7},{5,4},{6,5},{7,6},{8,11},{9,8},{10,9... | collective-permute-start | bytes 1363976 | tf_op jit(solution)/shard_map/ppermute | solution.py:41
  26.3 0.8 copy-start.1
  27.0 5.6 %copy-start.6 = (f32[816,128]{1,0:T(8,128)}, f32[816,128]{1,0:T(8,128)S(1)}, u32[]{:S(2)}) copy-start(f32[816,128]{1,0:T(8,128)S(1)} %get-tuple-element.22) | copy-start | bytes 1253380
  31.3 5.5 %copy-start.2 = (f32[816,128]{1,0:T(8,128)S(1)}, f32[816,128]{1,0:T(8,128)}, u32[]{:S(2)}) copy-start(f32[816,128]{1,0:T(8,128)} %copy-done.1) | copy-start | bytes 1253380
  31.3 9.4 %copy-start.5 = (f32[4,4,8,128]{3,2,1,0:T(8,128)S(1)}, f32[4,4,8,128]{3,2,1,0:T(8,128)}, u32[]{:S(2)}) copy-start(f32[4,4,8,128]{3,2,1,0:T(8,128)} %constant.10.clone.refs_0_) | copy-start | bytes 196612
  32.7 26.6 %all-to-all-start.1 = ((f32[8,2,120,128]{3,2,1,0:T(8,128)}), f32[8,2,120,128]{3,2,1,0:T(8,128)S(1)}, u32[]{:S(2)}, u32[]{:S(2)}) async-start(f32[8,2,120,128]{3,2,1,0:T(8,128)} %get-tuple-element.19), calls=%async_computation.1 | async-start | bytes 1966080 | tf_op jit(solution)/shard_map/all_to_all | solution.py:691
  36.9 14.4 %collective-permute-start.2 = (f32[816,128]{1,0:T(8,128)S(1)}, f32[816,128]{1,0:T(8,128)S(1)}, u32[]{:S(2)}, u32[]{:S(2)}) collective-permute-start(f32[816,128]{1,0:T(8,128)S(1)} %copy-done.2), channel_id=1, source_target_pairs={{0,1},{1,2},{2,3},{3,0},{4,5},{5,6},{6,7},{7,4},{8,9},{9,10},{10,1... | collective-permute-start | bytes 1253384 | tf_op jit(solution)/shard_map/ppermute | solution.py:41
  38.0 20.5 %collective-permute-start.3 = (f32[816,128]{1,0:T(8,128)}, f32[816,128]{1,0:T(8,128)S(1)}, u32[]{:S(2)}, u32[]{:S(2)}) collective-permute-start(f32[816,128]{1,0:T(8,128)} %copy-done.6), channel_id=1, source_target_pairs={{0,3},{1,0},{2,1},{3,2},{4,7},{5,4},{6,5},{7,6},{8,11},{9,8},{10,9... | collective-permute-start | bytes 1253384 | tf_op jit(solution)/shard_map/ppermute | solution.py:41
  58.5 0.8 copy-start.3
  59.3 1.0 %copy-start.4 = (f32[816,128]{1,0:T(8,128)S(1)}, f32[816,128]{1,0:T(8,128)}, u32[]{:S(2)}) copy-start(f32[816,128]{1,0:T(8,128)} %copy-done.3) | copy-start | bytes 1253380
  69.3 4.4 %copy-start = (f32[2,8,64,256]{3,2,1,0:T(8,128)S(1)}, f32[2,8,64,256]{3,2,1,0:T(8,128)}, u32[]{:S(2)}) copy-start(f32[2,8,64,256]{3,2,1,0:T(8,128)} %state.3) | copy-start | bytes 3145732
  69.4 23.9 %copy-start.7 = (f32[8,64,256]{2,1,0:T(8,128)S(1)}, f32[8,64,256]{2,1,0:T(8,128)}, u32[]{:S(2)}) copy-start(f32[8,64,256]{2,1,0:T(8,128)} %initial_hbm.1) | copy-start | bytes 1572868
  69.4 26.6 %all-to-all-start.2 = ((f32[8,2,4,32,128]{4,3,2,1,0:T(8,128)}), f32[8,2,4,32,128]{4,3,2,1,0:T(8,128)S(1)}, u32[]{:S(2)}, u32[]{:S(2)}) async-start(f32[8,2,4,32,128]{4,3,2,1,0:T(8,128)} %bitcast.10), calls=%async_computation.2 | async-start | bytes 2097152 | tf_op jit(solution)/shard_map/all_to_all | solution.py:691
  74.6 18.7 %collective-permute-start.4 = (f32[8,64,256]{2,1,0:T(8,128)}, f32[8,64,256]{2,1,0:T(8,128)S(1)}, u32[]{:S(2)}, u32[]{:S(2)}) collective-permute-start(f32[8,64,256]{2,1,0:T(8,128)} %slice_bitcast_fusion), channel_id=1, source_target_pairs={{0,4},{4,8},{8,12},{12,16},{16,20},{20,24},{24,28},{1,5},{5,9},{9,... | collective-permute-start | bytes 1572872 | tf_op jit(solution)/shard_map/ppermute | solution.py:755

commit v5 on v4

--- a/solution.py
+++ b/solution.py
@@ -91,7 +91,24 @@
 
 
 def pack_own(
-    position, state_hbm, initial_hbm, out_hbm, first_hbm, up, down, state, initial, out, first, stage, mix, sems, out_sems
+    position,
+    state_hbm,
+    initial_hbm,
+    out_hbm,
+    first_hbm,
+    up_hbm,
+    down_hbm,
+    state,
+    initial,
+    out,
+    first,
+    up,
+    down,
+    stage,
+    mix,
+    sems,
+    out_sems,
+    halo_sems,
 ):
     count, steps = out.shape[:2]
     width, second, third = state.shape[1:]
@@ -110,6 +127,18 @@
     for pair in range(pairs):
         for load in loads[4 * pair : 4 * pair + 4]:
             load.wait()
+        if pair < EARLY:
+            pieces = []
+            for step in range(steps):
+                for part in range(parts):
+                    here = pl.ds(part * LANES, LANES)
+                    for target, layer, j in (
+                        (up_hbm, width - 1 - pair, EARLY - 1 - pair),
+                        (down_hbm, pair, pair),
+                    ):
+                        row = ((step * EARLY + j) * parts + part) * second
+                        pieces.append((state.at[step, layer, :, here], target.at[pl.ds(row, second)]))
+            stores += copy_in(halo_sems.at[pl.ds(pair * len(pieces), len(pieces))], pieces)
         for step in range(steps + 1):
             slot = step % 2
             for part in range(parts):
@@ -133,13 +162,6 @@
             )
     stores += copy_in(out_sems.at[pl.ds(pairs // 2, 1)], [(first, first_hbm)])
     at = 0
-    for step in range(steps):
-        for j in range(EARLY):
-            for part in range(parts):
-                here = slice(part * LANES, (part + 1) * LANES)
-                up[at : at + second] = state[step, width - EARLY + j, :, here]
-                down[at : at + second] = state[step, j, :, here]
-                at += second
     short = size + 2 * (SWEEPS - 2)
     begin = PAD - SWEEPS + 2
     for slot in range(SWEEPS // 2):
@@ -155,6 +177,11 @@
                 0 if two_low else 1,
             )
         at += short
+    raw = up_hbm.shape[0] - at
+    stores += copy_in(
+        halo_sems.at[pl.ds(2 * EARLY * steps * parts, 2)],
+        [(up, up_hbm.at[pl.ds(raw, at)]), (down, down_hbm.at[pl.ds(raw, at)])],
+    )
     for store in stores:
         store.wait()
 
@@ -308,6 +335,9 @@
     return np.broadcast_to(spread, (quarter, 4, 8, lanes)).astype(np.float32)
 
 
+FAR = ("late_low", "late_high", "first", "first_low", "first_high")
+
+
 class Plan:
     def __init__(self, pairs):
         self.last = SWEEPS + pairs - 1
@@ -418,6 +448,9 @@
         return carry
 
     loop(horizon, 4, fill)
+    for name in FAR:
+        if name in loads:
+            loads.pop(name).wait()
     for x in held:
         if x < late_count:
             rows, where = late_sizes[x], late_at[x]
@@ -427,9 +460,6 @@
                 high = named["late_high"][where + t * rows : where + (t + 1) * rows]
                 state[1 + t, x - held.start, begin : begin + rows] = merge(low, high, 0, 0)
                 state[1 + half + t, x - held.start, begin : begin + rows] = merge(low, high, 1, 1)
-    for name in ("first", "first_low", "first_high"):
-        if name in loads:
-            loads.pop(name).wait()
     for x in fresh:
         if x >= SWEEPS:
             begin = at + EDGE - PAD
@@ -721,14 +751,17 @@
             vmem(*initial.shape),
             vmem(*own_shape),
             vmem(*first_shape),
+            vmem(sent_rows - raw_rows, LANES),
+            vmem(sent_rows - raw_rows, LANES),
             stage,
             mixer,
             semaphores(4 * pairs),
             semaphores(pairs // 2 + 1),
+            semaphores(2 * EARLY * steps * (third // LANES) + 2),
         ],
         scalars=1,
         far=(1, 2),
-        far_outs=(0, 1),
+        far_outs=(0, 1, 2, 3),
     )
     own = exchange(sent).reshape(horizon, -1, lanes)
 
@@ -778,7 +811,7 @@
         outs = [shape_of(*plan.shape(key, horizon, size, lanes)) for key in keys]
         fresh = len(plan.fresh(phase))
         halo = vmem((SWEEPS // 2) * (size + 2 * (SWEEPS - 2)), lanes)
-        far = [n for n in inputs if n in ("first", "first_low", "first_high") or n[0] == 0]
+        far = [n for n in inputs if n in FAR or n[0] == 0]
         near = [halo if n[:6] == "first_" else vmem(*inputs[n].shape) for n in far]
         scratch = near + [
             vmem(horizon + 1, fresh + 2, size + 2 * EDGE + 2 * PAD, lanes),

time: 97.7 us -> 97 us (level)
  local copies, waits for them, and re-layouts: 3.38 us -> 2.36 us
    unnamed x16 -> x14, local copies, waits for them, and re-layouts: 2.53 us -> 1.53 us
where the time goes in v5:
time: 97 us; the launch traced here: 96.6 us
  waiting for transfers between devices  47.6 us (49%)
  Pallas kernels  23.2 us (24%)
  starting transfers between devices  22.6 us (23%)
  local copies, waits for them, and re-layouts  2.36 us (2%)
    pallas_call x7, Pallas kernels, call(): pl.pallas_call(kernel, out_shape=tuple(outs), in_specs=[pl.BlockSpec(memo...  23.2 us
    ppermute x1, waiting for transfers between devices, iteration(): lax.ppermute(state[steps - 1], 'tm', [(i, i + 1) for i in range(count - 1)])  16.7 us
    ppermute x4, waiting for transfers between devices, hop(): return lax.ppermute(block, 'space', ring('space', step))  16.6 us
    all_to_all x3, waiting for transfers between devices, exchange(): return lax.all_to_all(block, 'tm', split_axis=0, concat_axis=0, tiled=True)  14.3 us
    all_to_all x3, starting transfers between devices, exchange(): return lax.all_to_all(block, 'tm', split_axis=0, concat_axis=0, tiled=True)  12.9 us
    ppermute x4, starting transfers between devices, hop(): return lax.ppermute(block, 'space', ring('space', step))  7.65 us
    ppermute x1, starting transfers between devices, iteration(): lax.ppermute(state[steps - 1], 'tm', [(i, i + 1) for i in range(count - 1)])  2.01 us
  transfers between devices with their start and end apart: 8, of which 5 were waited for; matrix products, arithmetic and copies ran while one was open for 1% of the time, Pallas kernels for 8%

profile of v5, /device:TPU:4, one launch (start us, length us, event | category | flops | bytes accessed | tf_op | source)
XLA Modules:
  0.0 96.6 jit_solution(1347890221738398188)
XLA Ops:
  0.6 3.2 %shard_map.50 = (f32[8,2,176,128]{3,2,1,0:T(8,128)}, f32[4,48,128]{2,1,0:T(8,128)}, f32[888,128]{1,0:T(8,128)}, f32[888,128]{1,0:T(8,128)}) custom-call(s32[1]{0:T(128)} %bitcast.position, f32[2,8,64,256]{3,2,1,0:T(8,128)} %state.3, f32[8,64,256]{2,1,0:T(8,128)} %initial_hbm.1), custom_call_target="tpu_custom_call" | custom-call | flops 2000000 | bytes 4026368 | tf_op jit(solution)/shard_map/pallas_call | solution.py:697
  3.9 0.0 copy-start.6
  3.9 4.4 %all-to-all-start = ((f32[8,2,176,128]{3,2,1,0:T(8,128)}), f32[8,2,176,128]{3,2,1,0:T(8,128)S(1)}, u32[]{:S(2)}, u32[]{:S(2)}) async-start(f32[8,2,176,128]{3,2,1,0:T(8,128)} %get-tuple-element.14), calls=%async_computation | async-start | bytes 2883584 | tf_op jit(solution)/shard_map/all_to_all | solution.py:721
  8.2 1.6 %collective-permute-start = (f32[888,128]{1,0:T(8,128)}, f32[888,128]{1,0:T(8,128)S(1)}, u32[]{:S(2)}, u32[]{:S(2)}) collective-permute-start(f32[888,128]{1,0:T(8,128)} %get-tuple-element.17), channel_id=1, source_target_pairs={{0,1},{1,2},{2,3},{3,0},{4,5},{5,6},{6,7},{7,4},{8,9},{9,10},{10,1... | collective-permute-start | bytes 1363976 | tf_op jit(solution)/shard_map/ppermute | solution.py:41
  9.8 0.0 copy-done.6
  9.8 2.2 %collective-permute-start.1 = (f32[888,128]{1,0:T(8,128)S(1)}, f32[888,128]{1,0:T(8,128)S(1)}, u32[]{:S(2)}, u32[]{:S(2)}) collective-permute-start(f32[888,128]{1,0:T(8,128)S(1)} %copy-done.6), channel_id=1, source_target_pairs={{0,3},{1,0},{2,1},{3,2},{4,7},{5,4},{6,5},{7,6},{8,11},{9,8},{10,9... | collective-permute-start | bytes 1363976 | tf_op jit(solution)/shard_map/ppermute | solution.py:41
  12.0 14.3 %all-to-all-done = f32[8,2,176,128]{3,2,1,0:T(8,128)S(1)} async-done(((f32[8,2,176,128]{3,2,1,0:T(8,128)}), f32[8,2,176,128]{3,2,1,0:T(8,128)S(1)}, u32[]{:S(2)}, u32[]{:S(2)}) %all-to-all-start) | async-done | bytes 1441824 | tf_op jit(solution)/shard_map/all_to_all | solution.py:721
  26.3 0.3 shard_map.51
  26.7 0.0 copy-start.1
  26.7 0.7 copy-done.1
  27.4 0.0 collective-permute-done.lower
  27.4 4.3 %collective-permute-done.1.upper = f32[888,128]{1,0:T(8,128)S(1)} collective-permute-done((f32[888,128]{1,0:T(8,128)S(1)}, f32[888,128]{1,0:T(8,128)S(1)}, u32[]{:S(2)}, u32[]{:S(2)}) %collective-permute-start.1) | collective-permute-done | bytes 454688 | tf_op jit(solution)/shard_map/ppermute | solution.py:41
  31.7 0.0 copy-start.2
  31.7 0.0 copy-start.3
  31.7 1.3 %shard_map.52 = (f32[8,2,120,128]{3,2,1,0:T(8,128)}, f32[376,128]{1,0:T(8,128)}, f32[376,128]{1,0:T(8,128)}) custom-call(f32[816,128]{1,0:T(8,128)} %copy-done.1, f32[888,128]{1,0:T(8,128)S(1)} %collective-permute-done.lower, f32[888,128]{1,0:T(8,128)S(1)} %collective-permute-done.1.upper), custom_call_target="tpu_custom_call" | custom-call | flops 2000000 | bytes 2695168 | tf_op jit(solution)/shard_map/pallas_call | solution.py:697
  33.0 4.2 %all-to-all-start.1 = ((f32[8,2,120,128]{3,2,1,0:T(8,128)}), f32[8,2,120,128]{3,2,1,0:T(8,128)S(1)}, u32[]{:S(2)}, u32[]{:S(2)}) async-start(f32[8,2,120,128]{3,2,1,0:T(8,128)} %get-tuple-element.19), calls=%async_computation.1 | async-start | bytes 1966080 | tf_op jit(solution)/shard_map/all_to_all | solution.py:721
  37.2 0.0 copy-done.2
  37.2 1.3 %collective-permute-start.2 = (f32[816,128]{1,0:T(8,128)S(1)}, f32[816,128]{1,0:T(8,128)S(1)}, u32[]{:S(2)}, u32[]{:S(2)}) collective-permute-start(f32[816,128]{1,0:T(8,128)S(1)} %copy-done.2), channel_id=1, source_target_pairs={{0,1},{1,2},{2,3},{3,0},{4,5},{5,6},{6,7},{7,4},{8,9},{9,10},{10,1... | collective-permute-start | bytes 1253384 | tf_op jit(solution)/shard_map/ppermute | solution.py:41
  38.6 2.5 %collective-permute-start.3 = (f32[816,128]{1,0:T(8,128)S(1)}, f32[816,128]{1,0:T(8,128)}, u32[]{:S(2)}, u32[]{:S(2)}) collective-permute-start(f32[816,128]{1,0:T(8,128)S(1)} %get-tuple-element.22), channel_id=1, source_target_pairs={{0,3},{1,0},{2,1},{3,2},{4,7},{5,4},{6,5},{7,6},{8,11},{9,8},{10,9... | collective-permute-start | bytes 1253384 | tf_op jit(solution)/shard_map/ppermute | solution.py:41
  41.1 0.0 copy-done.3
  41.1 4.9 %shard_map.53 = (f32[16,3,56,128]{3,2,1,0:T(8,128)}, f32[16,2,56,128]{3,2,1,0:T(8,128)}, f32[16,1,56,128]{3,2,1,0:T(8,128)}) custom-call(f32[4,4,8,128]{3,2,1,0:T(8,128)S(1)} %copy-done.3, f32[16,176,128]{2,1,0:T(8,128)S(1)} %bitcast.7, f32[4,48,128]{2,1,0:T(8,128)} %get-tuple-element.15.refs_2_), custom_call_target="tpu_custom_call" | custom-call | flops 30000000 | bytes 4358144 | tf_op jit(solution)/shard_map/pallas_call | solution.py:697
  46.0 5.6 %collective-permute-done.2.refs_6_ = f32[816,128]{1,0:T(8,128)S(1)} collective-permute-done((f32[816,128]{1,0:T(8,128)S(1)}, f32[816,128]{1,0:T(8,128)S(1)}, u32[]{:S(2)}, u32[]{:S(2)}) %collective-permute-start.2) | collective-permute-done | bytes 417824 | tf_op jit(solution)/shard_map/ppermute | solution.py:41
  51.6 0.0 copy-start.5
  51.6 0.8 copy-done.5
  52.4 6.7 %collective-permute-done.3.refs_7_ = f32[816,128]{1,0:T(8,128)} collective-permute-done((f32[816,128]{1,0:T(8,128)S(1)}, f32[816,128]{1,0:T(8,128)}, u32[]{:S(2)}, u32[]{:S(2)}) %collective-permute-start.3) | collective-permute-done | bytes 417824 | tf_op jit(solution)/shard_map/ppermute | solution.py:41
  59.0 0.0 all-to-all-done.1
  59.0 9.6 %shard_map.54 = f32[16,4,32,128]{3,2,1,0:T(8,128)} custom-call(f32[4,4,8,128]{3,2,1,0:T(8,128)S(1)} %copy-done.3, f32[16,176,128]{2,1,0:T(8,128)S(1)} %bitcast.8, f32[4,48,128]{2,1,0:T(8,128)} %get-tuple-element.15.refs_2_, f32[16,120,128]{2,1,0:T(8,128)S(1)} %bitcast.9, f32[376,128]{1,0:T(8,128)} %get-tuple-element.20.refs_4_.lower_hbm, ...), custom_call_target="tpu_custom_call" | custom-call | flops 30000000 | bytes 7610368 | tf_op jit(solution)/shard_map/pallas_call | solution.py:697
  68.7 0.0 copy-start
  68.7 0.0 copy-start.4
  68.7 4.3 %all-to-all-start.2 = ((f32[8,2,4,32,128]{4,3,2,1,0:T(8,128)}), f32[8,2,4,32,128]{4,3,2,1,0:T(8,128)S(1)}, u32[]{:S(2)}, u32[]{:S(2)}) async-start(f32[8,2,4,32,128]{4,3,2,1,0:T(8,128)} %bitcast.10), calls=%async_computation.2 | async-start | bytes 2097152 | tf_op jit(solution)/shard_map/all_to_all | solution.py:721
  73.0 0.0 copy-done
  73.0 0.8 slice_bitcast_fusion
  73.9 2.0 %collective-permute-start.4 = (f32[8,64,256]{2,1,0:T(8,128)}, f32[8,64,256]{2,1,0:T(8,128)S(1)}, u32[]{:S(2)}, u32[]{:S(2)}) collective-permute-start(f32[8,64,256]{2,1,0:T(8,128)} %slice_bitcast_fusion), channel_id=1, source_target_pairs={{0,4},{4,8},{8,12},{12,16},{16,20},{20,24},{24,28},{1,5},{5,9},{9,... | collective-permute-start | bytes 1572872 | tf_op jit(solution)/shard_map/ppermute | solution.py:788
  75.9 16.7 %collective-permute-done.4 = f32[8,64,256]{2,1,0:T(8,128)S(1)} collective-permute-done((f32[8,64,256]{2,1,0:T(8,128)}, f32[8,64,256]{2,1,0:T(8,128)S(1)}, u32[]{:S(2)}, u32[]{:S(2)}) %collective-permute-start.4) | collective-permute-done | bytes 524320 | tf_op jit(solution)/shard_map/ppermute | solution.py:788
  92.6 0.0 copy-done.4
  92.6 0.1 broadcast_select_fusion.carried
  92.6 2.7 %shard_map.56 = f32[2,8,64,256]{3,2,1,0:T(8,128)} custom-call(f32[2,8,64,256]{3,2,1,0:T(8,128)S(1)} %copy-done, f32[8,64,256]{2,1,0:T(8,128)S(1)} %broadcast_select_fusion.carried, f32[376,128]{1,0:T(8,128)} %get-tuple-element.20.refs_4_.lower_hbm, f32[376,128]{1,0:T(8,128)} %get-tuple-element.21.refs_5_.upper_hbm), custom_call_target="tpu_custom_call" | custom-call | flops 6000000 | bytes 3006464 | tf_op jit(solution)/shard_map/pallas_call | solution.py:697
  95.3 0.0 all-to-all-done.2.pieces
  95.3 1.2 %shard_map.55 = f32[2,8,64,256]{3,2,1,0:T(8,128)} custom-call(f32[2,8,64,256]{3,2,1,0:T(8,128)S(1)} %copy-done, f32[8,2,4,32,128]{4,3,2,1,0:T(8,128)S(1)} %all-to-all-done.2.pieces), custom_call_target="tpu_custom_call" | custom-call | flops 2000000 | bytes 3145728 | tf_op jit(solution)/shard_map/pallas_call | solution.py:697
Async XLA Ops:
  3.9 5.9 %copy-start.6 = (f32[888,128]{1,0:T(8,128)S(1)}, f32[888,128]{1,0:T(8,128)}, u32[]{:S(2)}) copy-start(f32[888,128]{1,0:T(8,128)} %get-tuple-element.18) | copy-start | bytes 1363972
  3.9 22.5 %all-to-all-start = ((f32[8,2,176,128]{3,2,1,0:T(8,128)}), f32[8,2,176,128]{3,2,1,0:T(8,128)S(1)}, u32[]{:S(2)}, u32[]{:S(2)}) async-start(f32[8,2,176,128]{3,2,1,0:T(8,128)} %get-tuple-element.14), calls=%async_computation | async-start | bytes 2883584 | tf_op jit(solution)/shard_map/all_to_all | solution.py:721
  8.2 19.2 %collective-permute-start = (f32[888,128]{1,0:T(8,128)}, f32[888,128]{1,0:T(8,128)S(1)}, u32[]{:S(2)}, u32[]{:S(2)}) collective-permute-start(f32[888,128]{1,0:T(8,128)} %get-tuple-element.17), channel_id=1, source_target_pairs={{0,1},{1,2},{2,3},{3,0},{4,5},{5,6},{6,7},{7,4},{8,9},{9,10},{10,1... | collective-permute-start | bytes 1363976 | tf_op jit(solution)/shard_map/ppermute | solution.py:41
  9.8 21.9 %collective-permute-start.1 = (f32[888,128]{1,0:T(8,128)S(1)}, f32[888,128]{1,0:T(8,128)S(1)}, u32[]{:S(2)}, u32[]{:S(2)}) collective-permute-start(f32[888,128]{1,0:T(8,128)S(1)} %copy-done.6), channel_id=1, source_target_pairs={{0,3},{1,0},{2,1},{3,2},{4,7},{5,4},{6,5},{7,6},{8,11},{9,8},{10,9... | collective-permute-start | bytes 1363976 | tf_op jit(solution)/shard_map/ppermute | solution.py:41
  26.7 0.8 copy-start.1
  31.7 5.5 %copy-start.2 = (f32[816,128]{1,0:T(8,128)S(1)}, f32[816,128]{1,0:T(8,128)}, u32[]{:S(2)}) copy-start(f32[816,128]{1,0:T(8,128)} %copy-done.1) | copy-start | bytes 1253380
  31.7 9.4 %copy-start.3 = (f32[4,4,8,128]{3,2,1,0:T(8,128)S(1)}, f32[4,4,8,128]{3,2,1,0:T(8,128)}, u32[]{:S(2)}) copy-start(f32[4,4,8,128]{3,2,1,0:T(8,128)} %constant.10.clone.refs_0_) | copy-start | bytes 196612
  33.0 26.0 %all-to-all-start.1 = ((f32[8,2,120,128]{3,2,1,0:T(8,128)}), f32[8,2,120,128]{3,2,1,0:T(8,128)S(1)}, u32[]{:S(2)}, u32[]{:S(2)}) async-start(f32[8,2,120,128]{3,2,1,0:T(8,128)} %get-tuple-element.19), calls=%async_computation.1 | async-start | bytes 1966080 | tf_op jit(solution)/shard_map/all_to_all | solution.py:721
  37.2 14.4 %collective-permute-start.2 = (f32[816,128]{1,0:T(8,128)S(1)}, f32[816,128]{1,0:T(8,128)S(1)}, u32[]{:S(2)}, u32[]{:S(2)}) collective-permute-start(f32[816,128]{1,0:T(8,128)S(1)} %copy-done.2), channel_id=1, source_target_pairs={{0,1},{1,2},{2,3},{3,0},{4,5},{5,6},{6,7},{7,4},{8,9},{9,10},{10,1... | collective-permute-start | bytes 1253384 | tf_op jit(solution)/shard_map/ppermute | solution.py:41
  38.6 20.4 %collective-permute-start.3 = (f32[816,128]{1,0:T(8,128)S(1)}, f32[816,128]{1,0:T(8,128)}, u32[]{:S(2)}, u32[]{:S(2)}) collective-permute-start(f32[816,128]{1,0:T(8,128)S(1)} %get-tuple-element.22), channel_id=1, source_target_pairs={{0,3},{1,0},{2,1},{3,2},{4,7},{5,4},{6,5},{7,6},{8,11},{9,8},{10,9... | collective-permute-start | bytes 1253384 | tf_op jit(solution)/shard_map/ppermute | solution.py:41
  51.6 0.8 copy-start.5
  68.7 4.4 %copy-start = (f32[2,8,64,256]{3,2,1,0:T(8,128)S(1)}, f32[2,8,64,256]{3,2,1,0:T(8,128)}, u32[]{:S(2)}) copy-start(f32[2,8,64,256]{3,2,1,0:T(8,128)} %state.3) | copy-start | bytes 3145732
  68.7 23.9 %copy-start.4 = (f32[8,64,256]{2,1,0:T(8,128)S(1)}, f32[8,64,256]{2,1,0:T(8,128)}, u32[]{:S(2)}) copy-start(f32[8,64,256]{2,1,0:T(8,128)} %initial_hbm.1) | copy-start | bytes 1572868
  68.7 26.6 %all-to-all-start.2 = ((f32[8,2,4,32,128]{4,3,2,1,0:T(8,128)}), f32[8,2,4,32,128]{4,3,2,1,0:T(8,128)S(1)}, u32[]{:S(2)}, u32[]{:S(2)}) async-start(f32[8,2,4,32,128]{4,3,2,1,0:T(8,128)} %bitcast.10), calls=%async_computation.2 | async-start | bytes 2097152 | tf_op jit(solution)/shard_map/all_to_all | solution.py:721
  73.9 18.7 %collective-permute-start.4 = (f32[8,64,256]{2,1,0:T(8,128)}, f32[8,64,256]{2,1,0:T(8,128)S(1)}, u32[]{:S(2)}, u32[]{:S(2)}) collective-permute-start(f32[8,64,256]{2,1,0:T(8,128)} %slice_bitcast_fusion), channel_id=1, source_target_pairs={{0,4},{4,8},{8,12},{12,16},{16,20},{20,24},{24,28},{1,5},{5,9},{9,... | collective-permute-start | bytes 1572872 | tf_op jit(solution)/shard_map/ppermute | solution.py:788

commit v6 on v5

--- a/solution.py
+++ b/solution.py
@@ -236,12 +236,13 @@
         store.wait()
 
 
-def pack_late(pairs, size, own, up, down):
+def pack_late(pairs, size, own, up_hbm, down_hbm, up, down, sems):
     horizon = own.shape[0]
     half = horizon // 2
     width = 2 * pairs
     stride = size + 2 * SWEEPS
     at = 0
+    stores = []
     for j, rows in enumerate(late_rows(size)):
         a = SWEEPS - j
         for t in range(half):
@@ -253,6 +254,13 @@
                 here = 0 if low else 1
                 out[at : at + rows] = merge(before, after, here, here)
             at += rows
+        region = pl.ds(at - half * rows, half * rows)
+        stores += copy_in(
+            sems.at[pl.ds(2 * j, 2)],
+            [(up.at[region], up_hbm.at[region]), (down.at[region], down_hbm.at[region])],
+        )
+    for store in stores:
+        store.wait()
 
 
 def real_forward(values):
@@ -769,7 +777,13 @@
     upper = hop(down, -1)
 
     late_shape = shape_of(half * sum(late_rows(size)), lanes)
-    late_up, late_down = call(functools.partial(pack_late, pairs, size), [late_shape] * 2, [own])
+    late_up, late_down = call(
+        functools.partial(pack_late, pairs, size),
+        [late_shape] * 2,
+        [own],
+        [vmem(*late_shape.shape), vmem(*late_shape.shape), semaphores(2 * (SWEEPS - EARLY))],
+        far_outs=(0, 1),
+    )
     late_low = hop(late_up, 1)
     late_high = hop(late_down, -1)
 

time: 97 us -> 97 us (level)
  local copies, waits for them, and re-layouts: 2.36 us -> 0.87 us
    unnamed x14, local copies, waits for them, and re-layouts: 1.53 us -> 0.04 us
  transfers between devices with their start and end apart: 8 -> 8, of which waited for: 5 -> 5; matrix products, arithmetic and copies ran while one was open for 1% -> 1% of each run, Pallas kernels for 8% -> 9%
where the time goes in v6:
time: 97 us; the launch traced here: 96.6 us
  waiting for transfers between devices  48.3 us (50%)
  Pallas kernels  24 us (25%)
  starting transfers between devices  22.6 us (23%)
    pallas_call x7, Pallas kernels, call(): pl.pallas_call(kernel, out_shape=tuple(outs), in_specs=[pl.BlockSpec(memo...  24 us
    ppermute x4, waiting for transfers between devices, hop(): return lax.ppermute(block, 'space', ring('space', step))  17.3 us
    ppermute x1, waiting for transfers between devices, iteration(): lax.ppermute(state[steps - 1], 'tm', [(i, i + 1) for i in range(count - 1)])  16.7 us
    all_to_all x3, waiting for transfers between devices, exchange(): return lax.all_to_all(block, 'tm', split_axis=0, concat_axis=0, tiled=True)  14.3 us
    all_to_all x3, starting transfers between devices, exchange(): return lax.all_to_all(block, 'tm', split_axis=0, concat_axis=0, tiled=True)  12.9 us
    ppermute x4, starting transfers between devices, hop(): return lax.ppermute(block, 'space', ring('space', step))  7.65 us
    ppermute x1, starting transfers between devices, iteration(): lax.ppermute(state[steps - 1], 'tm', [(i, i + 1) for i in range(count - 1)])  2.01 us
  transfers between devices with their start and end apart: 8, of which 5 were waited for; matrix products, arithmetic and copies ran while one was open for 1% of the time, Pallas kernels for 9%

profile of v6, /device:TPU:4, one launch (start us, length us, event | category | flops | bytes accessed | tf_op | source)
XLA Modules:
  0.0 96.6 jit_solution(6522175332231477138)
XLA Ops:
  0.6 3.2 %shard_map.50 = (f32[8,2,176,128]{3,2,1,0:T(8,128)}, f32[4,48,128]{2,1,0:T(8,128)}, f32[888,128]{1,0:T(8,128)}, f32[888,128]{1,0:T(8,128)}) custom-call(s32[1]{0:T(128)} %bitcast.position, f32[2,8,64,256]{3,2,1,0:T(8,128)} %state.3, f32[8,64,256]{2,1,0:T(8,128)} %initial_hbm.1), custom_call_target="tpu_custom_call" | custom-call | flops 2000000 | bytes 4026368 | tf_op jit(solution)/shard_map/pallas_call | solution.py:705
  3.9 0.0 copy-start.6
  3.9 0.0 copy-start.5
  3.9 4.4 %all-to-all-start = ((f32[8,2,176,128]{3,2,1,0:T(8,128)}), f32[8,2,176,128]{3,2,1,0:T(8,128)S(1)}, u32[]{:S(2)}, u32[]{:S(2)}) async-start(f32[8,2,176,128]{3,2,1,0:T(8,128)} %get-tuple-element.14), calls=%async_computation | async-start | bytes 2883584 | tf_op jit(solution)/shard_map/all_to_all | solution.py:729
  8.2 0.0 copy-done.6
  8.2 1.6 %collective-permute-start = (f32[888,128]{1,0:T(8,128)S(1)}, f32[888,128]{1,0:T(8,128)S(1)}, u32[]{:S(2)}, u32[]{:S(2)}) collective-permute-start(f32[888,128]{1,0:T(8,128)S(1)} %copy-done.6), channel_id=1, source_target_pairs={{0,1},{1,2},{2,3},{3,0},{4,5},{5,6},{6,7},{7,4},{8,9},{9,10},{10,1... | collective-permute-start | bytes 1363976 | tf_op jit(solution)/shard_map/ppermute | solution.py:41
  9.8 0.0 copy-done.5
  9.8 2.2 %collective-permute-start.1 = (f32[888,128]{1,0:T(8,128)S(1)}, f32[888,128]{1,0:T(8,128)S(1)}, u32[]{:S(2)}, u32[]{:S(2)}) collective-permute-start(f32[888,128]{1,0:T(8,128)S(1)} %copy-done.5), channel_id=1, source_target_pairs={{0,3},{1,0},{2,1},{3,2},{4,7},{5,4},{6,5},{7,6},{8,11},{9,8},{10,9... | collective-permute-start | bytes 1363976 | tf_op jit(solution)/shard_map/ppermute | solution.py:41
  12.1 14.3 %all-to-all-done = f32[8,2,176,128]{3,2,1,0:T(8,128)S(1)} async-done(((f32[8,2,176,128]{3,2,1,0:T(8,128)}), f32[8,2,176,128]{3,2,1,0:T(8,128)S(1)}, u32[]{:S(2)}, u32[]{:S(2)}) %all-to-all-start) | async-done | bytes 1441824 | tf_op jit(solution)/shard_map/all_to_all | solution.py:729
  26.4 1.1 %shard_map.51 = (f32[816,128]{1,0:T(8,128)}, f32[816,128]{1,0:T(8,128)}) custom-call(f32[16,176,128]{2,1,0:T(8,128)S(1)} %bitcast.6), custom_call_target="tpu_custom_call" | custom-call | flops 2000000 | bytes 2277376 | tf_op jit(solution)/shard_map/pallas_call | solution.py:705
  27.4 0.0 collective-permute-done.lower
  27.4 4.3 %collective-permute-done.1.upper = f32[888,128]{1,0:T(8,128)S(1)} collective-permute-done((f32[888,128]{1,0:T(8,128)S(1)}, f32[888,128]{1,0:T(8,128)S(1)}, u32[]{:S(2)}, u32[]{:S(2)}) %collective-permute-start.1) | collective-permute-done | bytes 454688 | tf_op jit(solution)/shard_map/ppermute | solution.py:41
  31.7 0.0 copy-start.3
  31.7 0.0 copy-start.1
  31.7 1.3 %shard_map.52 = (f32[8,2,120,128]{3,2,1,0:T(8,128)}, f32[376,128]{1,0:T(8,128)}, f32[376,128]{1,0:T(8,128)}) custom-call(f32[816,128]{1,0:T(8,128)} %get-tuple-element.16.after, f32[888,128]{1,0:T(8,128)S(1)} %collective-permute-done.lower, f32[888,128]{1,0:T(8,128)S(1)} %collective-permute-done.1.upper), custom_call_target="tpu_custom_call" | custom-call | flops 2000000 | bytes 2695168 | tf_op jit(solution)/shard_map/pallas_call | solution.py:705
  33.0 4.2 %all-to-all-start.1 = ((f32[8,2,120,128]{3,2,1,0:T(8,128)}), f32[8,2,120,128]{3,2,1,0:T(8,128)S(1)}, u32[]{:S(2)}, u32[]{:S(2)}) async-start(f32[8,2,120,128]{3,2,1,0:T(8,128)} %get-tuple-element.19), calls=%async_computation.1 | async-start | bytes 1966080 | tf_op jit(solution)/shard_map/all_to_all | solution.py:729
  37.3 0.0 copy-done.3
  37.3 1.1 %collective-permute-start.2 = (f32[816,128]{1,0:T(8,128)S(1)}, f32[816,128]{1,0:T(8,128)S(1)}, u32[]{:S(2)}, u32[]{:S(2)}) collective-permute-start(f32[816,128]{1,0:T(8,128)S(1)} %copy-done.3), channel_id=1, source_target_pairs={{0,1},{1,2},{2,3},{3,0},{4,5},{5,6},{6,7},{7,4},{8,9},{9,10},{10,1... | collective-permute-start | bytes 1253384 | tf_op jit(solution)/shard_map/ppermute | solution.py:41
  38.4 2.7 %collective-permute-start.3 = (f32[816,128]{1,0:T(8,128)}, f32[816,128]{1,0:T(8,128)}, u32[]{:S(2)}, u32[]{:S(2)}) collective-permute-start(f32[816,128]{1,0:T(8,128)} %get-tuple-element.22), channel_id=1, source_target_pairs={{0,3},{1,0},{2,1},{3,2},{4,7},{5,4},{6,5},{7,6},{8,11},{9,8},{10,9... | collective-permute-start | bytes 1253384 | tf_op jit(solution)/shard_map/ppermute | solution.py:41
  41.1 0.0 copy-done.1
  41.1 4.9 %shard_map.53 = (f32[16,3,56,128]{3,2,1,0:T(8,128)}, f32[16,2,56,128]{3,2,1,0:T(8,128)}, f32[16,1,56,128]{3,2,1,0:T(8,128)}) custom-call(f32[4,4,8,128]{3,2,1,0:T(8,128)S(1)} %copy-done.1, f32[16,176,128]{2,1,0:T(8,128)S(1)} %bitcast.7, f32[4,48,128]{2,1,0:T(8,128)} %get-tuple-element.15.refs_2_), custom_call_target="tpu_custom_call" | custom-call | flops 30000000 | bytes 4358144 | tf_op jit(solution)/shard_map/pallas_call | solution.py:705
  46.0 5.6 %collective-permute-done.2.refs_6_ = f32[816,128]{1,0:T(8,128)S(1)} collective-permute-done((f32[816,128]{1,0:T(8,128)S(1)}, f32[816,128]{1,0:T(8,128)S(1)}, u32[]{:S(2)}, u32[]{:S(2)}) %collective-permute-start.2) | collective-permute-done | bytes 417824 | tf_op jit(solution)/shard_map/ppermute | solution.py:41
  51.6 0.0 copy-start.4
  51.6 7.4 %collective-permute-done.3.refs_7_ = f32[816,128]{1,0:T(8,128)} collective-permute-done((f32[816,128]{1,0:T(8,128)}, f32[816,128]{1,0:T(8,128)}, u32[]{:S(2)}, u32[]{:S(2)}) %collective-permute-start.3) | collective-permute-done | bytes 417824 | tf_op jit(solution)/shard_map/ppermute | solution.py:41
  59.0 0.0 all-to-all-done.1
  59.0 0.0 copy-done.4
  59.0 9.6 %shard_map.54 = f32[16,4,32,128]{3,2,1,0:T(8,128)} custom-call(f32[4,4,8,128]{3,2,1,0:T(8,128)S(1)} %copy-done.1, f32[16,176,128]{2,1,0:T(8,128)S(1)} %bitcast.8, f32[4,48,128]{2,1,0:T(8,128)} %get-tuple-element.15.refs_2_, f32[16,120,128]{2,1,0:T(8,128)S(1)} %bitcast.9, f32[376,128]{1,0:T(8,128)} %get-tuple-element.20.refs_4_.lower_hbm, ...), custom_call_target="tpu_custom_call" | custom-call | flops 30000000 | bytes 7610368 | tf_op jit(solution)/shard_map/pallas_call | solution.py:705
  68.7 0.0 copy-start
  68.7 0.0 copy-start.2
  68.7 4.3 %all-to-all-start.2 = ((f32[8,2,4,32,128]{4,3,2,1,0:T(8,128)}), f32[8,2,4,32,128]{4,3,2,1,0:T(8,128)S(1)}, u32[]{:S(2)}, u32[]{:S(2)}) async-start(f32[8,2,4,32,128]{4,3,2,1,0:T(8,128)} %bitcast.10), calls=%async_computation.2 | async-start | bytes 2097152 | tf_op jit(solution)/shard_map/all_to_all | solution.py:729
  73.1 0.0 copy-done
  73.1 0.8 slice_bitcast_fusion
  73.9 2.0 %collective-permute-start.4 = (f32[8,64,256]{2,1,0:T(8,128)}, f32[8,64,256]{2,1,0:T(8,128)S(1)}, u32[]{:S(2)}, u32[]{:S(2)}) collective-permute-start(f32[8,64,256]{2,1,0:T(8,128)} %slice_bitcast_fusion), channel_id=1, source_target_pairs={{0,4},{4,8},{8,12},{12,16},{16,20},{20,24},{24,28},{1,5},{5,9},{9,... | collective-permute-start | bytes 1572872 | tf_op jit(solution)/shard_map/ppermute | solution.py:802
  75.9 16.7 %collective-permute-done.4 = f32[8,64,256]{2,1,0:T(8,128)S(1)} collective-permute-done((f32[8,64,256]{2,1,0:T(8,128)}, f32[8,64,256]{2,1,0:T(8,128)S(1)}, u32[]{:S(2)}, u32[]{:S(2)}) %collective-permute-start.4) | collective-permute-done | bytes 524320 | tf_op jit(solution)/shard_map/ppermute | solution.py:802
  92.6 0.0 copy-done.2
  92.6 0.1 broadcast_select_fusion.carried
  92.7 2.7 %shard_map.56 = f32[2,8,64,256]{3,2,1,0:T(8,128)} custom-call(f32[2,8,64,256]{3,2,1,0:T(8,128)S(1)} %copy-done, f32[8,64,256]{2,1,0:T(8,128)S(1)} %broadcast_select_fusion.carried, f32[376,128]{1,0:T(8,128)} %get-tuple-element.20.refs_4_.lower_hbm, f32[376,128]{1,0:T(8,128)} %get-tuple-element.21.refs_5_.upper_hbm), custom_call_target="tpu_custom_call" | custom-call | flops 6000000 | bytes 3006464 | tf_op jit(solution)/shard_map/pallas_call | solution.py:705
  95.3 0.0 all-to-all-done.2.pieces
  95.3 1.2 %shard_map.55 = f32[2,8,64,256]{3,2,1,0:T(8,128)} custom-call(f32[2,8,64,256]{3,2,1,0:T(8,128)S(1)} %copy-done, f32[8,2,4,32,128]{4,3,2,1,0:T(8,128)S(1)} %all-to-all-done.2.pieces), custom_call_target="tpu_custom_call" | custom-call | flops 2000000 | bytes 3145728 | tf_op jit(solution)/shard_map/pallas_call | solution.py:705
Async XLA Ops:
  3.9 4.4 %copy-start.6 = (f32[888,128]{1,0:T(8,128)S(1)}, f32[888,128]{1,0:T(8,128)}, u32[]{:S(2)}) copy-start(f32[888,128]{1,0:T(8,128)} %get-tuple-element.17) | copy-start | bytes 1363972
  3.9 6.0 %copy-start.5 = (f32[888,128]{1,0:T(8,128)S(1)}, f32[888,128]{1,0:T(8,128)}, u32[]{:S(2)}) copy-start(f32[888,128]{1,0:T(8,128)} %get-tuple-element.18) | copy-start | bytes 1363972
  3.9 22.5 %all-to-all-start = ((f32[8,2,176,128]{3,2,1,0:T(8,128)}), f32[8,2,176,128]{3,2,1,0:T(8,128)S(1)}, u32[]{:S(2)}, u32[]{:S(2)}) async-start(f32[8,2,176,128]{3,2,1,0:T(8,128)} %get-tuple-element.14), calls=%async_computation | async-start | bytes 2883584 | tf_op jit(solution)/shard_map/all_to_all | solution.py:729
  8.2 19.2 %collective-permute-start = (f32[888,128]{1,0:T(8,128)S(1)}, f32[888,128]{1,0:T(8,128)S(1)}, u32[]{:S(2)}, u32[]{:S(2)}) collective-permute-start(f32[888,128]{1,0:T(8,128)S(1)} %copy-done.6), channel_id=1, source_target_pairs={{0,1},{1,2},{2,3},{3,0},{4,5},{5,6},{6,7},{7,4},{8,9},{9,10},{10,1... | collective-permute-start | bytes 1363976 | tf_op jit(solution)/shard_map/ppermute | solution.py:41
  9.8 21.9 %collective-permute-start.1 = (f32[888,128]{1,0:T(8,128)S(1)}, f32[888,128]{1,0:T(8,128)S(1)}, u32[]{:S(2)}, u32[]{:S(2)}) collective-permute-start(f32[888,128]{1,0:T(8,128)S(1)} %copy-done.5), channel_id=1, source_target_pairs={{0,3},{1,0},{2,1},{3,2},{4,7},{5,4},{6,5},{7,6},{8,11},{9,8},{10,9... | collective-permute-start | bytes 1363976 | tf_op jit(solution)/shard_map/ppermute | solution.py:41
  31.7 5.5 %copy-start.3 = (f32[816,128]{1,0:T(8,128)S(1)}, f32[816,128]{1,0:T(8,128)}, u32[]{:S(2)}) copy-start(f32[816,128]{1,0:T(8,128)} %get-tuple-element.16.after) | copy-start | bytes 1253380
  31.7 9.4 %copy-start.1 = (f32[4,4,8,128]{3,2,1,0:T(8,128)S(1)}, f32[4,4,8,128]{3,2,1,0:T(8,128)}, u32[]{:S(2)}) copy-start(f32[4,4,8,128]{3,2,1,0:T(8,128)} %constant.10.clone.refs_0_) | copy-start | bytes 196612
  33.0 26.0 %all-to-all-start.1 = ((f32[8,2,120,128]{3,2,1,0:T(8,128)}), f32[8,2,120,128]{3,2,1,0:T(8,128)S(1)}, u32[]{:S(2)}, u32[]{:S(2)}) async-start(f32[8,2,120,128]{3,2,1,0:T(8,128)} %get-tuple-element.19), calls=%async_computation.1 | async-start | bytes 1966080 | tf_op jit(solution)/shard_map/all_to_all | solution.py:729
  37.3 14.4 %collective-permute-start.2 = (f32[816,128]{1,0:T(8,128)S(1)}, f32[816,128]{1,0:T(8,128)S(1)}, u32[]{:S(2)}, u32[]{:S(2)}) collective-permute-start(f32[816,128]{1,0:T(8,128)S(1)} %copy-done.3), channel_id=1, source_target_pairs={{0,1},{1,2},{2,3},{3,0},{4,5},{5,6},{6,7},{7,4},{8,9},{9,10},{10,1... | collective-permute-start | bytes 1253384 | tf_op jit(solution)/shard_map/ppermute | solution.py:41
  38.4 20.7 %collective-permute-start.3 = (f32[816,128]{1,0:T(8,128)}, f32[816,128]{1,0:T(8,128)}, u32[]{:S(2)}, u32[]{:S(2)}) collective-permute-start(f32[816,128]{1,0:T(8,128)} %get-tuple-element.22), channel_id=1, source_target_pairs={{0,3},{1,0},{2,1},{3,2},{4,7},{5,4},{6,5},{7,6},{8,11},{9,8},{10,9... | collective-permute-start | bytes 1253384 | tf_op jit(solution)/shard_map/ppermute | solution.py:41
  51.6 7.4 %copy-start.4 = (f32[816,128]{1,0:T(8,128)}, f32[816,128]{1,0:T(8,128)S(1)}, u32[]{:S(2)}) copy-start(f32[816,128]{1,0:T(8,128)S(1)} %collective-permute-done.2.refs_6_) | copy-start | bytes 1253380
  68.7 4.4 %copy-start = (f32[2,8,64,256]{3,2,1,0:T(8,128)S(1)}, f32[2,8,64,256]{3,2,1,0:T(8,128)}, u32[]{:S(2)}) copy-start(f32[2,8,64,256]{3,2,1,0:T(8,128)} %state.3) | copy-start | bytes 3145732
  68.7 23.9 %copy-start.2 = (f32[8,64,256]{2,1,0:T(8,128)S(1)}, f32[8,64,256]{2,1,0:T(8,128)}, u32[]{:S(2)}) copy-start(f32[8,64,256]{2,1,0:T(8,128)} %initial_hbm.1) | copy-start | bytes 1572868
  68.7 26.6 %all-to-all-start.2 = ((f32[8,2,4,32,128]{4,3,2,1,0:T(8,128)}), f32[8,2,4,32,128]{4,3,2,1,0:T(8,128)S(1)}, u32[]{:S(2)}, u32[]{:S(2)}) async-start(f32[8,2,4,32,128]{4,3,2,1,0:T(8,128)} %bitcast.10), calls=%async_computation.2 | async-start | bytes 2097152 | tf_op jit(solution)/shard_map/all_to_all | solution.py:729
  73.9 18.7 %collective-permute-start.4 = (f32[8,64,256]{2,1,0:T(8,128)}, f32[8,64,256]{2,1,0:T(8,128)S(1)}, u32[]{:S(2)}, u32[]{:S(2)}) collective-permute-start(f32[8,64,256]{2,1,0:T(8,128)} %slice_bitcast_fusion), channel_id=1, source_target_pairs={{0,4},{4,8},{8,12},{12,16},{16,20},{20,24},{24,28},{1,5},{5,9},{9,... | collective-permute-start | bytes 1572872 | tf_op jit(solution)/shard_map/ppermute | solution.py:802
